TPU v7x, 32 devices: a whole 2x2x4 slice. The times are simulated.
32 devices in a mesh: dp: 16 (over z, y, x), tensor: 2 (over core).
Axes of the slice: x: 2, y: 2, z: 4, core: 2. Of those that a mesh axis runs over, the one named last changes fastest.
Arguments:
- layer_input: bfloat16 [16384, 768], P('dp'), may hold values from -6 to 6
- patch_features: bfloat16 [16384, 1024], P('dp', 'tensor'), may hold values from -400 to 400
- bucket_ids: int32 [64], P('dp'), may hold values from 0 to 1
- text_lengths: int32 [64], P('dp'), may hold values from 1 to 31
- upstream: bfloat16 [16384, 768], P('dp'), may hold values from -6 to 6
- query_weight: bfloat16 [768, 768], P(None, 'tensor'), may hold values from -0.21875 to 0.21875
- key_weight: bfloat16 [768, 768], P(None, 'tensor'), may hold values from -0.21875 to 0.21875
- value_weight: bfloat16 [768, 768], P(None, 'tensor'), may hold values from -0.21875 to 0.21875
- merge_weight: bfloat16 [768, 768], P('tensor'), may hold values from -1.75 to 1.75
- query_bias: float32 [768], P('tensor'), may hold values from -3 to 3
- value_bias: float32 [768], P('tensor'), may hold values from -3 to 3
- merge_bias: float32 [768], replicated, may hold values from -3 to 3
- head_gain: float32 [12], P('tensor'), may hold values from 0.25 to 1.75
- distance_table: float32 [12, 511], P('tensor'), may hold values from -4 to 4
- first_gain: float32 [768], replicated, may hold values from 0.25 to 1.75
- first_shift: float32 [768], replicated, may hold values from -3 to 3
- second_gain: float32 [768], replicated, may hold values from 0.25 to 1.75
- second_shift: float32 [768], replicated, may hold values from -3 to 3
- expand_weight: bfloat16 [768, 3072], P(None, 'tensor'), may hold values from -0.21875 to 0.21875
- expand_bias: float32 [3072], P('tensor'), may hold values from -3 to 3
- reduce_weight: bfloat16 [3072, 768], P('tensor'), may hold values from -0.15625 to 0.15625
- reduce_bias: float32 [768], replicated, may hold values from -3 to 3
- image_weight: bfloat16 [1024, 768], P('tensor'), may hold values from -0.1875 to 0.1875
- stem_gain: float32 [1024], P('tensor'), may hold values from 0.25 to 1.75
- stem_shift: float32 [1024], P('tensor'), may hold values from -3 to 3
Outputs:
- block_output: bfloat16 [16384, 768], P('dp')
- input_grad: float32 [16384, 768], P('dp')
- patch_grad: float32 [16384, 1024], P('dp', 'tensor')
- grad_query_weight: float32 [768, 768], P(None, 'tensor')
- grad_key_weight: float32 [768, 768], P(None, 'tensor')
- grad_value_weight: float32 [768, 768], P(None, 'tensor')
- grad_merge_weight: float32 [768, 768], P('tensor')
- grad_query_bias: float32 [768], P('tensor')
- grad_value_bias: float32 [768], P('tensor')
- grad_merge_bias: float32 [768], replicated
- grad_head_gain: float32 [12], P('tensor')
- grad_distance_table: float32 [12, 511], P('tensor')
- grad_first_gain: float32 [768], replicated
- grad_first_shift: float32 [768], replicated
- grad_second_gain: float32 [768], replicated
- grad_second_shift: float32 [768], replicated
- grad_expand_weight: float32 [768, 3072], P(None, 'tensor')
- grad_expand_bias: float32 [3072], P('tensor')
- grad_reduce_weight: float32 [3072, 768], P('tensor')
- grad_reduce_bias: float32 [768], replicated
- grad_image_weight: float32 [1024, 768], P('tensor')
- grad_stem_gain: float32 [1024], P('tensor')
- grad_stem_shift: float32 [1024], P('tensor')
All inputs are finite; a program needn't handle non-finite values.
Results may differ from a plain program's by a relative error of at most 0.014.
Values sent between devices are 32-bit elements; how exact they have to be, the bound alone decides.
No kernel may reach another device: no remote copies, remote signals or barrier semaphores. Data moves between devices by JAX's collectives and lax.ppermute only.
A program may use at most 128 MiB of HBM per device.

v0:
```python
from functools import partial

import jax
import jax.numpy as jnp
from jax import lax
from jax.sharding import PartitionSpec as P

HEAD_DIM = 64
PATCH_SMALL = 64
PATCH_LARGE = 225


EPSILON = 1e-05
NEGATIVE = -1e30


def layer_norm(values, gain, shift):
    centered = values - jnp.mean(values, axis=-1, keepdims=True)
    scaled = centered * lax.rsqrt(jnp.mean(centered * centered, axis=-1, keepdims=True) + EPSILON)
    return scaled * gain + shift


def distance_bias(table, length):
    count_heads = table.shape[0]
    padded = jnp.pad(table, ((0, 0), (0, 1)))
    tiled = jnp.broadcast_to(padded[:, None, :], (count_heads, length, 2 * length)).reshape(
        count_heads, 2 * length * length
    )
    window = tiled[:, length - 1 : length - 1 + length * (2 * length - 1)].reshape(
        count_heads, length, 2 * length - 1
    )
    return window[:, :, :length]


def scores_of(query_low, key_low, bias, key_valid, scale):
    scores = (
        jnp.einsum("bqhd,bkhd->bhqk", query_low, key_low, preferred_element_type=jnp.float32)
        * scale
        + bias[None]
    )
    return jnp.where(key_valid[:, None, None, :], scores, NEGATIVE)


def project_back(grad_low, weight):
    return jnp.einsum("tf,df->td", grad_low, weight, preferred_element_type=jnp.float32)


def weight_grad(inputs_low, grad_low):
    return jnp.einsum("tc,td->cd", inputs_low, grad_low, preferred_element_type=jnp.float32)


def local(
    layer_input,
    patch_features,
    bucket_ids,
    text_lengths,
    upstream,
    query_weight,
    key_weight,
    value_weight,
    merge_weight,
    query_bias,
    value_bias,
    merge_bias,
    head_gain,
    distance_table,
    first_gain,
    first_shift,
    second_gain,
    second_shift,
    expand_weight,
    expand_bias,
    reduce_weight,
    reduce_bias,
    image_weight,
    stem_gain,
    stem_shift,
):
    items = bucket_ids.shape[0]
    rows = layer_input.shape[0]
    length = rows // items
    heads = head_gain.shape[0]
    width = query_weight.shape[1]
    scale = HEAD_DIM ** (-0.5)
    patches = PATCH_SMALL + (PATCH_LARGE - PATCH_SMALL) * bucket_ids
    slots = jnp.arange(length, dtype=jnp.int32)
    patch_mask = (slots[None, :] < patches[:, None]).astype(jnp.float32).reshape(rows)
    key_valid = slots[None, :] < (patches + text_lengths)[:, None]
    valid_rows = key_valid.astype(jnp.float32).reshape(rows)
    features = patch_features.astype(jnp.float32)
    masked = features * patch_mask[:, None]
    feature_sum, square_sum, count = lax.psum(
        (jnp.sum(masked, axis=0), jnp.sum(masked * features, axis=0), jnp.sum(patch_mask)), "dp"
    )
    stem_mean = feature_sum / count
    stem_inverse = lax.rsqrt(square_sum / count - stem_mean * stem_mean + EPSILON)
    stem_hat = (features - stem_mean) * stem_inverse
    stem_low = (stem_hat * stem_gain + stem_shift).astype(jnp.bfloat16)
    embedded = lax.psum(
        jnp.dot(stem_low, image_weight, preferred_element_type=jnp.float32), "tensor"
    )
    hidden = layer_input.astype(jnp.float32) + patch_mask[:, None] * embedded
    first_normed, first_back = jax.vjp(layer_norm, hidden, first_gain, first_shift)
    first_low = first_normed.astype(jnp.bfloat16)
    split_shape = (items, length, heads, HEAD_DIM)
    query_low = (
        (jnp.dot(first_low, query_weight, preferred_element_type=jnp.float32) + query_bias)
        .astype(jnp.bfloat16)
        .reshape(split_shape)
    )
    key_low = (
        jnp.dot(first_low, key_weight, preferred_element_type=jnp.float32)
        .astype(jnp.bfloat16)
        .reshape(split_shape)
    )
    value_low = (
        (jnp.dot(first_low, value_weight, preferred_element_type=jnp.float32) + value_bias)
        .astype(jnp.bfloat16)
        .reshape(split_shape)
    )
    bias, bias_back = jax.vjp(lambda table: distance_bias(table, length), distance_table)
    scores = scores_of(query_low, key_low, bias, key_valid, scale)
    peak = jnp.max(scores, axis=-1, keepdims=True)
    log_total = peak + jnp.log(jnp.sum(jnp.exp(scores - peak), axis=-1, keepdims=True))
    probs_low = jnp.exp(scores - log_total).astype(jnp.bfloat16)
    mixed = jnp.einsum("bhqk,bkhd->bqhd", probs_low, value_low, preferred_element_type=jnp.float32)
    scaled_low = (mixed * head_gain[None, None, :, None]).astype(jnp.bfloat16).reshape(rows, width)
    branch = lax.psum(
        jnp.dot(scaled_low, merge_weight, preferred_element_type=jnp.float32), "tensor"
    )
    middle = hidden + branch + merge_bias
    second_normed, second_back = jax.vjp(layer_norm, middle, second_gain, second_shift)
    second_low = second_normed.astype(jnp.bfloat16)
    expanded = jnp.dot(second_low, expand_weight, preferred_element_type=jnp.float32) + expand_bias
    active, gelu_back = jax.vjp(partial(jax.nn.gelu, approximate=False), expanded)
    active_low = active.astype(jnp.bfloat16)
    reduced = lax.psum(
        jnp.dot(active_low, reduce_weight, preferred_element_type=jnp.float32), "tensor"
    )
    block_output = (middle + reduced + reduce_bias).astype(jnp.bfloat16)
    grad_result = upstream.astype(jnp.float32) * valid_rows[:, None]
    grad_reduce_bias = jnp.sum(grad_result, axis=0)
    grad_reduced_low = grad_result.astype(jnp.bfloat16)
    grad_reduce_weight = weight_grad(active_low, grad_reduced_low)
    (grad_expanded,) = gelu_back(project_back(grad_reduced_low, reduce_weight))
    grad_expanded_low = grad_expanded.astype(jnp.bfloat16)
    grad_expand_bias = jnp.sum(grad_expanded_low.astype(jnp.float32), axis=0)
    grad_expand_weight = weight_grad(second_low, grad_expanded_low)
    grad_second = lax.psum(project_back(grad_expanded_low, expand_weight), "tensor")
    grad_middle_part, grad_second_gain, grad_second_shift = second_back(grad_second)
    grad_middle = grad_result + grad_middle_part
    grad_merge_bias = jnp.sum(grad_middle, axis=0)
    grad_branch_low = grad_middle.astype(jnp.bfloat16)
    grad_merge_weight = weight_grad(scaled_low, grad_branch_low)
    grad_scaled = project_back(grad_branch_low, merge_weight).reshape(split_shape)
    grad_head_gain = jnp.sum(grad_scaled * mixed, axis=(0, 1, 3))
    grad_mixed_low = (grad_scaled * head_gain[None, None, :, None]).astype(jnp.bfloat16)
    again = scores_of(query_low, key_low, bias, key_valid, scale)
    probs = jnp.exp(again - log_total)
    probs_again = probs.astype(jnp.bfloat16)
    grad_value_low = jnp.einsum(
        "bhqk,bqhd->bkhd", probs_again, grad_mixed_low, preferred_element_type=jnp.float32
    ).astype(jnp.bfloat16)
    grad_probs = jnp.einsum(
        "bqhd,bkhd->bhqk", grad_mixed_low, value_low, preferred_element_type=jnp.float32
    )
    grad_scores = probs * (grad_probs - jnp.sum(probs * grad_probs, axis=-1, keepdims=True))
    grad_scores_low = grad_scores.astype(jnp.bfloat16)
    (grad_distance_table,) = bias_back(jnp.sum(grad_scores_low.astype(jnp.float32), axis=0))
    grad_query_low = (
        (
            jnp.einsum(
                "bhqk,bkhd->bqhd", grad_scores_low, key_low, preferred_element_type=jnp.float32
            )
            * scale
        )
        .astype(jnp.bfloat16)
        .reshape(rows, width)
    )
    grad_key_low = (
        (
            jnp.einsum(
                "bhqk,bqhd->bkhd", grad_scores_low, query_low, preferred_element_type=jnp.float32
            )
            * scale
        )
        .astype(jnp.bfloat16)
        .reshape(rows, width)
    )
    grad_value_low = grad_value_low.reshape(rows, width)
    grad_query_bias = jnp.sum(grad_query_low.astype(jnp.float32), axis=0)
    grad_value_bias = jnp.sum(grad_value_low.astype(jnp.float32), axis=0)
    grad_query_weight = weight_grad(first_low, grad_query_low)
    grad_key_weight = weight_grad(first_low, grad_key_low)
    grad_value_weight = weight_grad(first_low, grad_value_low)
    grad_first_part = (
        project_back(grad_query_low, query_weight)
        + project_back(grad_key_low, key_weight)
        + project_back(grad_value_low, value_weight)
    )
    grad_first = lax.psum(grad_first_part, "tensor")
    grad_hidden_part, grad_first_gain, grad_first_shift = first_back(grad_first)
    input_grad = grad_middle + grad_hidden_part
    grad_embedded_low = (input_grad * patch_mask[:, None]).astype(jnp.bfloat16)
    grad_image_weight = weight_grad(stem_low, grad_embedded_low)
    grad_stem = project_back(grad_embedded_low, image_weight)
    shift_local = jnp.sum(grad_stem, axis=0)
    gain_local = jnp.sum(grad_stem * stem_hat, axis=0)
    (
        grad_query_weight,
        grad_key_weight,
        grad_value_weight,
        grad_merge_weight,
        grad_query_bias,
        grad_value_bias,
        grad_merge_bias,
        grad_head_gain,
        grad_distance_table,
        grad_first_gain,
        grad_first_shift,
        grad_second_gain,
        grad_second_shift,
        grad_expand_weight,
        grad_expand_bias,
        grad_reduce_weight,
        grad_reduce_bias,
        grad_image_weight,
        grad_stem_gain,
        grad_stem_shift,
    ) = lax.psum(
        (
            grad_query_weight,
            grad_key_weight,
            grad_value_weight,
            grad_merge_weight,
            grad_query_bias,
            grad_value_bias,
            grad_merge_bias,
            grad_head_gain,
            grad_distance_table,
            grad_first_gain,
            grad_first_shift,
            grad_second_gain,
            grad_second_shift,
            grad_expand_weight,
            grad_expand_bias,
            grad_reduce_weight,
            grad_reduce_bias,
            grad_image_weight,
            gain_local,
            shift_local,
        ),
        "dp",
    )
    patch_grad = (
        patch_mask[:, None]
        * stem_inverse
        * stem_gain
        * (grad_stem - grad_stem_shift / count - stem_hat * grad_stem_gain / count)
    )
    return (
        block_output,
        input_grad,
        patch_grad,
        grad_query_weight,
        grad_key_weight,
        grad_value_weight,
        grad_merge_weight,
        grad_query_bias,
        grad_value_bias,
        grad_merge_bias,
        grad_head_gain,
        grad_distance_table,
        grad_first_gain,
        grad_first_shift,
        grad_second_gain,
        grad_second_shift,
        grad_expand_weight,
        grad_expand_bias,
        grad_reduce_weight,
        grad_reduce_bias,
        grad_image_weight,
        grad_stem_gain,
        grad_stem_shift,
    )


def solution(mesh):
    in_specs = (
        P("dp", None),
        P("dp", "tensor"),
        P("dp"),
        P("dp"),
        P("dp", None),
        P(None, "tensor"),
        P(None, "tensor"),
        P(None, "tensor"),
        P("tensor", None),
        P("tensor"),
        P("tensor"),
        P(),
        P("tensor"),
        P("tensor", None),
        P(),
        P(),
        P(),
        P(),
        P(None, "tensor"),
        P("tensor"),
        P("tensor", None),
        P(),
        P("tensor", None),
        P("tensor"),
        P("tensor"),
    )
    out_specs = (
        P("dp", None),
        P("dp", None),
        P("dp", "tensor"),
        P(None, "tensor"),
        P(None, "tensor"),
        P(None, "tensor"),
        P("tensor", None),
        P("tensor"),
        P("tensor"),
        P(),
        P("tensor"),
        P("tensor", None),
        P(),
        P(),
        P(),
        P(),
        P(None, "tensor"),
        P("tensor"),
        P("tensor", None),
        P(),
        P("tensor", None),
        P("tensor"),
        P("tensor"),
    )
    return jax.shard_map(local, mesh=mesh, in_specs=in_specs, out_specs=out_specs, check_vma=False)
```

profile of v0, /device:TPU:0, one launch (start us, length us, event | category | flops | bytes accessed | tf_op | source)
XLA Modules:
  0.0 741.7 jit_solution(8420082085746129560)
XLA Ops:
  8.8 1.7 fusion.9
  10.5 44.6 %all-reduce.4 = (f32[512]{0:T(512)S(1)}, f32[]{:T(128)}, f32[512]{0:T(512)S(1)}) all-reduce(f32[512]{0:T(512)S(1)} %get-tuple-element.34, f32[]{:T(128)} %convert_reduce_fusion.4, f32[512]{0:T(512)S(1)} %get-tuple-element.33), channel_id=1, replica_groups=mesh['dp'=16,'tensor'=2] {'dp'}, use_global_device_ids=true, to_apply=%region_5.0 | all-reduce | flops 1025 | bytes 8200 | tf_op jit(solution)/shard_map/psum | solution.py:92
  56.3 4.3 fusion.48
  61.7 1.9 copy.151
  63.6 3.2 slice.9
  66.7 6.6 reshape.233
  73.3 2.8 slice.10
  76.1 3.4 copy.127
  79.9 3.0 fusion.62
  86.7 1.2 copy.124
  87.8 2.1 reshape.231
  90.0 3.4 add_convert_fusion.4
  93.4 2.3 copy.123
  95.7 2.6 reshape.230
  98.3 3.3 fusion.63
  102.7 1.8 copy-done.2
  104.8 1.9 add_convert_fusion.5
  106.7 2.3 copy.122
  108.9 2.6 reshape.229
  111.6 5.2 fusion.21
  118.5 2.7 fusion.64
  121.2 24.6 %all-reduce.15.cloned.1.call-done = f32[1024,768]{1,0:T(8,128)} async-done(((f32[1024,768]{1,0:T(8,128)}), f32[1024,768]{1,0:T(8,128)}) %all-reduce.15.cloned.1.call-update) | async-done | bytes 3145744 | tf_op jit(solution)/shard_map/psum | solution.py:128
  145.8 3.3 fusion.61
  149.9 17.4 %multiply_convert_fusion.1 = (bf16[1024,1536]{1,0:T(8,128)(2,1)}, f32[1024,1536]{1,0:T(8,128)S(1)}, f32[1024,1536]{1,0:T(8,128)S(1)}) fusion(f32[1536]{0:T(1024)S(1)} %copy-done.61, bf16[768,1536]{1,0:T(8,128)(2,1)S(1)} %copy-done, f32[1024,768]{1,0:T(8,128)S(1)} %get-tuple-element.69, f32[768]{0:T(1024)S(1)} %copy-done.62, f32[768]{0:T(1024)S(1)} %copy-done.50, ...), kind=kOutput, calls=%fused_computation.7 | convolution fusion | flops 2523660288 | bytes 21254144 | tf_op jit(solution)/shard_map/dot_general | solution.py:134
  167.4 5.0 convert_reduce_fusion
  172.4 1.7 copy-done.66
  174.1 4.3 fusion.66
  178.5 1.6 copy-done.60
  180.0 6.5 fusion.65
  186.5 16.5 %all-reduce.17.cloned.1.call-done = f32[1024,768]{1,0:T(8,128)} async-done(((f32[1024,768]{1,0:T(8,128)}), f32[1024,768]{1,0:T(8,128)}) %all-reduce.17.cloned.1.call-update) | async-done | bytes 3145744 | tf_op jit(solution)/shard_map/psum | solution.py:149
  203.1 3.7 multiply_reduce_fusion.1
  207.8 1.4 fusion.59
  209.2 1.7 copy-done.8
  210.9 2.2 fusion.31
  213.1 2.2 reshape.235
  215.4 7.2 multiply_reduce_fusion
  222.5 7.9 %convert_reduce_fusion.1 = (f32[6,256,256]{1,2,0:T(8,128)}, bf16[4,6,256,256]{2,3,1,0:T(8,128)(2,1)S(1)}) fusion(f32[4,6,256,256]{2,3,1,0:T(8,128)} %get-tuple-element.85, f32[4,6,256]{2,1,0:T(8,128)S(1)} %get-tuple-element.84, f32[4,6,256,256]{2,3,1,0:T(8,128)} %copy-done.2, f32[4,6,256]{2,1,0:T(8,128)S(1)} %log_add_fusion), kind=kLoop, calls=%fused_computation.3 | loop fusion | flops 9043968 | bytes 17350656 | tf_op jit(solution)/shard_map/reduce_sum | solution.py:169
  232.7 1.3 convert_reduce_fusion.2
  239.6 2.7 add_add_fusion.3
  242.6 7.7 %fusion.40 = f32[1536,768]{1,0:T(8,128)} fusion(bf16[1024,1536]{1,0:T(8,128)(2,1)} %get-tuple-element.66, bf16[1024,768]{1,0:T(8,128)(2,1)} %param.29, f32[1024]{0:T(1024)S(1)} %bitcast.114), kind=kOutput, calls=%fused_computation.90 | convolution fusion | flops 2418278400 | bytes 9441280 | tf_op jit(solution)/shard_map/tc,td->cd/dot_general | solution.py:49
  250.3 4.7 fusion.54
  255.1 2.0 fusion.69
  257.1 2.0 fusion.70
  259.2 2.0 fusion.71
  262.1 2.2 fusion.29
  264.3 11.6 %all-reduce.21.cloned.1.call-done = (f32[1024,768]{1,0:T(8,128)}, f32[1024,768]{1,0:T(8,128)}) async-done(((f32[1024,768]{1,0:T(8,128)}, f32[1024,768]{1,0:T(8,128)}), (f32[1024,768]{1,0:T(8,128)}, f32[1024,768]{1,0:T(8,128)})) %all-reduce.21.cloned.1.call-update) | async-done | bytes 6291472 | tf_op jit(solution)/shard_map/psum | solution.py:137
  275.9 3.6 multiply_reduce_fusion.2
  280.6 1.5 fusion.58
  283.0 1.5 fusion.7
  284.5 1.7 copy-done.13
  286.1 2.5 fusion.46
  288.8 3.0 copy.149
  291.8 3.5 pad.16.clone
  295.3 7.4 reshape.239
  302.7 3.5 pad.17
  306.6 1.6 bitcast_reduce_fusion
  308.3 1.2 fusion.57
  309.5 82.4 %all-reduce.3 = (f32[512]{0:T(512)S(1)}, f32[512]{0:T(512)S(1)}, f32[384]{0:T(512)}, f32[384]{0:T(512)}, f32[768]{0:T(1024)}, /*index=5*/f32[6]{0:T(128)}, f32[6...) all-reduce(f32[512]{0:T(512)S(1)} %get-tuple-element.30, ...), channel_id=1, replica_groups=mesh['dp'=16,'tensor'=2] {'dp'}, use_global_device_ids=true, to_apply=%region_25.26 | all-reduce | flops 11008 | bytes 88064 | tf_op jit(solution)/shard_map/psum | solution.py:230
  392.5 4.5 add_convert_fusion.1
  397.0 2.6 fusion.19
  399.6 322.1 %all-reduce.19.cloned.1.call-done = (f32[768,384]{1,0:T(8,128)}, f32[768,384]{1,0:T(8,128)}, f32[768,384]{1,0:T(8,128)}, f32[384,768]{1,0:T(8,128)}, f32[768,153...) async-done(((f32[768,384]{1,0:T(8,128)}, f32[768,384]{1,0:T(8,128)}, f32[768,384]{1,0:T(8,128)}, f32[384,768]{1,0:T(8,128)}, f32[768,1536]{1,0:T(8,128)}, ...) | async-done | bytes 15728656 | tf_op jit(solution)/shard_map/psum | solution.py:230
  721.7 2.5 copy.201
  727.9 2.2 copy.205
  730.4 2.4 copy.206
  (195 shorter events, 30.9 us)
Async XLA Ops:
  7.2 142.5 %copy-start = (bf16[768,1536]{1,0:T(8,128)(2,1)S(1)}, bf16[768,1536]{1,0:T(8,128)(2,1)}, u32[]{:S(2)}) copy-start(bf16[768,1536]{1,0:T(8,128)(2,1)} %param.43) | copy-start | bytes 7077892
  7.2 72.7 %all-reduce.13.cloned.1.call-start = ((), (), s32[]{:S(2)}) async-start(), calls=%async_computation | async-start | bytes 6291456 | tf_op jit(solution)/shard_map/psum | solution.py:99
  60.6 85.2 %all-reduce.15.cloned.1.call-start = ((), (), s32[]{:S(2)}) async-start(), calls=%async_computation.1 | async-start | bytes 6291456 | tf_op jit(solution)/shard_map/psum | solution.py:128
  82.9 1.7 copy-start.3
  83.4 2.3 copy-start.41
  85.7 4.3 copy-start.63
  101.6 2.9 copy-start.2
  101.6 2.9 copy-start.34
  101.6 3.1 copy-start.43
  101.7 3.1 copy-start.64
  104.8 6.8 copy-start.52
  116.8 1.7 copy-start.30
  118.5 27.4 %copy-start.55 = (f32[768]{0:T(1024)S(1)}, f32[768]{0:T(1024)}, u32[]{:S(2)}) copy-start(f32[768]{0:T(1024)} %param.36) | copy-start | bytes 9220
  121.2 81.9 %all-reduce.17.cloned.1.call-start = ((), (), s32[]{:S(2)}) async-start(), calls=%async_computation.2 | async-start | bytes 6291456 | tf_op jit(solution)/shard_map/psum | solution.py:149
  149.1 18.3 %copy-start.5 = (f32[1024,768]{1,0:T(8,128)}, f32[1024,768]{1,0:T(8,128)S(1)}, u32[]{:S(2)}) copy-start(f32[1024,768]{1,0:T(8,128)S(1)} %get-tuple-element.69) | copy-start | bytes 9437188
  149.9 17.5 %copy-start.18 = (bf16[1024,768]{1,0:T(8,128)(2,1)S(1)}, bf16[1024,768]{1,0:T(8,128)(2,1)}, u32[]{:S(2)}) copy-start(bf16[1024,768]{1,0:T(8,128)(2,1)} %param.29) | copy-start | bytes 4718596
  149.9 17.5 %copy-start.59 = (bf16[1536,768]{1,0:T(8,128)(2,1)S(1)}, bf16[1536,768]{1,0:T(8,128)(2,1)}, u32[]{:S(2)}) copy-start(bf16[1536,768]{1,0:T(8,128)(2,1)} %param.45) | copy-start | bytes 7077892
  172.4 1.7 copy-start.66
  178.4 1.7 copy-start.60
  178.4 97.5 %all-reduce.21.cloned.1.call-start = ((), (), s32[]{:S(2)}) async-start(), calls=%async_computation.4 | async-start | bytes 12582912 | tf_op jit(solution)/shard_map/psum | solution.py:137
  203.0 3.8 copy-start.6
  203.0 4.7 copy-start.12
  207.8 3.1 copy-start.19
  207.8 3.1 copy-start.31
  209.2 1.7 copy-start.8
  213.1 2.2 copy-start.16
  215.4 17.3 %slice-start = ((s8[6291456]{0:T(1024)(128)(4,1)}), s8[4194304]{0:T(1024)(128)(4,1)S(1)}, s32[]{:S(2)}) async-start(s8[6291456]{0:T(1024)(128)(4,1)} %bitcast.88), calls=%async_computation.5 | async-start | bytes 8388608
  222.5 10.1 %slice-start.1 = ((s8[6291456]{0:T(1024)(128)(4,1)}), s8[2097152]{0:T(1024)(128)(4,1)S(1)}, s32[]{:S(2)}) async-start(s8[6291456]{0:T(1024)(128)(4,1)} %bitcast.88), calls=%async_computation.6 | async-start | bytes 4194304
  235.0 1.8 copy-start.42
  236.8 1.8 copy-start.26
  236.9 2.7 copy-start.44
  242.3 479.4 %all-reduce.19.cloned.1.call-start = ((), (), s32[]{:S(2)}) async-start(), calls=%async_computation.3 | async-start | bytes 31457280 | tf_op jit(solution)/shard_map/psum | solution.py:230
  242.6 7.7 %copy-start.7 = (f32[1024,768]{1,0:T(8,128)S(1)}, f32[1024,768]{1,0:T(8,128)}, u32[]{:S(2)}) copy-start(f32[1024,768]{1,0:T(8,128)} %copy-done.5) | copy-start | bytes 9437188
  242.6 7.7 %copy-start.67 = (bf16[1024,1536]{1,0:T(8,128)(2,1)S(1)}, bf16[1024,1536]{1,0:T(8,128)(2,1)}, u32[]{:S(2)}) copy-start(bf16[1024,1536]{1,0:T(8,128)(2,1)} %copy-done.66) | copy-start | bytes 9437188
  250.3 4.7 copy-start.35
  255.1 2.0 copy-start.27
  257.1 2.0 copy-start.29
  259.1 2.1 copy-start.9
  259.1 2.8 copy-start.20
  259.1 3.0 copy-start.25
  275.9 3.8 copy-start.4
  275.9 4.7 copy-start.11
  280.6 1.9 copy-start.10
  280.6 2.4 copy-start.21
  283.0 3.2 copy-start.15
  283.0 3.2 copy-start.47
  283.0 3.2 copy-start.49
  283.0 3.2 copy-start.56
  283.0 3.2 copy-start.65
  284.5 1.7 copy-start.13
  302.7 3.5 copy-start.22
  306.2 2.1 copy-start.14
  306.2 2.1 copy-start.39
  308.3 84.2 %copy-start.53 = (f32[768]{0:T(1024)S(1)}, f32[768]{0:T(1024)}, u32[]{:S(2)}) copy-start(f32[768]{0:T(1024)} %param.46) | copy-start | bytes 9220
  391.9 5.1 copy-start.58
  391.9 5.1 copy-start.57
  721.7 2.5 copy-start.38
  721.7 3.5 copy-start.37
  721.7 4.5 copy-start.36
  724.2 3.6 copy-start.23
  726.3 3.8 slice-start.2
  727.9 2.5 slice-start.3
  730.4 2.5 copy-start.32
  730.4 4.4 copy-start.1
  (13 other events, 10.7 us)
Sparse Core Ops, SparseCore 0:
  60.7 19.1 all-reduce.12
  121.3 24.4 all-reduce.14
  178.5 24.4 all-reduce.16
  242.4 33.4 all-reduce.20
  288.8 432.9 all-reduce.18
where the time goes:
time: 750 us; the launch traced here: 742 us
  waiting for transfers between devices  375 us (50%)
  blocking collectives  127 us (17%)
  matrix products  96.5 us (13%)
  local copies, waits for them, and re-layouts  85.5 us (11%)
  other arithmetic  42 us (6%)
  between operations  14.9 us (2%)
    psum x1, waiting for transfers between devices, local(): lax.psum((grad_query_weight, grad_key_weight, grad_value_weight, grad_mer...  322 us
    psum x1, blocking collectives, local(): lax.psum((grad_query_weight, grad_key_weight, grad_value_weight, grad_mer...  82.4 us
    psum x1, blocking collectives, local(): lax.psum((jnp.sum(masked, axis=0), jnp.sum(masked * features, axis=0), jn...  44.6 us
    unnamed x160, local copies, waits for them, and re-layouts  37.2 us
    psum x1, waiting for transfers between devices, local(): lax.psum(jnp.dot(scaled_low, merge_weight, preferred_element_type=jnp.flo...  24.6 us
    dot_general x7, matrix products, weight_grad(): jnp.einsum('tc,td->cd', inputs_low, grad_low, preferred_element_type=jnp....  23.2 us
    dot_general x1, matrix products, local(): jnp.dot(second_low, expand_weight, preferred_element_type=jnp.float32)  17.4 us
    dot_general x7, matrix products, project_back(): jnp.einsum('tf,df->td', grad_low, weight, preferred_element_type=jnp.floa...  17.4 us
  transfers between devices with their start and end apart: 5, of which 5 were waited for; matrix products, arithmetic and copies ran while one was open for 10% of the time, Pallas kernels for 0%

commit v1 on v0

--- a/solution.py
+++ b/solution.py
@@ -47,6 +47,60 @@
 
 def weight_grad(inputs_low, grad_low):
     return jnp.einsum("tc,td->cd", inputs_low, grad_low, preferred_element_type=jnp.float32)
+
+
+def swap_core(values):
+    count = lax.axis_size("tensor")
+    pairs = [(core, core ^ 1) for core in range(count)]
+    return values + lax.ppermute(values, "tensor", pairs)
+
+
+def exchange(values, bit):
+    count = lax.axis_size("dp")
+    pairs = [(rank, rank ^ (1 << bit)) for rank in range(count)]
+    return lax.ppermute(values, "dp", pairs)
+
+
+def sum_by_doubling(values):
+    for bit in range(lax.axis_size("dp").bit_length() - 1):
+        values = values + exchange(values, bit)
+    return values
+
+
+def sum_by_halving(values, order):
+    rank = lax.axis_index("dp")
+    for bit in order:
+        half = values.shape[0] // 2
+        side = (rank >> bit) & 1
+        sent = lax.dynamic_slice_in_dim(values, (1 - side) * half, half, 0)
+        kept = lax.dynamic_slice_in_dim(values, side * half, half, 0)
+        values = kept + exchange(sent, bit)
+    for bit in reversed(order):
+        side = (rank >> bit) & 1
+        other = exchange(values, bit)
+        values = jnp.where(
+            side == 1, jnp.concatenate([other, values]), jnp.concatenate([values, other])
+        )
+    return values
+
+
+def orders():
+    bits = tuple(range(lax.axis_size("dp").bit_length() - 1))
+    return bits, (bits[1], bits[0]) + bits[2:]
+
+
+def pack(arrays):
+    flat = jnp.concatenate([entry.reshape(-1) for entry in arrays])
+    short = -flat.shape[0] % 1024
+    return jnp.pad(flat, (0, short)).reshape(-1, 128)
+
+
+def unpack(packed, arrays):
+    flat, at, parts = packed.reshape(-1), 0, []
+    for entry in arrays:
+        parts.append(flat[at : at + entry.size].reshape(entry.shape))
+        at += entry.size
+    return parts
 
 
 def local(
@@ -89,16 +143,20 @@
     valid_rows = key_valid.astype(jnp.float32).reshape(rows)
     features = patch_features.astype(jnp.float32)
     masked = features * patch_mask[:, None]
-    feature_sum, square_sum, count = lax.psum(
-        (jnp.sum(masked, axis=0), jnp.sum(masked * features, axis=0), jnp.sum(patch_mask)), "dp"
+    feature_sum, square_sum, count = sum_by_doubling(
+        jnp.stack(
+            [
+                jnp.sum(masked, axis=0),
+                jnp.sum(masked * features, axis=0),
+                jnp.full((features.shape[1],), jnp.sum(patch_mask)),
+            ]
+        )
     )
     stem_mean = feature_sum / count
     stem_inverse = lax.rsqrt(square_sum / count - stem_mean * stem_mean + EPSILON)
     stem_hat = (features - stem_mean) * stem_inverse
     stem_low = (stem_hat * stem_gain + stem_shift).astype(jnp.bfloat16)
-    embedded = lax.psum(
-        jnp.dot(stem_low, image_weight, preferred_element_type=jnp.float32), "tensor"
-    )
+    embedded = swap_core(jnp.dot(stem_low, image_weight, preferred_element_type=jnp.float32))
     hidden = layer_input.astype(jnp.float32) + patch_mask[:, None] * embedded
     first_normed, first_back = jax.vjp(layer_norm, hidden, first_gain, first_shift)
     first_low = first_normed.astype(jnp.bfloat16)
@@ -125,18 +183,14 @@
     probs_low = jnp.exp(scores - log_total).astype(jnp.bfloat16)
     mixed = jnp.einsum("bhqk,bkhd->bqhd", probs_low, value_low, preferred_element_type=jnp.float32)
     scaled_low = (mixed * head_gain[None, None, :, None]).astype(jnp.bfloat16).reshape(rows, width)
-    branch = lax.psum(
-        jnp.dot(scaled_low, merge_weight, preferred_element_type=jnp.float32), "tensor"
-    )
+    branch = swap_core(jnp.dot(scaled_low, merge_weight, preferred_element_type=jnp.float32))
     middle = hidden + branch + merge_bias
     second_normed, second_back = jax.vjp(layer_norm, middle, second_gain, second_shift)
     second_low = second_normed.astype(jnp.bfloat16)
     expanded = jnp.dot(second_low, expand_weight, preferred_element_type=jnp.float32) + expand_bias
     active, gelu_back = jax.vjp(partial(jax.nn.gelu, approximate=False), expanded)
     active_low = active.astype(jnp.bfloat16)
-    reduced = lax.psum(
-        jnp.dot(active_low, reduce_weight, preferred_element_type=jnp.float32), "tensor"
-    )
+    reduced = swap_core(jnp.dot(active_low, reduce_weight, preferred_element_type=jnp.float32))
     block_output = (middle + reduced + reduce_bias).astype(jnp.bfloat16)
     grad_result = upstream.astype(jnp.float32) * valid_rows[:, None]
     grad_reduce_bias = jnp.sum(grad_result, axis=0)
@@ -146,7 +200,7 @@
     grad_expanded_low = grad_expanded.astype(jnp.bfloat16)
     grad_expand_bias = jnp.sum(grad_expanded_low.astype(jnp.float32), axis=0)
     grad_expand_weight = weight_grad(second_low, grad_expanded_low)
-    grad_second = lax.psum(project_back(grad_expanded_low, expand_weight), "tensor")
+    grad_second = swap_core(project_back(grad_expanded_low, expand_weight))
     grad_middle_part, grad_second_gain, grad_second_shift = second_back(grad_second)
     grad_middle = grad_result + grad_middle_part
     grad_merge_bias = jnp.sum(grad_middle, axis=0)
@@ -190,15 +244,14 @@
     grad_value_low = grad_value_low.reshape(rows, width)
     grad_query_bias = jnp.sum(grad_query_low.astype(jnp.float32), axis=0)
     grad_value_bias = jnp.sum(grad_value_low.astype(jnp.float32), axis=0)
-    grad_query_weight = weight_grad(first_low, grad_query_low)
-    grad_key_weight = weight_grad(first_low, grad_key_low)
-    grad_value_weight = weight_grad(first_low, grad_value_low)
+    grad_heads_low = jnp.concatenate([grad_query_low, grad_key_low, grad_value_low], axis=1)
+    grad_heads_weight = weight_grad(first_low, grad_heads_low)
     grad_first_part = (
         project_back(grad_query_low, query_weight)
         + project_back(grad_key_low, key_weight)
         + project_back(grad_value_low, value_weight)
     )
-    grad_first = lax.psum(grad_first_part, "tensor")
+    grad_first = swap_core(grad_first_part)
     grad_hidden_part, grad_first_gain, grad_first_shift = first_back(grad_first)
     input_grad = grad_middle + grad_hidden_part
     grad_embedded_low = (input_grad * patch_mask[:, None]).astype(jnp.bfloat16)
@@ -206,11 +259,19 @@
     grad_stem = project_back(grad_embedded_low, image_weight)
     shift_local = jnp.sum(grad_stem, axis=0)
     gain_local = jnp.sum(grad_stem * stem_hat, axis=0)
-    (
-        grad_query_weight,
-        grad_key_weight,
-        grad_value_weight,
-        grad_merge_weight,
+    first_order, second_order = orders()
+    grad_reduce_weight = lax.psum(grad_reduce_weight, "dp")
+    grad_expand_weight = sum_by_halving(grad_expand_weight, second_order)
+    merge_rows = grad_merge_weight.shape[0]
+    row_weights = sum_by_halving(
+        jnp.concatenate([grad_merge_weight, grad_image_weight]), second_order
+    )
+    grad_merge_weight, grad_image_weight = row_weights[:merge_rows], row_weights[merge_rows:]
+    grad_heads_weight = sum_by_halving(grad_heads_weight, first_order)
+    grad_query_weight = grad_heads_weight[:, :width]
+    grad_key_weight = grad_heads_weight[:, width : 2 * width]
+    grad_value_weight = grad_heads_weight[:, 2 * width :]
+    small = (
         grad_query_bias,
         grad_value_bias,
         grad_merge_bias,
@@ -220,38 +281,26 @@
         grad_first_shift,
         grad_second_gain,
         grad_second_shift,
-        grad_expand_weight,
         grad_expand_bias,
-        grad_reduce_weight,
         grad_reduce_bias,
-        grad_image_weight,
+        gain_local,
+        shift_local,
+    )
+    (
+        grad_query_bias,
+        grad_value_bias,
+        grad_merge_bias,
+        grad_head_gain,
+        grad_distance_table,
+        grad_first_gain,
+        grad_first_shift,
+        grad_second_gain,
+        grad_second_shift,
+        grad_expand_bias,
+        grad_reduce_bias,
         grad_stem_gain,
         grad_stem_shift,
-    ) = lax.psum(
-        (
-            grad_query_weight,
-            grad_key_weight,
-            grad_value_weight,
-            grad_merge_weight,
-            grad_query_bias,
-            grad_value_bias,
-            grad_merge_bias,
-            grad_head_gain,
-            grad_distance_table,
-            grad_first_gain,
-            grad_first_shift,
-            grad_second_gain,
-            grad_second_shift,
-            grad_expand_weight,
-            grad_expand_bias,
-            grad_reduce_weight,
-            grad_reduce_bias,
-            grad_image_weight,
-            gain_local,
-            shift_local,
-        ),
-        "dp",
-    )
+    ) = unpack(sum_by_doubling(pack(small)), small)
     patch_grad = (
         patch_mask[:, None]
         * stem_inverse

time: 750 us -> 611 us (0.81)
  blocking collectives: 127 us -> 0 us
  waiting for transfers between devices: 375 us -> 281 us
  starting transfers between devices: 0.42 us -> 51.4 us
  other arithmetic: 42 us -> 73.3 us
  local copies, waits for them, and re-layouts: 85.5 us -> 93.8 us
    psum x5 -> x1, waiting for transfers between devices: 375 us -> 67.6 us  [local(): grad_reduce_weight = lax.psum(grad_reduce_weight, 'dp')]
    ppermute x0 -> x37, waiting for transfers between devices: none -> 214 us  [the longest x32 211 us: exchange(): return lax.ppermute(values, 'dp', pairs)]
    psum x2 -> x0, blocking collectives: 127 us -> none  [the longest x1 82.4 us: local(): lax.psum((grad_query_weight, grad_key_weight, grad_value_weight, grad_mer...]
    ppermute x0 -> x37, starting transfers between devices: none -> 51.3 us  [the longest x32 50.2 us: exchange(): return lax.ppermute(values, 'dp', pairs)]
    select_n x0 -> x12, other arithmetic: none -> 24 us  [sum_by_halving(): jnp.where(side == 1, jnp.concatenate([other, values]), jnp.concatenate([v...]
    add x0 -> x21, other arithmetic: none -> 10 us  [the longest x12 8.71 us: sum_by_halving(): values = kept + exchange(sent, bit)]
    dot_general x7 -> x5, matrix products: 23.2 us -> 13.3 us  [weight_grad(): jnp.einsum('tc,td->cd', inputs_low, grad_low, preferred_element_type=jnp....]
    unnamed x160 -> x164, local copies, waits for them, and re-layouts: 37.2 us -> 31.3 us
  transfers between devices with their start and end apart: 5 -> 38, of which waited for: 5 -> 21; matrix products, arithmetic and copies ran while one was open for 10% -> 27% of each run, Pallas kernels for 0% -> 0%
where the time goes in v1:
time: 611 us; the launch traced here: 608 us
  waiting for transfers between devices  281 us (46%)
  local copies, waits for them, and re-layouts  93.8 us (15%)
  matrix products  92.7 us (15%)
  other arithmetic  73.3 us (12%)
  starting transfers between devices  51.4 us (8%)
  between operations  15.4 us (3%)
    ppermute x32, waiting for transfers between devices, exchange(): return lax.ppermute(values, 'dp', pairs)  211 us
    psum x1, waiting for transfers between devices, local(): grad_reduce_weight = lax.psum(grad_reduce_weight, 'dp')  67.6 us
    ppermute x32, starting transfers between devices, exchange(): return lax.ppermute(values, 'dp', pairs)  50.2 us
    unnamed x164, local copies, waits for them, and re-layouts  31.3 us
    select_n x12, other arithmetic, sum_by_halving(): jnp.where(side == 1, jnp.concatenate([other, values]), jnp.concatenate([v...  24 us
    dot_general x7, matrix products, project_back(): jnp.einsum('tf,df->td', grad_low, weight, preferred_element_type=jnp.floa...  20.8 us
    dot_general x1, matrix products, local(): jnp.dot(second_low, expand_weight, preferred_element_type=jnp.float32)  19 us
    dot_general x5, matrix products, weight_grad(): jnp.einsum('tc,td->cd', inputs_low, grad_low, preferred_element_type=jnp....  13.3 us
  transfers between devices with their start and end apart: 38, of which 21 were waited for; matrix products, arithmetic and copies ran while one was open for 27% of the time, Pallas kernels for 0%

profile of v1, /device:TPU:0, one launch (start us, length us, event | category | flops | bytes accessed | tf_op | source)
XLA Modules:
  0.0 607.7 jit_solution(3583659250479429453)
XLA Ops:
  11.3 3.0 collective-permute-start
  23.4 3.0 collective-permute-start.3
  28.8 4.2 fusion.58
  33.1 2.9 copy.166
  38.2 3.2 slice.125
  41.4 6.4 %reshape.255 = f32[6,256,511]{2,1,0:T(8,128)} reshape(f32[6,130816]{1,0:T(8,128)} %slice.125) | data formatting | bytes 6279168 | tf_op jit(solution)/shard_map/jvp()/reshape | solution.py:29
  47.8 2.7 slice.126
  50.5 3.0 copy.172
  53.6 4.2 fusion.77
  64.8 3.4 add_convert_fusion.4
  68.2 2.3 copy.168
  70.5 3.1 reshape.252
  73.7 3.4 add_convert_fusion.5
  79.4 2.6 reshape.251
  82.1 3.3 fusion.79
  91.3 2.7 fusion.80
  94.5 2.6 copy.178
  97.1 3.0 collective-permute-done.5
  100.1 4.2 fusion.76
  105.2 19.0 %multiply_convert_fusion.1 = (bf16[1024,1536]{1,0:T(8,128)(2,1)S(1)}, f32[1024,1536]{1,0:T(8,128)}, f32[1024,1536]{1,0:T(8,128)}) fusion(f32[1536]{0:T(1024)S(1)} %copy-done.66, bf16[768,1536]{1,0:T(8,128)(2,1)S(1)} %copy-done, f32[1024,768]{0,1:T(8,128)S(1)} %get-tuple-element.159, f32[768]{0:T(1024)S(1)} %copy-done.67, f32[768]{0:T(1024)S(1)} %copy-done.52, ...), kind=kOutput, calls=%fused_computation.7 | convolution fusion | flops 2523660288 | bytes 21254144 | tf_op jit(solution)/shard_map/dot_general | solution.py:190
  124.2 9.1 %convert_reduce_fusion = (f32[1536]{0:T(1024)S(1)}, bf16[1024,1536]{1,0:T(8,128)(2,1)S(1)}) fusion(f32[1024,1536]{1,0:T(8,128)} %get-tuple-element.157, bf16[1536,768]{1,0:T(8,128)(2,1)S(1)} %copy-done.65, bf16[1024,768]{0,1:T(8,128)(2,1)S(1)} %copy-done.23, f32[1024]{0:T(1024)S(1)} %bitcast.158, f32[1024,1536]{1,0:T(8,128)} %get-tuple-element.190, ...), kind=kOutput, calls=%fused_computation.2 | convolution fusion | flops 2445015552 | bytes 19677184 | tf_op jit(solution)/shard_map/tf,df->td/dot_general | solution.py:45
  133.3 2.8 fusion.69
  139.8 4.4 fusion.82
  144.2 4.3 fusion.81
  149.0 42.9 %collective-permute-done.29 = f32[384,1536]{1,0:T(8,128)} collective-permute-done((f32[384,1536]{1,0:T(8,128)}, f32[384,1536]{1,0:T(8,128)}, u32[]{:S(2)}, u32[]{:S(2)}) %collective-permute-start.29) | collective-permute-done | bytes 2359328 | tf_op jit(solution)/shard_map/ppermute | solution.py:61
  191.9 2.8 dynamic-slice_add_fusion
  197.5 4.0 fusion.71
  202.9 5.3 fusion.74
  211.8 2.4 reshape.257
  214.2 5.0 convert_reduce_fusion.2
  219.2 7.2 %multiply_reduce_fusion = (f32[4,6,256]{2,1,0:T(8,128)S(1)}, f32[4,6,256,256]{2,3,1,0:T(8,128)}) fusion(f32[4,6,256,256]{2,3,1,0:T(8,128)} %copy-done.2, f32[4,6,256]{2,1,0:T(8,128)S(1)} %log_add_fusion, bf16[4,256,6,64]{1,0,3,2:T(4,128)(2,1)S(1)} %copy-done.17, f32[4,256,6,64]{1,0,3,2:T(4,128)S(1)} %reshape.257, f32[6]{0:T(128)S(1)} %copy-done.60), kind=kOutput, calls=%fused_computation.5 | convolution fusion | flops 206825472 | bytes 14991384 | tf_op jit(solution)/shard_map/bqhd,bkhd->bhqk/dot_general | solution.py:218
  226.4 6.0 convert_reduce_fusion.1
  238.1 3.0 copy.209
  244.8 6.6 %reshape.261 = f32[6,130816]{1,0:T(8,128)} reshape(f32[6,256,511]{2,1,0:T(8,128)} %pad.20.clone) | data formatting | bytes 6279168 | tf_op jit(solution)/shard_map/transpose(jvp())/reshape | solution.py:29
  251.4 3.7 pad.21
  255.1 4.0 fusion.10
  270.5 11.1 %collective-permute-done.31 = f32[96,1536]{1,0:T(8,128)S(1)} collective-permute-done((f32[96,1536]{1,0:T(8,128)S(1)}, f32[96,1536]{1,0:T(8,128)S(1)}, u32[]{:S(2)}, u32[]{:S(2)}) %collective-permute-start.31) | collective-permute-done | bytes 589856 | tf_op jit(solution)/shard_map/ppermute | solution.py:61
  281.7 2.6 collective-permute-start.32
  284.3 18.0 %collective-permute-done.13 = f32[384,1152]{1,0:T(8,128)S(1)} collective-permute-done((f32[384,1152]{1,0:T(8,128)S(1)}, f32[384,1152]{1,0:T(8,128)S(1)}, u32[]{:S(2)}, u32[]{:S(2)}) %collective-permute-start.13) | collective-permute-done | bytes 1769504 | tf_op jit(solution)/shard_map/ppermute | solution.py:61
  304.2 2.6 collective-permute-start.33
  307.7 10.8 %collective-permute-done.33 = f32[48,1536]{1,0:T(8,128)S(1)} collective-permute-done((f32[48,1536]{1,0:T(8,128)S(1)}, f32[48,1536]{1,0:T(8,128)S(1)}, u32[]{:S(2)}, u32[]{:S(2)}) %collective-permute-start.33) | collective-permute-done | bytes 294944 | tf_op jit(solution)/shard_map/ppermute | solution.py:61
  320.0 2.6 collective-permute-done.14
  333.1 2.4 fusion.73
  336.2 7.3 %collective-permute-done.15 = f32[96,1152]{1,0:T(8,128)} collective-permute-done((f32[96,1152]{1,0:T(8,128)}, f32[96,1152]{1,0:T(8,128)}, u32[]{:S(2)}, u32[]{:S(2)}) %collective-permute-start.15) | collective-permute-done | bytes 442400 | tf_op jit(solution)/shard_map/ppermute | solution.py:61
  345.3 3.3 collective-permute-start.16
  348.6 13.5 %collective-permute-done.10 = f32[88,128]{1,0:T(8,128)S(1)} collective-permute-done((f32[88,128]{1,0:T(8,128)S(1)}, f32[88,128]{1,0:T(8,128)S(1)}, u32[]{:S(2)}, u32[]{:S(2)}) %collective-permute-start.10) | collective-permute-done | bytes 45088 | tf_op jit(solution)/shard_map/ppermute | solution.py:61
  365.4 2.8 collective-permute-start.17
  368.2 2.8 maximum_select_fusion.6
  372.7 3.3 collective-permute-done.17
  377.2 5.7 collective-permute-done.22
  385.2 4.3 fusion.29
  392.5 3.8 copy.198
  400.8 2.6 collective-permute-start.24
  403.3 11.7 %collective-permute-done.35 = f32[192,1536]{1,0:T(8,128)} collective-permute-done((f32[192,1536]{1,0:T(8,128)}, f32[192,1536]{1,0:T(8,128)}, u32[]{:S(2)}, u32[]{:S(2)}) %collective-permute-start.35) | collective-permute-done | bytes 1179680 | tf_op jit(solution)/shard_map/ppermute | solution.py:61
  415.0 3.0 maximum_select_fusion.3
  423.2 13.1 %collective-permute-done.25 = f32[56,768]{1,0:T(8,128)S(1)} collective-permute-done((f32[56,768]{1,0:T(8,128)S(1)}, f32[56,768]{1,0:T(8,128)S(1)}, u32[]{:S(2)}, u32[]{:S(2)}) %collective-permute-start.25) | collective-permute-done | bytes 172064 | tf_op jit(solution)/shard_map/ppermute | solution.py:61
  440.0 13.2 %collective-permute-done.26 = f32[112,768]{1,0:T(8,128)S(1)} collective-permute-done((f32[112,768]{1,0:T(8,128)S(1)}, f32[112,768]{1,0:T(8,128)S(1)}, u32[]{:S(2)}, u32[]{:S(2)}) %collective-permute-start.26) | collective-permute-done | bytes 344096 | tf_op jit(solution)/shard_map/ppermute | solution.py:61
  458.3 35.2 %collective-permute-done.27 = f32[224,768]{1,0:T(8,128)S(1)} collective-permute-done((f32[224,768]{1,0:T(8,128)S(1)}, f32[224,768]{1,0:T(8,128)S(1)}, u32[]{:S(2)}, u32[]{:S(2)}) %collective-permute-start.27) | collective-permute-done | bytes 688160 | tf_op jit(solution)/shard_map/ppermute | solution.py:61
  498.2 5.3 maximum_select_fusion
  503.5 3.6 maximum_select_fusion.1
  509.0 13.4 %collective-permute-done.28 = f32[448,768]{1,0:T(8,128)} collective-permute-done((f32[448,768]{1,0:T(8,128)}, f32[448,768]{1,0:T(8,128)}, u32[]{:S(2)}, u32[]{:S(2)}) %collective-permute-start.28) | collective-permute-done | bytes 1376288 | tf_op jit(solution)/shard_map/ppermute | solution.py:61
  522.3 3.3 maximum_select_fusion.2
  528.0 67.6 %all-reduce.6.cloned.1.call-done = f32[1536,768]{1,0:T(8,128)} async-done(((f32[1536,768]{1,0:T(8,128)}), f32[1536,768]{1,0:T(8,128)}) %all-reduce.6.cloned.1.call-update) | async-done | bytes 4718608 | tf_op jit(solution)/shard_map/psum | solution.py:263
  595.6 5.0 copy.250
  (315 shorter events, 122.8 us)
Async XLA Ops:
  7.2 97.6 %copy-start = (bf16[768,1536]{1,0:T(8,128)(2,1)S(1)}, bf16[768,1536]{1,0:T(8,128)(2,1)}, u32[]{:S(2)}) copy-start(bf16[768,1536]{1,0:T(8,128)(2,1)} %param.43) | copy-start | bytes 7077892
  7.2 588.4 %all-reduce.6.cloned.1.call-start = ((), (), s32[]{:S(2)}) async-start(), calls=%async_computation | async-start | bytes 9437184 | tf_op jit(solution)/shard_map/psum | solution.py:263
  8.8 44.8 %copy-start.44 = (f32[1,2,4,128]{3,1,2,0:T(2,128)}, f32[1,2,4,128]{3,1,2,0:T(2,128)S(1)}, u32[]{:S(2)}) copy-start(f32[1,2,4,128]{3,1,2,0:T(2,128)S(1)} %copy.210) | copy-start | bytes 12292
  11.3 4.6 collective-permute-start
  16.0 3.7 collective-permute-start.1
  19.7 3.7 collective-permute-start.2
  23.4 4.7 collective-permute-start.3
  33.0 20.7 %collective-permute-start.4 = (f32[1024,768]{0,1:T(8,128)}, f32[1024,768]{0,1:T(8,128)}, u32[]{:S(2)}, u32[]{:S(2)}) collective-permute-start(f32[1024,768]{0,1:T(8,128)} %fusion.58), channel_id=1, source_target_pairs={{0,1},{1,0},{2,3},{3,2},{4,5},{5,4},{6,7},{7,6},{8,9},{9,8},{10,11... | collective-permute-start | bytes 9437192 | tf_op jit(solution)/shard_map/ppermute | solution.py:55
  94.0 6.1 %copy-start.62 = (f32[768]{0:T(1024)S(1)}, f32[768]{0:T(1024)}, u32[]{:S(2)}) copy-start(f32[768]{0:T(1024)} %param.36) | copy-start | bytes 9220
  94.0 6.1 %collective-permute-start.5 = (f32[1024,768]{0,1:T(8,128)}, f32[1024,768]{0,1:T(8,128)}, u32[]{:S(2)}, u32[]{:S(2)}) collective-permute-start(f32[1024,768]{0,1:T(8,128)} %fusion.80), channel_id=1, source_target_pairs={{0,1},{1,0},{2,3},{3,2},{4,5},{5,4},{6,7},{7,6},{8,9},{9,8},{10,11... | collective-permute-start | bytes 9437192 | tf_op jit(solution)/shard_map/ppermute | solution.py:55
  104.4 29.0 %copy-start.5 = (f32[1024,768]{0,1:T(8,128)}, f32[1024,768]{0,1:T(8,128)S(1)}, u32[]{:S(2)}) copy-start(f32[1024,768]{0,1:T(8,128)S(1)} %get-tuple-element.159) | copy-start | bytes 9437188
  105.2 19.0 %copy-start.23 = (bf16[1024,768]{0,1:T(8,128)(2,1)S(1)}, bf16[1024,768]{0,1:T(8,128)(2,1)}, u32[]{:S(2)}) copy-start(bf16[1024,768]{0,1:T(8,128)(2,1)} %copy.178) | copy-start | bytes 4718596
  105.2 19.0 %copy-start.65 = (bf16[1536,768]{1,0:T(8,128)(2,1)S(1)}, bf16[1536,768]{1,0:T(8,128)(2,1)}, u32[]{:S(2)}) copy-start(bf16[1536,768]{1,0:T(8,128)(2,1)} %param.45) | copy-start | bytes 7077892
  124.2 20.1 %copy-start.71 = (bf16[1024,1536]{1,0:T(8,128)(2,1)}, bf16[1024,1536]{1,0:T(8,128)(2,1)S(1)}, u32[]{:S(2)}) copy-start(bf16[1024,1536]{1,0:T(8,128)(2,1)S(1)} %get-tuple-element.156) | copy-start | bytes 9437188
  136.1 8.0 %copy-start.27 = (f32[768,1536]{1,0:T(8,128)}, f32[768,1536]{1,0:T(8,128)S(1)}, u32[]{:S(2)}) copy-start(f32[768,1536]{1,0:T(8,128)S(1)} %fusion.69) | copy-start | bytes 14155780
  137.8 54.0 %collective-permute-start.29 = (f32[384,1536]{1,0:T(8,128)}, f32[384,1536]{1,0:T(8,128)}, u32[]{:S(2)}, u32[]{:S(2)}) collective-permute-start(f32[384,1536]{1,0:T(8,128)} %constant_dynamic-slice_fusion.3), channel_id=1, source_target_pairs={{0,4},{2,6},{4,0},{6,2},{8,12},{10,14},{12,8},{14,10},{16,20},{18,... | collective-permute-start | bytes 7077896 | tf_op jit(solution)/shard_map/ppermute | solution.py:61
  144.1 53.4 %collective-permute-start.7 = (f32[1024,768]{0,1:T(8,128)}, f32[1024,768]{0,1:T(8,128)}, u32[]{:S(2)}, u32[]{:S(2)}) collective-permute-start(f32[1024,768]{0,1:T(8,128)} %fusion.82), channel_id=1, source_target_pairs={{0,1},{1,0},{2,3},{3,2},{4,5},{5,4},{6,7},{7,6},{8,9},{9,8},{10,11... | collective-permute-start | bytes 9437192 | tf_op jit(solution)/shard_map/ppermute | solution.py:55
  148.5 54.3 %collective-permute-start.6 = (f32[1024,768]{0,1:T(8,128)}, f32[1024,768]{0,1:T(8,128)}, u32[]{:S(2)}, u32[]{:S(2)}) collective-permute-start(f32[1024,768]{0,1:T(8,128)} %fusion.81), channel_id=1, source_target_pairs={{0,1},{1,0},{2,3},{3,2},{4,5},{5,4},{6,7},{7,6},{8,9},{9,8},{10,11... | collective-permute-start | bytes 9437192 | tf_op jit(solution)/shard_map/ppermute | solution.py:55
  149.0 48.5 %copy-start.6 = (f32[1024,768]{0,1:T(8,128)S(1)}, f32[1024,768]{0,1:T(8,128)}, u32[]{:S(2)}) copy-start(f32[1024,768]{0,1:T(8,128)} %copy-done.5) | copy-start | bytes 9437188
  194.6 6.9 %copy-start.12 = (f32[384,1536]{1,0:T(8,128)}, f32[384,1536]{1,0:T(8,128)S(1)}, u32[]{:S(2)}) copy-start(f32[384,1536]{1,0:T(8,128)S(1)} %dynamic-slice_add_fusion) | copy-start | bytes 7077892
  195.8 69.1 %collective-permute-start.30 = (f32[192,1536]{1,0:T(8,128)}, f32[192,1536]{1,0:T(8,128)}, u32[]{:S(2)}, u32[]{:S(2)}) collective-permute-start(f32[192,1536]{1,0:T(8,128)} %constant_dynamic-slice_fusion.2), channel_id=1, source_target_pairs={{0,2},{2,0},{4,6},{6,4},{8,10},{10,8},{12,14},{14,12},{16,18},{18,... | collective-permute-start | bytes 3538952 | tf_op jit(solution)/shard_map/ppermute | solution.py:61
  202.8 7.1 %copy-start.34 = (bf16[384,768]{1,0:T(8,128)(2,1)S(1)}, bf16[384,768]{1,0:T(8,128)(2,1)}, u32[]{:S(2)}) copy-start(bf16[384,768]{1,0:T(8,128)(2,1)} %param.33) | copy-start | bytes 1769476
  214.2 12.2 %slice-start = ((s8[6291456]{0:T(1024)(128)(4,1)}), s8[4194304]{0:T(1024)(128)(4,1)S(1)}, s32[]{:S(2)}) async-start(s8[6291456]{0:T(1024)(128)(4,1)} %bitcast.120), calls=%async_computation.1 | async-start | bytes 8388608
  219.2 7.2 %slice-start.1 = ((s8[6291456]{0:T(1024)(128)(4,1)}), s8[2097152]{0:T(1024)(128)(4,1)S(1)}, s32[]{:S(2)}) async-start(s8[6291456]{0:T(1024)(128)(4,1)} %bitcast.120), calls=%async_computation.2 | async-start | bytes 4194304
  226.4 6.0 copy-start.18
  235.2 6.0 copy-start.30
  262.5 39.8 %collective-permute-start.13 = (f32[384,1152]{1,0:T(8,128)S(1)}, f32[384,1152]{1,0:T(8,128)S(1)}, u32[]{:S(2)}, u32[]{:S(2)}) collective-permute-start(f32[384,1152]{1,0:T(8,128)S(1)} %constant_dynamic-slice_fusion.10), channel_id=1, source_target_pairs={{0,2},{2,0},{4,6},{6,4},{8,10},{10,8},{12,14},{14,12},{16,18},{18,... | collective-permute-start | bytes 5308424 | tf_op jit(solution)/shard_map/ppermute | solution.py:61
  267.1 14.4 %collective-permute-start.31 = (f32[96,1536]{1,0:T(8,128)S(1)}, f32[96,1536]{1,0:T(8,128)S(1)}, u32[]{:S(2)}, u32[]{:S(2)}) collective-permute-start(f32[96,1536]{1,0:T(8,128)S(1)} %constant_dynamic-slice_fusion.1), channel_id=1, source_target_pairs={{0,8},{2,10},{4,12},{6,14},{8,0},{10,2},{12,4},{14,6},{16,24},{18,... | collective-permute-start | bytes 1769480 | tf_op jit(solution)/shard_map/ppermute | solution.py:61
  269.9 32.4 %copy-start.29 = (f32[768,1152]{1,0:T(8,128)S(1)}, f32[768,1152]{1,0:T(8,128)}, u32[]{:S(2)}) copy-start(f32[768,1152]{1,0:T(8,128)} %fusion.10) | copy-start | bytes 10616836
  270.0 55.2 %collective-permute-start.8 = (f32[1024,768]{0,1:T(8,128)S(1)}, f32[1024,768]{0,1:T(8,128)S(1)}, u32[]{:S(2)}, u32[]{:S(2)}) collective-permute-start(f32[1024,768]{0,1:T(8,128)S(1)} %add_add_fusion.3), channel_id=1, source_target_pairs={{0,1},{1,0},{2,3},{3,2},{4,5},{5,4},{6,7},{7,6},{8,9},{9,8},{10,11... | collective-permute-start | bytes 9437192 | tf_op jit(solution)/shard_map/ppermute | solution.py:55
  281.7 25.2 %copy-start.8 = (f32[1024,768]{0,1:T(8,128)S(1)}, f32[1024,768]{0,1:T(8,128)}, u32[]{:S(2)}) copy-start(f32[1024,768]{0,1:T(8,128)} %copy-done.7) | copy-start | bytes 9437188
  281.7 25.2 %copy-start.11 = (bf16[48,8,4,256]{3,1,2,0:T(8,128)(2,1)S(1)}, bf16[48,8,4,256]{3,1,2,0:T(8,128)(2,1)}, u32[]{:S(2)}) copy-start(bf16[48,8,4,256]{3,1,2,0:T(8,128)(2,1)} %copy-done.10) | copy-start | bytes 2359300
  281.7 22.5 %collective-permute-start.32 = (f32[48,1536]{1,0:T(8,128)S(1)}, f32[48,1536]{1,0:T(8,128)S(1)}, u32[]{:S(2)}, u32[]{:S(2)}) collective-permute-start(f32[48,1536]{1,0:T(8,128)S(1)} %constant_dynamic-slice_fusion), channel_id=1, source_target_pairs={{0,16},{2,18},{4,20},{6,22},{8,24},{10,26},{12,28},{14,30},{16,0},... | collective-permute-start | bytes 884744 | tf_op jit(solution)/shard_map/ppermute | solution.py:61
  302.6 20.0 %collective-permute-start.14 = (f32[192,1152]{1,0:T(8,128)S(1)}, f32[192,1152]{1,0:T(8,128)S(1)}, u32[]{:S(2)}, u32[]{:S(2)}) collective-permute-start(f32[192,1152]{1,0:T(8,128)S(1)} %constant_dynamic-slice_fusion.9), channel_id=1, source_target_pairs={{0,4},{2,6},{4,0},{6,2},{8,12},{10,14},{12,8},{14,10},{16,20},{18,... | collective-permute-start | bytes 2654216 | tf_op jit(solution)/shard_map/ppermute | solution.py:61
  304.2 14.3 %collective-permute-start.33 = (f32[48,1536]{1,0:T(8,128)S(1)}, f32[48,1536]{1,0:T(8,128)S(1)}, u32[]{:S(2)}, u32[]{:S(2)}) collective-permute-start(f32[48,1536]{1,0:T(8,128)S(1)} %dynamic-slice_add_fusion.8), channel_id=1, source_target_pairs={{0,16},{2,18},{4,20},{6,22},{8,24},{10,26},{12,28},{14,30},{16,0},... | collective-permute-start | bytes 884744 | tf_op jit(solution)/shard_map/ppermute | solution.py:61
  307.7 17.4 %copy-start.4 = (f32[1024,768]{0,1:T(8,128)S(1)}, f32[1024,768]{0,1:T(8,128)}, u32[]{:S(2)}) copy-start(f32[1024,768]{0,1:T(8,128)} %copy-done.3) | copy-start | bytes 9437188
  307.7 17.4 %copy-start.43 = (f32[1024]{0:T(1024)S(1)}, f32[1024]{0:T(1024)}, u32[]{:S(2)}) copy-start(f32[1024]{0:T(1024)} %copy-done.42) | copy-start | bytes 12292
  307.7 17.4 %copy-start.47 = (f32[768]{0:T(1024)S(1)}, f32[768]{0:T(1024)}, u32[]{:S(2)}) copy-start(f32[768]{0:T(1024)} %param.39) | copy-start | bytes 9220
  319.4 48.8 %collective-permute-start.34 = (f32[96,1536]{1,0:T(8,128)}, f32[96,1536]{1,0:T(8,128)}, u32[]{:S(2)}, u32[]{:S(2)}) collective-permute-start(f32[96,1536]{1,0:T(8,128)} %maximum_select_fusion.9), channel_id=1, source_target_pairs={{0,8},{2,10},{4,12},{6,14},{8,0},{10,2},{12,4},{14,6},{16,24},{18,... | collective-permute-start | bytes 1769480 | tf_op jit(solution)/shard_map/ppermute | solution.py:61
  323.6 19.9 %collective-permute-start.15 = (f32[96,1152]{1,0:T(8,128)}, f32[96,1152]{1,0:T(8,128)}, u32[]{:S(2)}, u32[]{:S(2)}) collective-permute-start(f32[96,1152]{1,0:T(8,128)} %constant_dynamic-slice_fusion.8), channel_id=1, source_target_pairs={{0,8},{2,10},{4,12},{6,14},{8,0},{10,2},{12,4},{14,6},{16,24},{18,... | collective-permute-start | bytes 1327112 | tf_op jit(solution)/shard_map/ppermute | solution.py:61
  331.6 31.1 %collective-permute-start.21 = (f32[448,768]{1,0:T(8,128)}, f32[448,768]{1,0:T(8,128)}, u32[]{:S(2)}, u32[]{:S(2)}) collective-permute-start(f32[448,768]{1,0:T(8,128)} %fusion.35), channel_id=1, source_target_pairs={{0,4},{2,6},{4,0},{6,2},{8,12},{10,14},{12,8},{14,10},{16,20},{18,... | collective-permute-start | bytes 4128776 | tf_op jit(solution)/shard_map/ppermute | solution.py:61
  335.6 27.1 %copy-start.22 = (f32[512,768]{1,0:T(8,128)S(1)}, f32[512,768]{1,0:T(8,128)}, u32[]{:S(2)}) copy-start(f32[512,768]{1,0:T(8,128)} %copy-done.21) | copy-start | bytes 4718596
  335.6 9.1 %collective-permute-start.9 = (f32[88,128]{1,0:T(8,128)S(1)}, f32[88,128]{1,0:T(8,128)S(1)}, u32[]{:S(2)}, u32[]{:S(2)}) collective-permute-start(f32[88,128]{1,0:T(8,128)S(1)} %pad_bitcast_fusion), channel_id=1, source_target_pairs={{0,2},{2,0},{4,6},{6,4},{8,10},{10,8},{12,14},{14,12},{16,18},{18,... | collective-permute-start | bytes 135176 | tf_op jit(solution)/shard_map/ppermute | solution.py:61
  344.7 17.4 %collective-permute-start.10 = (f32[88,128]{1,0:T(8,128)S(1)}, f32[88,128]{1,0:T(8,128)S(1)}, u32[]{:S(2)}, u32[]{:S(2)}) collective-permute-start(f32[88,128]{1,0:T(8,128)S(1)} %fusion.65), channel_id=1, source_target_pairs={{0,4},{2,6},{4,0},{6,2},{8,12},{10,14},{12,8},{14,10},{16,20},{18,... | collective-permute-start | bytes 135176 | tf_op jit(solution)/shard_map/ppermute | solution.py:61
  345.3 20.1 %collective-permute-start.16 = (f32[48,1152]{1,0:T(8,128)S(1)}, f32[48,1152]{1,0:T(8,128)S(1)}, u32[]{:S(2)}, u32[]{:S(2)}) collective-permute-start(f32[48,1152]{1,0:T(8,128)S(1)} %constant_dynamic-slice_fusion.7), channel_id=1, source_target_pairs={{0,16},{2,18},{4,20},{6,22},{8,24},{10,26},{12,28},{14,30},{16,0},... | collective-permute-start | bytes 663560 | tf_op jit(solution)/shard_map/ppermute | solution.py:61
  362.1 10.4 %collective-permute-start.11 = (f32[88,128]{1,0:T(8,128)S(1)}, f32[88,128]{1,0:T(8,128)S(1)}, u32[]{:S(2)}, u32[]{:S(2)}) collective-permute-start(f32[88,128]{1,0:T(8,128)S(1)} %fusion.114), channel_id=1, source_target_pairs={{0,8},{2,10},{4,12},{6,14},{8,0},{10,2},{12,4},{14,6},{16,24},{18,... | collective-permute-start | bytes 135176 | tf_op jit(solution)/shard_map/ppermute | solution.py:61
  364.5 18.4 %collective-permute-start.22 = (f32[224,768]{1,0:T(8,128)S(1)}, f32[224,768]{1,0:T(8,128)S(1)}, u32[]{:S(2)}, u32[]{:S(2)}) collective-permute-start(f32[224,768]{1,0:T(8,128)S(1)} %constant_dynamic-slice_fusion.6), channel_id=1, source_target_pairs={{0,2},{2,0},{4,6},{6,4},{8,10},{10,8},{12,14},{14,12},{16,18},{18,... | collective-permute-start | bytes 2064392 | tf_op jit(solution)/shard_map/ppermute | solution.py:61
  365.4 19.8 %copy-start.25 = (bf16[1024,768]{0,1:T(8,128)(2,1)S(1)}, bf16[1024,768]{0,1:T(8,128)(2,1)}, u32[]{:S(2)}) copy-start(bf16[1024,768]{0,1:T(8,128)(2,1)} %copy.178) | copy-start | bytes 4718596
  365.4 19.8 %copy-start.72 = (bf16[1024,1536]{1,0:T(8,128)(2,1)S(1)}, bf16[1024,1536]{1,0:T(8,128)(2,1)}, u32[]{:S(2)}) copy-start(bf16[1024,1536]{1,0:T(8,128)(2,1)} %copy-done.71) | copy-start | bytes 9437188
  365.4 10.6 %collective-permute-start.17 = (f32[48,1152]{1,0:T(8,128)S(1)}, f32[48,1152]{1,0:T(8,128)S(1)}, u32[]{:S(2)}, u32[]{:S(2)}) collective-permute-start(f32[48,1152]{1,0:T(8,128)S(1)} %dynamic-slice_add_fusion.9), channel_id=1, source_target_pairs={{0,16},{2,18},{4,20},{6,22},{8,24},{10,26},{12,28},{14,30},{16,0},... | collective-permute-start | bytes 663560 | tf_op jit(solution)/shard_map/ppermute | solution.py:61
  371.0 44.0 %collective-permute-start.35 = (f32[192,1536]{1,0:T(8,128)}, f32[192,1536]{1,0:T(8,128)}, u32[]{:S(2)}, u32[]{:S(2)}) collective-permute-start(f32[192,1536]{1,0:T(8,128)} %maximum_select_fusion.6), channel_id=1, source_target_pairs={{0,2},{2,0},{4,6},{6,4},{8,10},{10,8},{12,14},{14,12},{16,18},{18,... | collective-permute-start | bytes 3538952 | tf_op jit(solution)/shard_map/ppermute | solution.py:61
  372.5 23.8 %collective-permute-start.12 = (f32[88,128]{1,0:T(8,128)S(1)}, f32[88,128]{1,0:T(8,128)S(1)}, u32[]{:S(2)}, u32[]{:S(2)}) collective-permute-start(f32[88,128]{1,0:T(8,128)S(1)} %add.330), channel_id=1, source_target_pairs={{0,16},{2,18},{4,20},{6,22},{8,24},{10,26},{12,28},{14,30},{16,0},... | collective-permute-start | bytes 135176 | tf_op jit(solution)/shard_map/ppermute | solution.py:61
  376.8 19.5 %collective-permute-start.18 = (f32[96,1152]{1,0:T(8,128)}, f32[96,1152]{1,0:T(8,128)}, u32[]{:S(2)}, u32[]{:S(2)}) collective-permute-start(f32[96,1152]{1,0:T(8,128)} %maximum_select_fusion.10), channel_id=1, source_target_pairs={{0,8},{2,10},{4,12},{6,14},{8,0},{10,2},{12,4},{14,6},{16,24},{18,... | collective-permute-start | bytes 1327112 | tf_op jit(solution)/shard_map/ppermute | solution.py:61
  383.7 16.0 %collective-permute-start.23 = (f32[112,768]{1,0:T(8,128)}, f32[112,768]{1,0:T(8,128)}, u32[]{:S(2)}, u32[]{:S(2)}) collective-permute-start(f32[112,768]{1,0:T(8,128)} %constant_dynamic-slice_fusion.5), channel_id=1, source_target_pairs={{0,8},{2,10},{4,12},{6,14},{8,0},{10,2},{12,4},{14,6},{16,24},{18,... | collective-permute-start | bytes 1032200 | tf_op jit(solution)/shard_map/ppermute | solution.py:61
  398.0 39.5 %collective-permute-start.19 = (f32[192,1152]{1,0:T(8,128)S(1)}, f32[192,1152]{1,0:T(8,128)S(1)}, u32[]{:S(2)}, u32[]{:S(2)}) collective-permute-start(f32[192,1152]{1,0:T(8,128)S(1)} %maximum_select_fusion.7), channel_id=1, source_target_pairs={{0,4},{2,6},{4,0},{6,2},{8,12},{10,14},{12,8},{14,10},{16,20},{18,... | collective-permute-start | bytes 2654216 | tf_op jit(solution)/shard_map/ppermute | solution.py:61
  400.8 21.1 %collective-permute-start.24 = (f32[56,768]{1,0:T(8,128)S(1)}, f32[56,768]{1,0:T(8,128)S(1)}, u32[]{:S(2)}, u32[]{:S(2)}) collective-permute-start(f32[56,768]{1,0:T(8,128)S(1)} %constant_dynamic-slice_fusion.4), channel_id=1, source_target_pairs={{0,16},{2,18},{4,20},{6,22},{8,24},{10,26},{12,28},{14,30},{16,0},... | collective-permute-start | bytes 516104 | tf_op jit(solution)/shard_map/ppermute | solution.py:61
  418.0 38.3 %copy-start.15 = (f32[1024,512]{1,0:T(8,128)S(1)}, f32[1024,512]{1,0:T(8,128)}, u32[]{:S(2)}) copy-start(f32[1024,512]{1,0:T(8,128)} %get-tuple-element.199) | copy-start | bytes 6291460
  418.0 80.2 %collective-permute-start.36 = (f32[384,1536]{1,0:T(8,128)S(1)}, f32[384,1536]{1,0:T(8,128)}, u32[]{:S(2)}, u32[]{:S(2)}) collective-permute-start(f32[384,1536]{1,0:T(8,128)S(1)} %maximum_select_fusion.3), channel_id=1, source_target_pairs={{0,4},{2,6},{4,0},{6,2},{8,12},{10,14},{12,8},{14,10},{16,20},{18,... | collective-permute-start | bytes 7077896 | tf_op jit(solution)/shard_map/ppermute | solution.py:61
  421.9 14.4 %collective-permute-start.25 = (f32[56,768]{1,0:T(8,128)S(1)}, f32[56,768]{1,0:T(8,128)S(1)}, u32[]{:S(2)}, u32[]{:S(2)}) collective-permute-start(f32[56,768]{1,0:T(8,128)S(1)} %dynamic-slice_add_fusion.10), channel_id=1, source_target_pairs={{0,16},{2,18},{4,20},{6,22},{8,24},{10,26},{12,28},{14,30},{16,0},... | collective-permute-start | bytes 516104 | tf_op jit(solution)/shard_map/ppermute | solution.py:61
  436.4 16.8 %collective-permute-start.26 = (f32[112,768]{1,0:T(8,128)S(1)}, f32[112,768]{1,0:T(8,128)S(1)}, u32[]{:S(2)}, u32[]{:S(2)}) collective-permute-start(f32[112,768]{1,0:T(8,128)S(1)} %maximum_select_fusion.11), channel_id=1, source_target_pairs={{0,8},{2,10},{4,12},{6,14},{8,0},{10,2},{12,4},{14,6},{16,24},{18,... | collective-permute-start | bytes 1032200 | tf_op jit(solution)/shard_map/ppermute | solution.py:61
  437.5 20.8 %copy-start.59 = (f32[512]{0:T(512)}, f32[512]{0:T(512)S(1)}, u32[]{:S(2)}) copy-start(f32[512]{0:T(512)S(1)} %get-tuple-element.221) | copy-start | bytes 6148
  438.9 64.6 %collective-permute-start.20 = (f32[384,1152]{1,0:T(8,128)}, f32[384,1152]{1,0:T(8,128)}, u32[]{:S(2)}, u32[]{:S(2)}) collective-permute-start(f32[384,1152]{1,0:T(8,128)} %maximum_select_fusion.4), channel_id=1, source_target_pairs={{0,2},{2,0},{4,6},{6,4},{8,10},{10,8},{12,14},{14,12},{16,18},{18,... | collective-permute-start | bytes 5308424 | tf_op jit(solution)/shard_map/ppermute | solution.py:61
  453.3 40.3 %collective-permute-start.27 = (f32[224,768]{1,0:T(8,128)S(1)}, f32[224,768]{1,0:T(8,128)S(1)}, u32[]{:S(2)}, u32[]{:S(2)}) collective-permute-start(f32[224,768]{1,0:T(8,128)S(1)} %maximum_select_fusion.8), channel_id=1, source_target_pairs={{0,2},{2,0},{4,6},{6,4},{8,10},{10,8},{12,14},{14,12},{16,18},{18,... | collective-permute-start | bytes 2064392 | tf_op jit(solution)/shard_map/ppermute | solution.py:61
  494.7 27.6 %collective-permute-start.28 = (f32[448,768]{1,0:T(8,128)}, f32[448,768]{1,0:T(8,128)}, u32[]{:S(2)}, u32[]{:S(2)}) collective-permute-start(f32[448,768]{1,0:T(8,128)} %maximum_select_fusion.5), channel_id=1, source_target_pairs={{0,4},{2,6},{4,0},{6,2},{8,12},{10,14},{12,8},{14,10},{16,20},{18,... | collective-permute-start | bytes 4128776 | tf_op jit(solution)/shard_map/ppermute | solution.py:61
  (49 other events, 113.7 us)
Sparse Core Ops, SparseCore 0:
  389.7 205.8 all-reduce.5

commit v2 on v1

v2 whole, which is shorter than its diff:
```python
from functools import partial

import jax
import jax.numpy as jnp
from jax import lax
from jax.experimental import pallas as pl
from jax.experimental.pallas import tpu as pltpu
from jax.sharding import PartitionSpec as P

HEAD_DIM = 64
PATCH_SMALL = 64
PATCH_LARGE = 225
EPSILON = 1e-05
NEGATIVE = -1e30
SCALE = HEAD_DIM ** (-0.5)
LANES = 128
FULL = ((1,), (0,))
RIGHT = ((1,), (1,))
LEFT = ((0,), (0,))


def mult(left, right, dims=FULL):
    return lax.dot_general(left, right, (dims, ((), ())), preferred_element_type=jnp.float32)


def rows_of(length):
    return pl.BlockSpec((length[0], length[1]), lambda item, *_: (item, 0))


def whole(shape):
    return pl.BlockSpec(shape, lambda item, *_: (0,) * len(shape))


def normed(values):
    centered = values - jnp.mean(values, axis=-1, keepdims=True)
    inverse = lax.rsqrt(jnp.mean(centered * centered, axis=-1, keepdims=True) + EPSILON)
    return centered * inverse, inverse


def before(length, limit):
    slots = lax.broadcasted_iota(jnp.int32, (length, 1), 0)
    return jnp.where(slots < limit, 1.0, 0.0).astype(jnp.float32)


def norm_back(normal, inverse, grad, gain):
    scaled = grad * gain
    first = jnp.mean(scaled, axis=-1, keepdims=True)
    second = jnp.mean(scaled * normal, axis=-1, keepdims=True)
    return (scaled - first - normal * second) * inverse


def row_sum(values):
    return jnp.sum(values, axis=0, keepdims=True)


def start_sums(*refs):
    @pl.when(pl.program_id(0) == 0)
    def _():
        for ref in refs:
            ref[...] = jnp.zeros(ref.shape, ref.dtype)


def bias_kernel(table_ref, out_ref):
    length = out_ref.shape[1]
    for head in range(out_ref.shape[0]):
        rows = jnp.broadcast_to(table_ref[head : head + 1, :], (length, 2 * length))
        turned = pltpu.roll(rows, length + 1, 1, stride=1, stride_axis=0)
        out_ref[head] = turned[:, :length]


def distance_bias(table, length):
    heads = table.shape[0]
    padded = jnp.pad(table, ((0, 0), (0, 2 * length - table.shape[1])))
    return pl.pallas_call(
        bias_kernel,
        out_shape=jax.ShapeDtypeStruct((heads, length, length), jnp.float32),
        name="distance_bias",
    )(padded)


def half_of(pair, side):
    lanes = lax.broadcasted_iota(jnp.int32, pair.shape, 1)
    keep = lanes < HEAD_DIM if side == 0 else lanes >= HEAD_DIM
    return jnp.where(keep, pair, jnp.zeros_like(pair))


def join(left, right):
    lanes = lax.broadcasted_iota(jnp.int32, left.shape, 1)
    return jnp.where(lanes < HEAD_DIM, left, right)


def attend_kernel(
    patches_ref,
    valid_ref,
    input_ref,
    own_ref,
    other_ref,
    gain_ref,
    shift_ref,
    heads_weight_ref,
    heads_bias_ref,
    bias_ref,
    head_gain_ref,
    merge_ref,
    hidden_ref,
    first_ref,
    heads_ref,
    probs_ref,
    mixed_ref,
    scaled_ref,
    branch_ref,
):
    item = pl.program_id(0)
    length = input_ref.shape[0]
    width = mixed_ref.shape[1]
    mask = before(length, patches_ref[item])
    hidden = input_ref[...].astype(jnp.float32) + mask * (own_ref[...] + other_ref[...])
    hidden_ref[...] = hidden
    normal, _ = normed(hidden)
    first = (normal * gain_ref[...] + shift_ref[...]).astype(jnp.bfloat16)
    first_ref[...] = first
    heads_ref[...] = (mult(first, heads_weight_ref[...]) + heads_bias_ref[...]).astype(jnp.bfloat16)
    slots = lax.broadcasted_iota(jnp.int32, (length, length), 1)
    valid = slots < valid_ref[item]
    for pair in range(width // LANES):
        at = pair * LANES
        queries = heads_ref[:, at : at + LANES]
        keys = heads_ref[:, width + at : width + at + LANES]
        values = heads_ref[:, 2 * width + at : 2 * width + at + LANES]
        halves = []
        for side in range(2):
            head = 2 * pair + side
            scores = mult(half_of(queries, side), keys, RIGHT) * SCALE + bias_ref[head]
            scores = jnp.where(valid, scores, NEGATIVE)
            peak = jnp.max(scores, axis=-1, keepdims=True)
            powers = jnp.exp(scores - peak)
            probs = powers * (1.0 / jnp.sum(powers, axis=-1, keepdims=True))
            probs_ref[0, head] = probs
            halves.append(mult(probs.astype(jnp.bfloat16), values))
        mixed = join(*halves)
        mixed_ref[:, at : at + LANES] = mixed
        gains = head_gain_ref[:, at : at + LANES]
        scaled_ref[:, at : at + LANES] = (mixed * gains).astype(jnp.bfloat16)
    branch_ref[...] = mult(scaled_ref[...], merge_ref[...])


def attend(
    patches,
    valid,
    layer_input,
    own,
    other,
    gain,
    shift,
    heads_weight,
    heads_bias,
    bias,
    head_gain,
    merge,
):
    items = patches.shape[0]
    rows, model = layer_input.shape
    length = rows // items
    width = merge.shape[0]
    heads = bias.shape[0]
    out = lambda columns, kind: jax.ShapeDtypeStruct((rows, columns), kind)
    return pl.pallas_call(
        attend_kernel,
        grid_spec=pltpu.PrefetchScalarGridSpec(
            num_scalar_prefetch=2,
            grid=(items,),
            in_specs=[
                rows_of((length, model)),
                rows_of((length, model)),
                rows_of((length, model)),
                whole((1, model)),
                whole((1, model)),
                whole(heads_weight.shape),
                whole(heads_bias.shape),
                whole(bias.shape),
                whole(head_gain.shape),
                whole(merge.shape),
            ],
            out_specs=[
                rows_of((length, model)),
                rows_of((length, model)),
                rows_of((length, 3 * width)),
                pl.BlockSpec((1, heads, length, length), lambda item, *_: (item, 0, 0, 0)),
                rows_of((length, width)),
                rows_of((length, width)),
                rows_of((length, model)),
            ],
        ),
        out_shape=[
            out(model, jnp.float32),
            out(model, jnp.bfloat16),
            out(3 * width, jnp.bfloat16),
            jax.ShapeDtypeStruct((items, heads, length, length), jnp.float32),
            out(width, jnp.float32),
            out(width, jnp.bfloat16),
            out(model, jnp.float32),
        ],
        name="attend",
    )(
        patches,
        valid,
        layer_input,
        own,
        other,
        gain,
        shift,
        heads_weight,
        heads_bias,
        bias,
        head_gain,
        merge,
    )


def error_function(values):
    limited = jnp.clip(values, -3.7439211, 3.7439211)
    square = limited * limited
    top = jnp.full_like(square, 2.2905065861350646e-4)
    for factor in (
        3.4082910107109506e-3,
        5.0955695062380861e-2,
        1.8520832239976145e-1,
        1.128379143519084,
    ):
        top = top * square + factor
    bottom = jnp.full_like(square, -1.1791602954361697e-7)
    for factor in (
        2.3547966471313185e-5,
        1.0179625278914885e-3,
        1.4070470171167667e-2,
        1.1098505178285362e-1,
        4.9746925110067538e-1,
        1.0,
    ):
        bottom = bottom * square + factor
    return limited * top / bottom


def feed_kernel(
    valid_ref,
    hidden_ref,
    own_ref,
    other_ref,
    merge_bias_ref,
    gain_ref,
    shift_ref,
    expand_ref,
    expand_bias_ref,
    reduce_ref,
    upstream_ref,
    middle_ref,
    second_ref,
    active_ref,
    grad_expanded_ref,
    reduced_ref,
    grad_second_ref,
    grad_reduced_ref,
    expand_sum_ref,
    reduce_sum_ref,
):
    item = pl.program_id(0)
    length = hidden_ref.shape[0]
    start_sums(expand_sum_ref, reduce_sum_ref)
    middle = hidden_ref[...] + (own_ref[...] + other_ref[...]) + merge_bias_ref[...]
    middle_ref[...] = middle
    normal, _ = normed(middle)
    second = (normal * gain_ref[...] + shift_ref[...]).astype(jnp.bfloat16)
    second_ref[...] = second
    grad_result = upstream_ref[...].astype(jnp.float32) * before(length, valid_ref[item])
    reduce_sum_ref[...] += row_sum(grad_result)
    grad_reduced = grad_result.astype(jnp.bfloat16)
    grad_reduced_ref[...] = grad_reduced
    hidden_units = expand_ref.shape[1]
    part = hidden_units // 3
    reduced = None
    for at in range(0, hidden_units, part):
        span = slice(at, at + part)
        expanded = mult(second, expand_ref[:, span]) + expand_bias_ref[:, span]
        cumulative = 0.5 + 0.5 * error_function(expanded * 0.7071067811865476)
        active = (expanded * cumulative).astype(jnp.bfloat16)
        density = jnp.exp(expanded * expanded * -0.5) * 0.3989422804014327
        slope = cumulative + expanded * density
        active_ref[:, span] = active
        grad_active = mult(grad_reduced, reduce_ref[span, :], RIGHT)
        grad_expanded = (grad_active * slope).astype(jnp.bfloat16)
        grad_expanded_ref[:, span] = grad_expanded
        expand_sum_ref[:, span] += row_sum(grad_expanded.astype(jnp.float32))
        reduced_part = mult(active, reduce_ref[span, :])
        grad_part = mult(grad_expanded, expand_ref[:, span], RIGHT)
        if reduced is None:
            reduced, grad_second = reduced_part, grad_part
        else:
            reduced, grad_second = reduced + reduced_part, grad_second + grad_part
    reduced_ref[...] = reduced
    grad_second_ref[...] = grad_second


def feed(
    valid,
    hidden,
    own,
    other,
    merge_bias,
    gain,
    shift,
    expand,
    expand_bias,
    reduce_weight,
    upstream,
):
    items = valid.shape[0]
    rows, model = hidden.shape
    length = rows // items
    units = expand.shape[1]
    out = lambda columns, kind: jax.ShapeDtypeStruct((rows, columns), kind)
    model_rows = rows_of((length, model))
    unit_rows = rows_of((length, units))
    return pl.pallas_call(
        feed_kernel,
        grid_spec=pltpu.PrefetchScalarGridSpec(
            num_scalar_prefetch=1,
            grid=(items,),
            in_specs=[
                model_rows,
                model_rows,
                model_rows,
                whole((1, model)),
                whole((1, model)),
                whole((1, model)),
                whole(expand.shape),
                whole(expand_bias.shape),
                whole(reduce_weight.shape),
                model_rows,
            ],
            out_specs=[
                model_rows,
                model_rows,
                unit_rows,
                unit_rows,
                model_rows,
                model_rows,
                model_rows,
                whole((1, units)),
                whole((1, model)),
            ],
        ),
        out_shape=[
            out(model, jnp.float32),
            out(model, jnp.bfloat16),
            out(units, jnp.bfloat16),
            out(units, jnp.bfloat16),
            out(model, jnp.float32),
            out(model, jnp.float32),
            out(model, jnp.bfloat16),
            jax.ShapeDtypeStruct((1, units), jnp.float32),
            jax.ShapeDtypeStruct((1, model), jnp.float32),
        ],
        name="feed",
    )(
        valid,
        hidden,
        own,
        other,
        merge_bias,
        gain,
        shift,
        expand,
        expand_bias,
        reduce_weight,
        upstream,
    )


def attend_back_kernel(
    middle_ref,
    own_ref,
    other_ref,
    grad_reduced_ref,
    gain_ref,
    merge_ref,
    mixed_ref,
    head_gain_ref,
    probs_ref,
    heads_ref,
    heads_weight_ref,
    grad_middle_ref,
    grad_branch_ref,
    grad_heads_ref,
    grad_first_ref,
    gain_sum_ref,
    shift_sum_ref,
    merge_sum_ref,
    head_sum_ref,
    heads_sum_ref,
    table_ref,
    total_ref,
):
    item = pl.program_id(0)
    length = middle_ref.shape[0]
    width = mixed_ref.shape[1]
    start_sums(gain_sum_ref, shift_sum_ref, merge_sum_ref, head_sum_ref, heads_sum_ref, total_ref)
    normal, inverse = normed(middle_ref[...])
    grad_second = own_ref[...] + other_ref[...]
    gain_sum_ref[...] += row_sum(grad_second * normal)
    shift_sum_ref[...] += row_sum(grad_second)
    grad_middle = grad_reduced_ref[...].astype(jnp.float32) + norm_back(
        normal, inverse, grad_second, gain_ref[...]
    )
    grad_middle_ref[...] = grad_middle
    merge_sum_ref[...] += row_sum(grad_middle)
    grad_branch = grad_middle.astype(jnp.bfloat16)
    grad_branch_ref[...] = grad_branch
    grad_scaled = mult(grad_branch, merge_ref[...], RIGHT)
    head_sum_ref[...] += row_sum(grad_scaled * mixed_ref[...])
    grad_mixed = (grad_scaled * head_gain_ref[...]).astype(jnp.bfloat16)
    for pair in range(width // LANES):
        at = pair * LANES
        spans = [slice(k * width + at, k * width + at + LANES) for k in range(3)]
        queries, keys, values = (heads_ref[:, span] for span in spans)
        grads = grad_mixed[:, at : at + LANES]
        halves = []
        for side in range(2):
            head = 2 * pair + side
            probs = probs_ref[0, head]
            grad_values = mult(probs.astype(jnp.bfloat16), grads, LEFT)
            grad_probs = mult(half_of(grads, side), values, RIGHT)
            weighted = jnp.sum(probs * grad_probs, axis=-1, keepdims=True)
            grad_scores = (probs * (grad_probs - weighted)).astype(jnp.bfloat16)
            total_ref[head] += grad_scores.astype(jnp.float32)
            grad_queries = mult(grad_scores, keys) * SCALE
            grad_keys = mult(grad_scores, queries, LEFT) * SCALE
            halves.append((grad_queries, grad_keys, grad_values))
        for span, left, right in zip(spans, *halves):
            low = join(left, right).astype(jnp.bfloat16)
            grad_heads_ref[:, span] = low
            heads_sum_ref[:, span] += row_sum(low.astype(jnp.float32))
    grad_first_ref[...] = mult(grad_heads_ref[...], heads_weight_ref[...], RIGHT)

    @pl.when(item == pl.num_programs(0) - 1)
    def _():
        blank = jnp.zeros((length, length), jnp.float32)
        for head in range(total_ref.shape[0]):
            wide = jnp.concatenate([blank, total_ref[head]], axis=1)
            slots = length - 1 - lax.broadcasted_iota(jnp.int32, (length, length), 0)
            swap = jnp.where(lax.broadcasted_iota(jnp.int32, (length, length), 1) == slots, 1.0, 0.0)
            turned = lax.dot_general(
                swap,
                wide,
                (FULL, ((), ())),
                precision=lax.Precision.HIGHEST,
                preferred_element_type=jnp.float32,
            )
            turned = pltpu.roll(turned, length, 1, stride=1, stride_axis=0)
            table_ref[head : head + 1, :] = row_sum(turned)


def attend_back(
    items,
    middle,
    own,
    other,
    grad_reduced,
    gain,
    merge,
    mixed,
    head_gain,
    probs,
    heads_low,
    heads_weight,
):
    rows, model = middle.shape
    length = rows // items
    width = merge.shape[0]
    heads = probs.shape[1]
    out = lambda columns, kind: jax.ShapeDtypeStruct((rows, columns), kind)
    model_rows = rows_of((length, model))
    sums = lambda columns: jax.ShapeDtypeStruct((1, columns), jnp.float32)
    return pl.pallas_call(
        attend_back_kernel,
        grid_spec=pltpu.PrefetchScalarGridSpec(
            num_scalar_prefetch=0,
            grid=(items,),
            in_specs=[
                model_rows,
                model_rows,
                model_rows,
                model_rows,
                whole((1, model)),
                whole(merge.shape),
                rows_of((length, width)),
                whole(head_gain.shape),
                pl.BlockSpec((1, heads, length, length), lambda item, *_: (item, 0, 0, 0)),
                rows_of((length, 3 * width)),
                whole(heads_weight.shape),
            ],
            out_specs=[
                model_rows,
                model_rows,
                rows_of((length, 3 * width)),
                model_rows,
                whole((1, model)),
                whole((1, model)),
                whole((1, model)),
                whole((1, width)),
                whole((1, 3 * width)),
                whole((heads, 2 * length)),
            ],
            scratch_shapes=[pltpu.VMEM((heads, length, length), jnp.float32)],
        ),
        out_shape=[
            out(model, jnp.float32),
            out(model, jnp.bfloat16),
            out(3 * width, jnp.bfloat16),
            out(model, jnp.float32),
            sums(model),
            sums(model),
            sums(model),
            sums(width),
            sums(3 * width),
            jax.ShapeDtypeStruct((heads, 2 * length), jnp.float32),
        ],
        name="attend_back",
    )(
        middle,
        own,
        other,
        grad_reduced,
        gain,
        merge,
        mixed,
        head_gain,
        probs,
        heads_low,
        heads_weight,
    )


def stem_back_kernel(
    patches_ref,
    hidden_ref,
    own_ref,
    other_ref,
    grad_middle_ref,
    gain_ref,
    image_ref,
    features_ref,
    mean_ref,
    inverse_ref,
    input_grad_ref,
    grad_embedded_ref,
    grad_stem_ref,
    gain_sum_ref,
    shift_sum_ref,
    stem_gain_ref,
    stem_shift_ref,
):
    item = pl.program_id(0)
    length = hidden_ref.shape[0]
    start_sums(gain_sum_ref, shift_sum_ref, stem_gain_ref, stem_shift_ref)
    normal, inverse = normed(hidden_ref[...])
    grad_first = own_ref[...] + other_ref[...]
    gain_sum_ref[...] += row_sum(grad_first * normal)
    shift_sum_ref[...] += row_sum(grad_first)
    input_grad = grad_middle_ref[...] + norm_back(normal, inverse, grad_first, gain_ref[...])
    input_grad_ref[...] = input_grad
    mask = before(length, patches_ref[item])
    grad_embedded = (input_grad * mask).astype(jnp.bfloat16)
    grad_embedded_ref[...] = grad_embedded
    grad_stem = mult(grad_embedded, image_ref[...], RIGHT)
    grad_stem_ref[...] = grad_stem
    stem_hat = (features_ref[...].astype(jnp.float32) - mean_ref[...]) * inverse_ref[...]
    stem_shift_ref[...] += row_sum(grad_stem)
    stem_gain_ref[...] += row_sum(grad_stem * stem_hat)


def stem_back(
    patches, hidden, own, other, grad_middle, gain, image, features, mean, inverse
):
    items = patches.shape[0]
    rows, model = hidden.shape
    length = rows // items
    channels = features.shape[1]
    out = lambda columns, kind: jax.ShapeDtypeStruct((rows, columns), kind)
    model_rows = rows_of((length, model))
    channel_rows = rows_of((length, channels))
    sums = lambda columns: jax.ShapeDtypeStruct((1, columns), jnp.float32)
    return pl.pallas_call(
        stem_back_kernel,
        grid_spec=pltpu.PrefetchScalarGridSpec(
            num_scalar_prefetch=1,
            grid=(items,),
            in_specs=[
                model_rows,
                model_rows,
                model_rows,
                model_rows,
                whole((1, model)),
                whole(image.shape),
                channel_rows,
                whole((1, channels)),
                whole((1, channels)),
            ],
            out_specs=[
                model_rows,
                model_rows,
                channel_rows,
                whole((1, model)),
                whole((1, model)),
                whole((1, channels)),
                whole((1, channels)),
            ],
        ),
        out_shape=[
            out(model, jnp.float32),
            out(model, jnp.bfloat16),
            out(channels, jnp.float32),
            sums(model),
            sums(model),
            sums(channels),
            sums(channels),
        ],
        name="stem_back",
    )(patches, hidden, own, other, grad_middle, gain, image, features, mean, inverse)


def swap_core(values):
    count = lax.axis_size("tensor")
    return lax.ppermute(values, "tensor", [(core, core ^ 1) for core in range(count)])


def exchange(values, bit):
    count = lax.axis_size("dp")
    return lax.ppermute(values, "dp", [(rank, rank ^ (1 << bit)) for rank in range(count)])


def sum_by_doubling(values):
    for bit in range(lax.axis_size("dp").bit_length() - 1):
        values = values + exchange(values, bit)
    return values


def sum_by_halving(values, order):
    rank = lax.axis_index("dp")
    for bit in order:
        half = values.shape[0] // 2
        side = (rank >> bit) & 1
        sent = lax.dynamic_slice_in_dim(values, (1 - side) * half, half, 0)
        kept = lax.dynamic_slice_in_dim(values, side * half, half, 0)
        values = kept + exchange(sent, bit)
    for bit in reversed(order):
        side = (rank >> bit) & 1
        other = exchange(values, bit)
        values = jnp.where(
            side == 1, jnp.concatenate([other, values]), jnp.concatenate([values, other])
        )
    return values


def orders():
    bits = tuple(range(lax.axis_size("dp").bit_length() - 1))
    return bits, (bits[1], bits[0]) + bits[2:]


def pack(arrays):
    flat = jnp.concatenate([entry.reshape(-1) for entry in arrays])
    short = -flat.shape[0] % 1024
    return jnp.pad(flat, (0, short)).reshape(-1, 128)


def unpack(packed, arrays):
    flat, at, parts = packed.reshape(-1), 0, []
    for entry in arrays:
        parts.append(flat[at : at + entry.size].reshape(entry.shape))
        at += entry.size
    return parts


def local(
    layer_input,
    patch_features,
    bucket_ids,
    text_lengths,
    upstream,
    query_weight,
    key_weight,
    value_weight,
    merge_weight,
    query_bias,
    value_bias,
    merge_bias,
    head_gain,
    distance_table,
    first_gain,
    first_shift,
    second_gain,
    second_shift,
    expand_weight,
    expand_bias,
    reduce_weight,
    reduce_bias,
    image_weight,
    stem_gain,
    stem_shift,
):
    items = bucket_ids.shape[0]
    rows = layer_input.shape[0]
    length = rows // items
    heads = head_gain.shape[0]
    width = query_weight.shape[1]
    row = lambda vector: vector.reshape(1, -1)
    patches = PATCH_SMALL + (PATCH_LARGE - PATCH_SMALL) * bucket_ids
    valid = patches + text_lengths
    slots = jnp.arange(length, dtype=jnp.int32)
    patch_mask = (slots[None, :] < patches[:, None]).astype(jnp.float32).reshape(rows)
    features = patch_features.astype(jnp.float32)
    masked = features * patch_mask[:, None]
    feature_sum, square_sum, count = sum_by_doubling(
        jnp.stack(
            [
                jnp.sum(masked, axis=0),
                jnp.sum(masked * features, axis=0),
                jnp.full((features.shape[1],), jnp.sum(patch_mask)),
            ]
        )
    )
    bias = distance_bias(distance_table, length)
    heads_weight = jnp.concatenate([query_weight, key_weight, value_weight], axis=1)
    heads_bias = row(jnp.concatenate([query_bias, jnp.zeros_like(query_bias), value_bias]))
    head_gains = row(jnp.repeat(head_gain, HEAD_DIM))
    stem_mean = feature_sum / count
    stem_inverse = lax.rsqrt(square_sum / count - stem_mean * stem_mean + EPSILON)
    stem_hat = (features - stem_mean) * stem_inverse
    stem_low = (stem_hat * stem_gain + stem_shift).astype(jnp.bfloat16)
    embedded = mult(stem_low, image_weight)
    hidden, first_low, heads_low, probs, mixed, scaled_low, branch = attend(
        patches,
        valid,
        layer_input,
        embedded,
        swap_core(embedded),
        row(first_gain),
        row(first_shift),
        heads_weight,
        heads_bias,
        bias,
        head_gains,
        merge_weight,
    )
    (
        middle,
        second_low,
        active_low,
        grad_expanded_low,
        reduced,
        grad_second,
        grad_reduced_low,
        grad_expand_bias,
        grad_reduce_bias,
    ) = feed(
        valid,
        hidden,
        branch,
        swap_core(branch),
        row(merge_bias),
        row(second_gain),
        row(second_shift),
        expand_weight,
        row(expand_bias),
        reduce_weight,
        upstream,
    )
    grad_reduce_weight = mult(active_low, grad_reduced_low, LEFT)
    grad_expand_weight = mult(second_low, grad_expanded_low, LEFT)
    block_output = (middle + (reduced + swap_core(reduced)) + reduce_bias).astype(jnp.bfloat16)
    (
        grad_middle,
        grad_branch_low,
        grad_heads_low,
        grad_first,
        grad_second_gain,
        grad_second_shift,
        grad_merge_bias,
        head_sums,
        heads_sums,
        grad_table,
    ) = attend_back(
        items,
        middle,
        grad_second,
        swap_core(grad_second),
        grad_reduced_low,
        row(second_gain),
        merge_weight,
        mixed,
        head_gains,
        probs,
        heads_low,
        heads_weight,
    )
    grad_merge_weight = mult(scaled_low, grad_branch_low, LEFT)
    grad_heads_weight = mult(first_low, grad_heads_low, LEFT)
    (
        input_grad,
        grad_embedded_low,
        grad_stem,
        grad_first_gain,
        grad_first_shift,
        gain_local,
        shift_local,
    ) = stem_back(
        patches,
        hidden,
        grad_first,
        swap_core(grad_first),
        grad_middle,
        row(first_gain),
        image_weight,
        patch_features,
        row(stem_mean),
        row(stem_inverse),
    )
    grad_image_weight = mult(stem_low, grad_embedded_low, LEFT)
    first_order, second_order = orders()
    grad_reduce_weight = sum_by_halving(grad_reduce_weight, first_order)
    grad_expand_weight = sum_by_halving(grad_expand_weight, second_order)
    merge_rows = grad_merge_weight.shape[0]
    row_weights = sum_by_halving(
        jnp.concatenate([grad_merge_weight, grad_image_weight]), second_order
    )
    grad_merge_weight, grad_image_weight = row_weights[:merge_rows], row_weights[merge_rows:]
    grad_heads_weight = sum_by_halving(grad_heads_weight, first_order)
    small = (
        heads_sums,
        grad_merge_bias,
        jnp.sum(head_sums.reshape(heads, HEAD_DIM), axis=1),
        grad_table[:, : distance_table.shape[1]],
        grad_first_gain,
        grad_first_shift,
        grad_second_gain,
        grad_second_shift,
        grad_expand_bias,
        grad_reduce_bias,
        gain_local,
        shift_local,
    )
    (
        heads_sums,
        grad_merge_bias,
        grad_head_gain,
        grad_distance_table,
        grad_first_gain,
        grad_first_shift,
        grad_second_gain,
        grad_second_shift,
        grad_expand_bias,
        grad_reduce_bias,
        grad_stem_gain,
        grad_stem_shift,
    ) = unpack(sum_by_doubling(pack(small)), small)
    patch_grad = (
        patch_mask[:, None]
        * stem_inverse
        * stem_gain
        * (grad_stem - grad_stem_shift / count - stem_hat * grad_stem_gain / count)
    )
    return (
        block_output,
        input_grad,
        patch_grad,
        grad_heads_weight[:, :width],
        grad_heads_weight[:, width : 2 * width],
        grad_heads_weight[:, 2 * width :],
        grad_merge_weight,
        heads_sums[0, :width],
        heads_sums[0, 2 * width :],
        grad_merge_bias[0],
        grad_head_gain,
        grad_distance_table,
        grad_first_gain[0],
        grad_first_shift[0],
        grad_second_gain[0],
        grad_second_shift[0],
        grad_expand_weight,
        grad_expand_bias[0],
        grad_reduce_weight,
        grad_reduce_bias[0],
        grad_image_weight,
        grad_stem_gain[0],
        grad_stem_shift[0],
    )


def solution(mesh):
    in_specs = (
        P("dp", None),
        P("dp", "tensor"),
        P("dp"),
        P("dp"),
        P("dp", None),
        P(None, "tensor"),
        P(None, "tensor"),
        P(None, "tensor"),
        P("tensor", None),
        P("tensor"),
        P("tensor"),
        P(),
        P("tensor"),
        P("tensor", None),
        P(),
        P(),
        P(),
        P(),
        P(None, "tensor"),
        P("tensor"),
        P("tensor", None),
        P(),
        P("tensor", None),
        P("tensor"),
        P("tensor"),
    )
    out_specs = (
        P("dp", None),
        P("dp", None),
        P("dp", "tensor"),
        P(None, "tensor"),
        P(None, "tensor"),
        P(None, "tensor"),
        P("tensor", None),
        P("tensor"),
        P("tensor"),
        P(),
        P("tensor"),
        P("tensor", None),
        P(),
        P(),
        P(),
        P(),
        P(None, "tensor"),
        P("tensor"),
        P("tensor", None),
        P(),
        P("tensor", None),
        P("tensor"),
        P("tensor"),
    )
    return jax.shard_map(local, mesh=mesh, in_specs=in_specs, out_specs=out_specs, check_vma=False)
```

time: 611 us -> 516 us (0.84)
  Pallas kernels: 0 us -> 74.5 us
  matrix products: 92.7 us -> 22.3 us
  local copies, waits for them, and re-layouts: 93.8 us -> 36.8 us
  waiting for transfers between devices: 281 us -> 258 us
  between operations: 15.4 us -> 1.87 us
  other arithmetic: 73.3 us -> 62.3 us
    pallas_call x0 -> x5, Pallas kernels: none -> 74.5 us  [the longest x1 23.5 us: attend_back(): pl.pallas_call(attend_back_kernel, grid_spec=pltpu.PrefetchScalarGridSpec...]
    dot_general x25 -> x6, matrix products: 92.7 us -> 22.3 us  [mult(): lax.dot_general(left, right, (dims, ((), ())), preferred_element_type=jnp...]
    psum x1 -> x0, waiting for transfers between devices: 67.6 us -> none  [local(): grad_reduce_weight = lax.psum(grad_reduce_weight, 'dp')]
    ppermute x37 -> x45, waiting for transfers between devices: 214 us -> 258 us  [the longest x40 255 us: exchange(): lax.ppermute(values, 'dp', [(rank, rank ^ 1 << bit) for rank in range(cou...]
    reduce_sum x13 -> x1, other arithmetic: 31 us -> 0.63 us  [local(): jnp.sum(head_sums.reshape(heads, HEAD_DIM), axis=1)]
    unnamed x164 -> x109, local copies, waits for them, and re-layouts: 31.3 us -> 11.5 us
    reshape x6 -> x8, local copies, waits for them, and re-layouts: 23.1 us -> 4.18 us  [the longest x7 4.1 us: local(): row = lambda vector: vector.reshape(1, -1)]
    convert_element_type x7 -> x0, local copies, waits for them, and re-layouts: 9.41 us -> none  [the longest x1 2.3 us: local(): query_low = (jnp.dot(first_low, query_weight, preferred_element_type=jnp....]
  transfers between devices with their start and end apart: 38 -> 45, of which waited for: 21 -> 25; matrix products, arithmetic and copies ran while one was open for 27% -> 18% of each run, Pallas kernels for 0% -> 7%
where the time goes in v2:
time: 516 us; the launch traced here: 508 us
  waiting for transfers between devices  258 us (50%)
  Pallas kernels  74.5 us (14%)
  other arithmetic  62.3 us (12%)
  starting transfers between devices  52.1 us (10%)
  local copies, waits for them, and re-layouts  36.8 us (7%)
  matrix products  22.3 us (4%)
    ppermute x40, waiting for transfers between devices, exchange(): lax.ppermute(values, 'dp', [(rank, rank ^ 1 << bit) for rank in range(cou...  255 us
    ppermute x40, starting transfers between devices, exchange(): lax.ppermute(values, 'dp', [(rank, rank ^ 1 << bit) for rank in range(cou...  51.3 us
    select_n x16, other arithmetic, sum_by_halving(): jnp.where(side == 1, jnp.concatenate([other, values]), jnp.concatenate([v...  26 us
    pallas_call x1, Pallas kernels, attend_back(): pl.pallas_call(attend_back_kernel, grid_spec=pltpu.PrefetchScalarGridSpec...  23.5 us
    pallas_call x1, Pallas kernels, feed(): pl.pallas_call(feed_kernel, grid_spec=pltpu.PrefetchScalarGridSpec(num_sc...  22.9 us
    dot_general x6, matrix products, mult(): lax.dot_general(left, right, (dims, ((), ())), preferred_element_type=jnp...  22.3 us
    pallas_call x1, Pallas kernels, attend(): pl.pallas_call(attend_kernel, grid_spec=pltpu.PrefetchScalarGridSpec(num_...  14.9 us
    add x16, other arithmetic, sum_by_halving(): values = kept + exchange(sent, bit)  14.3 us
  transfers between devices with their start and end apart: 45, of which 25 were waited for; matrix products, arithmetic and copies ran while one was open for 18% of the time, Pallas kernels for 7%

profile of v2, /device:TPU:0, one launch (start us, length us, event | category | flops | bytes accessed | tf_op | source)
XLA Modules:
  0.0 508.3 jit_solution(2093340346358116586)
XLA Ops:
  2.6 1.7 fusion
  5.0 3.0 collective-permute-start
  8.0 1.6 collective-permute-done
  9.7 2.1 collective-permute-start.1
  11.8 1.6 collective-permute-done.1
  13.5 2.1 collective-permute-start.2
  15.6 1.6 collective-permute-done.2
  17.2 3.0 collective-permute-start.3
  20.2 1.6 collective-permute-done.3
  22.5 4.3 fusion.15.own_ref
  29.4 2.3 distance_bias.1.bias_ref
  33.9 14.9 %attend.1 = (f32[1024,768]{1,0:T(8,128)}, bf16[1024,768]{1,0:T(8,128)(2,1)}, bf16[1024,1152]{1,0:T(8,128)(2,1)}, f32[4,6,256,256]{3,2,1,0:T(8,128)}, f32[1024,38...) custom-call(s32[4]{0:T(128)} %copy-done.35, s32[4]{0:T(128)} %get-tuple-element.110.valid_ref, ...), custom_call_target="tpu_custom_call" | custom-call | tf_op jit(solution)/shard_map/attend/pallas_call | solution.py:167
  51.8 3.1 collective-permute-done.5.other_ref
  54.9 1.7 copy-done.15
  56.6 22.9 %feed.1 = (f32[1024,768]{1,0:T(8,128)}, bf16[1024,768]{1,0:T(8,128)(2,1)}, bf16[1024,1536]{1,0:T(8,128)(2,1)}, bf16[1024,1536]{1,0:T(8,128)(2,1)}, f32[1024,768]...) custom-call(s32[4]{0:T(128)} %get-tuple-element.110.valid_ref, ...), custom_call_target="tpu_custom_call" | custom-call | tf_op jit(solution)/shard_map/feed/pallas_call | solution.py:323
  79.4 5.0 fusion.24
  84.5 1.6 constant_dynamic-slice_fusion.7
  86.1 1.8 copy-done
  87.9 1.9 collective-permute-start.29
  89.9 5.1 %fusion.25 = f32[1536,768]{1,0:T(8,128)S(1)} fusion(bf16[1024,1536]{1,0:T(8,128)(2,1)} %get-tuple-element.88, bf16[1024,768]{1,0:T(8,128)(2,1)} %get-tuple-element.61.grad_reduced_ref), kind=kOutput, calls=%fused_computation.104 | convolution fusion | flops 2415919104 | bytes 9437184 | tf_op jit(solution)/shard_map/dot_general | solution.py:23
  95.0 1.7 constant_dynamic-slice_fusion.3
  99.4 42.5 %collective-permute-done.29 = f32[384,1536]{1,0:T(8,128)} collective-permute-done((f32[384,1536]{1,0:T(8,128)}, f32[384,1536]{1,0:T(8,128)}, u32[]{:S(2)}, u32[]{:S(2)}) %collective-permute-start.29) | collective-permute-done | bytes 2359328 | tf_op jit(solution)/shard_map/ppermute | solution.py:638
  141.9 2.8 dynamic-slice_add_fusion.1
  147.3 1.7 collective-permute-start.30
  150.2 2.1 collective-permute-done.37
  152.3 2.7 dynamic-slice_add_fusion
  158.5 23.5 %attend_back.1 = (f32[1024,768]{1,0:T(8,128)}, bf16[1024,768]{1,0:T(8,128)(2,1)}, bf16[1024,1152]{1,0:T(8,128)(2,1)}, f32[1024,768]{1,0:T(8,128)}, f32[1,768]{1,...) custom-call(f32[1024,768]{1,0:T(8,128)} %get-tuple-element.58.middle, ...), custom_call_target="tpu_custom_call" | custom-call | tf_op jit(solution)/shard_map/attend_back/pallas_call | solution.py:483
  182.2 4.5 fusion.22
  188.3 1.6 collective-permute-start.31
  196.5 8.0 %collective-permute-done.31 = f32[96,1536]{1,0:T(8,128)S(1)} collective-permute-done((f32[96,1536]{1,0:T(8,128)S(1)}, f32[96,1536]{1,0:T(8,128)S(1)}, u32[]{:S(2)}, u32[]{:S(2)}) %collective-permute-start.31) | collective-permute-done | bytes 589856 | tf_op jit(solution)/shard_map/ppermute | solution.py:638
  206.1 2.5 collective-permute-start.32
  208.7 4.9 add_convert_fusion
  220.3 1.8 collective-permute-done.32
  223.2 3.4 collective-permute-start.33
  228.1 19.1 %collective-permute-done.33 = f32[48,1536]{1,0:T(8,128)S(1)} collective-permute-done((f32[48,1536]{1,0:T(8,128)S(1)}, f32[48,1536]{1,0:T(8,128)S(1)}, u32[]{:S(2)}, u32[]{:S(2)}) %collective-permute-start.33) | collective-permute-done | bytes 294944 | tf_op jit(solution)/shard_map/ppermute | solution.py:638
  247.3 1.7 dynamic-slice_add_fusion.2
  250.1 2.4 collective-permute-done.40
  254.1 13.8 %collective-permute-done.41 = f32[96,768]{1,0:T(8,128)S(1)} collective-permute-done((f32[96,768]{1,0:T(8,128)S(1)}, f32[96,768]{1,0:T(8,128)S(1)}, u32[]{:S(2)}, u32[]{:S(2)}) %collective-permute-start.41) | collective-permute-done | bytes 294944 | tf_op jit(solution)/shard_map/ppermute | solution.py:638
  269.1 2.4 collective-permute-done.34
  271.6 1.6 collective-permute-start.35
  274.4 10.8 %stem_back.1 = (f32[1024,768]{1,0:T(8,128)}, bf16[1024,768]{1,0:T(8,128)(2,1)}, f32[1024,512]{1,0:T(8,128)}, f32[1,768]{1,0:T(1,128)}, f32[1,768]{1,0:T(1,128)}, /*index=5*/f32[1,512]{1,0:T(1,128)}, f32[1,512]{1,0:T(1,128)}) custom-call(s32[4]{0:T(128)} %copy-done.35, f32[1024,768]{1,0:T(8,128)} %get-tuple-element.56.hidden_ref, ...), custom_call_target="tpu_custom_call" | custom-call | tf_op jit(solution)/shard_map/stem_back/pallas_call | solution.py:592
  288.1 2.5 fusion.13
  294.7 5.8 %collective-permute-done.9 = f32[96,128]{1,0:T(8,128)S(1)} collective-permute-done((f32[96,128]{1,0:T(8,128)S(1)}, f32[96,128]{1,0:T(8,128)S(1)}, u32[]{:S(2)}, u32[]{:S(2)}) %collective-permute-start.9) | collective-permute-done | bytes 49184 | tf_op jit(solution)/shard_map/ppermute | solution.py:638
  302.2 21.5 %collective-permute-done.10 = f32[96,128]{1,0:T(8,128)S(1)} collective-permute-done((f32[96,128]{1,0:T(8,128)S(1)}, f32[96,128]{1,0:T(8,128)S(1)}, u32[]{:S(2)}, u32[]{:S(2)}) %collective-permute-start.10) | collective-permute-done | bytes 49184 | tf_op jit(solution)/shard_map/ppermute | solution.py:638
  323.7 1.7 collective-permute-start.11
  325.4 1.9 maximum_select_fusion.9
  328.4 2.4 collective-permute-start.12
  333.6 1.9 maximum_select_fusion.4
  336.6 19.6 %collective-permute-done.43 = f32[384,768]{1,0:T(8,128)S(1)} collective-permute-done((f32[384,768]{1,0:T(8,128)S(1)}, f32[384,768]{1,0:T(8,128)S(1)}, u32[]{:S(2)}, u32[]{:S(2)}) %collective-permute-start.43) | collective-permute-done | bytes 1179680 | tf_op jit(solution)/shard_map/ppermute | solution.py:638
  356.2 1.7 maximum_select_fusion.5
  360.7 1.7 collective-permute-start.23
  362.4 7.3 %collective-permute-done.18 = f32[96,1152]{1,0:T(8,128)S(1)} collective-permute-done((f32[96,1152]{1,0:T(8,128)S(1)}, f32[96,1152]{1,0:T(8,128)S(1)}, u32[]{:S(2)}, u32[]{:S(2)}) %collective-permute-start.18) | collective-permute-done | bytes 442400 | tf_op jit(solution)/shard_map/ppermute | solution.py:638
  370.8 4.4 collective-permute-done.23
  375.3 2.0 collective-permute-start.24
  377.9 6.5 %collective-permute-done.24 = f32[56,768]{1,0:T(8,128)S(1)} collective-permute-done((f32[56,768]{1,0:T(8,128)S(1)}, f32[56,768]{1,0:T(8,128)S(1)}, u32[]{:S(2)}, u32[]{:S(2)}) %collective-permute-start.24) | collective-permute-done | bytes 172064 | tf_op jit(solution)/shard_map/ppermute | solution.py:638
  385.1 7.0 %collective-permute-done.25 = f32[56,768]{1,0:T(8,128)S(1)} collective-permute-done((f32[56,768]{1,0:T(8,128)S(1)}, f32[56,768]{1,0:T(8,128)S(1)}, u32[]{:S(2)}, u32[]{:S(2)}) %collective-permute-start.25) | collective-permute-done | bytes 172064 | tf_op jit(solution)/shard_map/ppermute | solution.py:638
  392.8 29.9 %collective-permute-done.19 = f32[192,1152]{1,0:T(8,128)S(1)} collective-permute-done((f32[192,1152]{1,0:T(8,128)S(1)}, f32[192,1152]{1,0:T(8,128)S(1)}, u32[]{:S(2)}, u32[]{:S(2)}) %collective-permute-start.19) | collective-permute-done | bytes 884768 | tf_op jit(solution)/shard_map/ppermute | solution.py:638
  430.3 3.6 fusion.9
  433.9 42.9 %collective-permute-done.27 = f32[224,768]{1,0:T(8,128)S(1)} collective-permute-done((f32[224,768]{1,0:T(8,128)S(1)}, f32[224,768]{1,0:T(8,128)S(1)}, u32[]{:S(2)}, u32[]{:S(2)}) %collective-permute-start.27) | collective-permute-done | bytes 688160 | tf_op jit(solution)/shard_map/ppermute | solution.py:638
  477.9 5.3 %maximum_select_fusion = f32[768,1536]{1,0:T(8,128)} fusion(f32[384,1536]{1,0:T(8,128)S(1)} %maximum_select_fusion.4, f32[384,1536]{1,0:T(8,128)} %collective-permute-done.36, pred[]{:T(512)S(6)} %eq.9), kind=kLoop, calls=%fused_computation | loop fusion | flops 3538944 | bytes 9437185 | tf_op jit(solution)/shard_map/jit(_where)/select_n | solution.py:658
  483.2 6.6 %maximum_select_fusion.1 = f32[1536,768]{1,0:T(8,128)} fusion(f32[768,768]{1,0:T(8,128)} %maximum_select_fusion.5, f32[768,768]{1,0:T(8,128)} %collective-permute-done.44, pred[]{:T(512)S(6)} %eq.8), kind=kLoop, calls=%fused_computation.1 | loop fusion | flops 3538944 | bytes 9437185 | tf_op jit(solution)/shard_map/jit(_where)/select_n | solution.py:658
  489.8 3.7 maximum_select_fusion.2
  493.5 1.9 fusion.21
  495.3 9.9 %collective-permute-done.28 = f32[448,768]{1,0:T(8,128)S(1)} collective-permute-done((f32[448,768]{1,0:T(8,128)S(1)}, f32[448,768]{1,0:T(8,128)S(1)}, u32[]{:S(2)}, u32[]{:S(2)}) %collective-permute-start.28) | collective-permute-done | bytes 1376288 | tf_op jit(solution)/shard_map/ppermute | solution.py:638
  (249 shorter events, 76.1 us)
Async XLA Ops:
  1.8 25.0 %copy-start.35 = (s32[4]{0:T(128)}, s32[4]{0:T(128)S(1)}, u32[]{:S(2)}) copy-start(s32[4]{0:T(128)S(1)} %get-tuple-element.109.patches_ref) | copy-start | bytes 52
  5.0 4.6 collective-permute-start
  9.7 3.7 collective-permute-start.1
  13.5 3.7 collective-permute-start.2
  17.2 4.7 collective-permute-start.3
  26.9 6.1 %collective-permute-start.4 = (f32[1024,768]{1,0:T(8,128)}, f32[1024,768]{1,0:T(8,128)}, u32[]{:S(2)}, u32[]{:S(2)}) collective-permute-start(f32[1024,768]{1,0:T(8,128)} %fusion.15.own_ref), channel_id=1, source_target_pairs={{0,1},{1,0},{2,3},{3,2},{4,5},{5,4},{6,7},{7,6},{8,9},{9,8},{10,11... | collective-permute-start | bytes 9437192 | tf_op jit(solution)/shard_map/ppermute | solution.py:633
  33.9 15.5 %copy-start.42 = (f32[768]{0:T(1024)S(1)}, f32[768]{0:T(1024)}, u32[]{:S(2)}) copy-start(f32[768]{0:T(1024)} %param.36) | copy-start | bytes 9220
  33.9 16.1 %copy-start.43 = (f32[768]{0:T(1024)S(1)}, f32[768]{0:T(1024)}, u32[]{:S(2)}) copy-start(f32[768]{0:T(1024)} %param.41) | copy-start | bytes 9220
  33.9 16.7 %copy-start.44 = (f32[768]{0:T(1024)S(1)}, f32[768]{0:T(1024)}, u32[]{:S(2)}) copy-start(f32[768]{0:T(1024)} %param.42) | copy-start | bytes 9220
  33.9 17.2 %copy-start.36 = (f32[1536]{0:T(1024)S(1)}, f32[1536]{0:T(1024)}, u32[]{:S(2)}) copy-start(f32[1536]{0:T(1024)} %param.44) | copy-start | bytes 18436
  48.9 6.0 %collective-permute-start.5 = (f32[1024,768]{1,0:T(8,128)}, f32[1024,768]{1,0:T(8,128)S(1)}, u32[]{:S(2)}, u32[]{:S(2)}) collective-permute-start(f32[1024,768]{1,0:T(8,128)} %get-tuple-element.57.own_ref), channel_id=1, source_target_pairs={{0,1},{1,0},{2,3},{3,2},{4,5},{5,4},{6,7},{7,6},{8,9},{9,8},{10,11... | collective-permute-start | bytes 9437192 | tf_op jit(solution)/shard_map/ppermute | solution.py:633
  87.9 54.0 %collective-permute-start.29 = (f32[384,1536]{1,0:T(8,128)}, f32[384,1536]{1,0:T(8,128)}, u32[]{:S(2)}, u32[]{:S(2)}) collective-permute-start(f32[384,1536]{1,0:T(8,128)} %constant_dynamic-slice_fusion.7), channel_id=1, source_target_pairs={{0,4},{2,6},{4,0},{6,2},{8,12},{10,14},{12,8},{14,10},{16,20},{18,... | collective-permute-start | bytes 7077896 | tf_op jit(solution)/shard_map/ppermute | solution.py:638
  89.8 68.7 %collective-permute-start.7 = (f32[1024,768]{1,0:T(8,128)S(1)}, f32[1024,768]{1,0:T(8,128)}, u32[]{:S(2)}, u32[]{:S(2)}) collective-permute-start(f32[1024,768]{1,0:T(8,128)S(1)} %copy-done.14), channel_id=1, source_target_pairs={{0,1},{1,0},{2,3},{3,2},{4,5},{5,4},{6,7},{7,6},{8,9},{9,8},{10,11... | collective-permute-start | bytes 9437192 | tf_op jit(solution)/shard_map/ppermute | solution.py:633
  97.9 54.4 %collective-permute-start.37 = (f32[768,768]{1,0:T(8,128)}, f32[768,768]{1,0:T(8,128)}, u32[]{:S(2)}, u32[]{:S(2)}) collective-permute-start(f32[768,768]{1,0:T(8,128)} %constant_dynamic-slice_fusion.3), channel_id=1, source_target_pairs={{0,2},{2,0},{4,6},{6,4},{8,10},{10,8},{12,14},{14,12},{16,18},{18,... | collective-permute-start | bytes 7077896 | tf_op jit(solution)/shard_map/ppermute | solution.py:638
  147.3 39.4 %collective-permute-start.30 = (f32[192,1536]{1,0:T(8,128)}, f32[192,1536]{1,0:T(8,128)}, u32[]{:S(2)}, u32[]{:S(2)}) collective-permute-start(f32[192,1536]{1,0:T(8,128)} %constant_dynamic-slice_fusion.6), channel_id=1, source_target_pairs={{0,2},{2,0},{4,6},{6,4},{8,10},{10,8},{12,14},{14,12},{16,18},{18,... | collective-permute-start | bytes 3538952 | tf_op jit(solution)/shard_map/ppermute | solution.py:638
  149.0 59.7 %collective-permute-start.6 = (f32[1024,768]{1,0:T(8,128)}, f32[1024,768]{1,0:T(8,128)}, u32[]{:S(2)}, u32[]{:S(2)}) collective-permute-start(f32[1024,768]{1,0:T(8,128)} %get-tuple-element.59), channel_id=1, source_target_pairs={{0,1},{1,0},{2,3},{3,2},{4,5},{5,4},{6,7},{7,6},{8,9},{9,8},{10,11... | collective-permute-start | bytes 9437192 | tf_op jit(solution)/shard_map/ppermute | solution.py:633
  157.5 35.2 %collective-permute-start.38 = (f32[384,768]{1,0:T(8,128)}, f32[384,768]{1,0:T(8,128)}, u32[]{:S(2)}, u32[]{:S(2)}) collective-permute-start(f32[384,768]{1,0:T(8,128)} %constant_dynamic-slice_fusion.2), channel_id=1, source_target_pairs={{0,4},{2,6},{4,0},{6,2},{8,12},{10,14},{12,8},{14,10},{16,20},{18,... | collective-permute-start | bytes 3538952 | tf_op jit(solution)/shard_map/ppermute | solution.py:638
  182.1 92.1 %collective-permute-start.8 = (f32[1024,768]{1,0:T(8,128)}, f32[1024,768]{1,0:T(8,128)}, u32[]{:S(2)}, u32[]{:S(2)}) collective-permute-start(f32[1024,768]{1,0:T(8,128)} %get-tuple-element.65.own_ref), channel_id=1, source_target_pairs={{0,1},{1,0},{2,3},{3,2},{4,5},{5,4},{6,7},{7,6},{8,9},{9,8},{10,11... | collective-permute-start | bytes 9437192 | tf_op jit(solution)/shard_map/ppermute | solution.py:633
  188.3 16.3 %collective-permute-start.31 = (f32[96,1536]{1,0:T(8,128)S(1)}, f32[96,1536]{1,0:T(8,128)S(1)}, u32[]{:S(2)}, u32[]{:S(2)}) collective-permute-start(f32[96,1536]{1,0:T(8,128)S(1)} %constant_dynamic-slice_fusion.5), channel_id=1, source_target_pairs={{0,8},{2,10},{4,12},{6,14},{8,0},{10,2},{12,4},{14,6},{16,24},{18,... | collective-permute-start | bytes 1769480 | tf_op jit(solution)/shard_map/ppermute | solution.py:638
  191.2 56.1 %collective-permute-start.13 = (f32[384,1152]{1,0:T(8,128)}, f32[384,1152]{1,0:T(8,128)}, u32[]{:S(2)}, u32[]{:S(2)}) collective-permute-start(f32[384,1152]{1,0:T(8,128)} %constant_dynamic-slice_fusion.14), channel_id=1, source_target_pairs={{0,2},{2,0},{4,6},{6,4},{8,10},{10,8},{12,14},{14,12},{16,18},{18,... | collective-permute-start | bytes 5308424 | tf_op jit(solution)/shard_map/ppermute | solution.py:638
  195.1 13.6 %copy-start.1 = (f32[1024,768]{1,0:T(8,128)S(1)}, f32[1024,768]{1,0:T(8,128)}, u32[]{:S(2)}) copy-start(f32[1024,768]{1,0:T(8,128)} %get-tuple-element.58.middle_ref) | copy-start | bytes 9437188
  195.1 13.6 %copy-start.39 = (f32[768]{0:T(1024)S(1)}, f32[768]{0:T(1024)}, u32[]{:S(2)}) copy-start(f32[768]{0:T(1024)} %param.46) | copy-start | bytes 9220
  196.0 30.7 %collective-permute-start.39 = (f32[192,768]{1,0:T(8,128)}, f32[192,768]{1,0:T(8,128)}, u32[]{:S(2)}, u32[]{:S(2)}) collective-permute-start(f32[192,768]{1,0:T(8,128)} %constant_dynamic-slice_fusion.1), channel_id=1, source_target_pairs={{0,8},{2,10},{4,12},{6,14},{8,0},{10,2},{12,4},{14,6},{16,24},{18,... | collective-permute-start | bytes 1769480 | tf_op jit(solution)/shard_map/ppermute | solution.py:638
  206.1 16.0 %collective-permute-start.32 = (f32[48,1536]{1,0:T(8,128)}, f32[48,1536]{1,0:T(8,128)}, u32[]{:S(2)}, u32[]{:S(2)}) collective-permute-start(f32[48,1536]{1,0:T(8,128)} %constant_dynamic-slice_fusion.4), channel_id=1, source_target_pairs={{0,16},{2,18},{4,20},{6,22},{8,24},{10,26},{12,28},{14,30},{16,0},... | collective-permute-start | bytes 884744 | tf_op jit(solution)/shard_map/ppermute | solution.py:638
  223.2 23.9 %collective-permute-start.33 = (f32[48,1536]{1,0:T(8,128)S(1)}, f32[48,1536]{1,0:T(8,128)S(1)}, u32[]{:S(2)}, u32[]{:S(2)}) collective-permute-start(f32[48,1536]{1,0:T(8,128)S(1)} %dynamic-slice_add_fusion.12), channel_id=1, source_target_pairs={{0,16},{2,18},{4,20},{6,22},{8,24},{10,26},{12,28},{14,30},{16,0},... | collective-permute-start | bytes 884744 | tf_op jit(solution)/shard_map/ppermute | solution.py:638
  228.0 24.5 %collective-permute-start.40 = (f32[96,768]{1,0:T(8,128)S(1)}, f32[96,768]{1,0:T(8,128)S(1)}, u32[]{:S(2)}, u32[]{:S(2)}) collective-permute-start(f32[96,768]{1,0:T(8,128)S(1)} %constant_dynamic-slice_fusion), channel_id=1, source_target_pairs={{0,16},{2,18},{4,20},{6,22},{8,24},{10,26},{12,28},{14,30},{16,0},... | collective-permute-start | bytes 884744 | tf_op jit(solution)/shard_map/ppermute | solution.py:638
  247.2 24.3 %collective-permute-start.34 = (f32[96,1536]{1,0:T(8,128)S(1)}, f32[96,1536]{1,0:T(8,128)S(1)}, u32[]{:S(2)}, u32[]{:S(2)}) collective-permute-start(f32[96,1536]{1,0:T(8,128)S(1)} %maximum_select_fusion.12), channel_id=1, source_target_pairs={{0,8},{2,10},{4,12},{6,14},{8,0},{10,2},{12,4},{14,6},{16,24},{18,... | collective-permute-start | bytes 1769480 | tf_op jit(solution)/shard_map/ppermute | solution.py:638
  249.1 24.1 %collective-permute-start.14 = (f32[192,1152]{1,0:T(8,128)S(1)}, f32[192,1152]{1,0:T(8,128)S(1)}, u32[]{:S(2)}, u32[]{:S(2)}) collective-permute-start(f32[192,1152]{1,0:T(8,128)S(1)} %constant_dynamic-slice_fusion.13), channel_id=1, source_target_pairs={{0,4},{2,6},{4,0},{6,2},{8,12},{10,14},{12,8},{14,10},{16,20},{18,... | collective-permute-start | bytes 2654216 | tf_op jit(solution)/shard_map/ppermute | solution.py:638
  252.6 15.3 %collective-permute-start.41 = (f32[96,768]{1,0:T(8,128)S(1)}, f32[96,768]{1,0:T(8,128)S(1)}, u32[]{:S(2)}, u32[]{:S(2)}) collective-permute-start(f32[96,768]{1,0:T(8,128)S(1)} %dynamic-slice_add_fusion.11), channel_id=1, source_target_pairs={{0,16},{2,18},{4,20},{6,22},{8,24},{10,26},{12,28},{14,30},{16,0},... | collective-permute-start | bytes 884744 | tf_op jit(solution)/shard_map/ppermute | solution.py:638
  268.8 56.6 %collective-permute-start.42 = (f32[192,768]{1,0:T(8,128)}, f32[192,768]{1,0:T(8,128)}, u32[]{:S(2)}, u32[]{:S(2)}) collective-permute-start(f32[192,768]{1,0:T(8,128)} %maximum_select_fusion.13), channel_id=1, source_target_pairs={{0,8},{2,10},{4,12},{6,14},{8,0},{10,2},{12,4},{14,6},{16,24},{18,... | collective-permute-start | bytes 1769480 | tf_op jit(solution)/shard_map/ppermute | solution.py:638
  271.6 13.7 %copy-start.8 = (f32[192,1536]{1,0:T(8,128)}, f32[192,1536]{1,0:T(8,128)S(1)}, u32[]{:S(2)}) copy-start(f32[192,1536]{1,0:T(8,128)S(1)} %maximum_select_fusion.8) | copy-start | bytes 3538948
  271.6 62.0 %collective-permute-start.35 = (f32[192,1536]{1,0:T(8,128)S(1)}, f32[192,1536]{1,0:T(8,128)}, u32[]{:S(2)}, u32[]{:S(2)}) collective-permute-start(f32[192,1536]{1,0:T(8,128)S(1)} %maximum_select_fusion.8), channel_id=1, source_target_pairs={{0,2},{2,0},{4,6},{6,4},{8,10},{10,8},{12,14},{14,12},{16,18},{18,... | collective-permute-start | bytes 3538952 | tf_op jit(solution)/shard_map/ppermute | solution.py:638
  274.2 19.4 %collective-permute-start.15 = (f32[96,1152]{1,0:T(8,128)}, f32[96,1152]{1,0:T(8,128)}, u32[]{:S(2)}, u32[]{:S(2)}) collective-permute-start(f32[96,1152]{1,0:T(8,128)} %constant_dynamic-slice_fusion.12), channel_id=1, source_target_pairs={{0,8},{2,10},{4,12},{6,14},{8,0},{10,2},{12,4},{14,6},{16,24},{18,... | collective-permute-start | bytes 1327112 | tf_op jit(solution)/shard_map/ppermute | solution.py:638
  274.3 12.3 %copy-start.30 = (f32[768]{0:T(1024)S(1)}, f32[768]{0:T(1024)}, u32[]{:S(2)}) copy-start(f32[768]{0:T(1024)} %reduce.9) | copy-start | bytes 9220
  274.3 12.3 %copy-start.31 = (f32[768]{0:T(1024)S(1)}, f32[768]{0:T(1024)}, u32[]{:S(2)}) copy-start(f32[768]{0:T(1024)} %reduce.2) | copy-start | bytes 9220
  274.3 12.3 %copy-start.32 = (f32[768]{0:T(1024)S(1)}, f32[768]{0:T(1024)}, u32[]{:S(2)}) copy-start(f32[768]{0:T(1024)} %reduce.6) | copy-start | bytes 9220
  274.4 12.3 %copy-start.33 = (f32[768]{0:T(1024)S(1)}, f32[768]{0:T(1024)}, u32[]{:S(2)}) copy-start(f32[768]{0:T(1024)} %reduce.7) | copy-start | bytes 9220
  274.4 12.3 %copy-start.47 = (f32[6]{0:T(128)S(1)}, f32[6]{0:T(128)}, u32[]{:S(2)}) copy-start(f32[6]{0:T(128)} %reduce_sum.39) | copy-start | bytes 76
  274.4 13.7 %copy-start.7 = (bf16[1024,512]{1,0:T(8,128)(2,1)S(1)}, bf16[1024,512]{1,0:T(8,128)(2,1)}, u32[]{:S(2)}) copy-start(bf16[1024,512]{1,0:T(8,128)(2,1)} %features_ref.1) | copy-start | bytes 3145732
  274.4 13.7 %copy-start.26 = (f32[1,512]{1,0:T(1,128)S(1)}, f32[1,512]{1,0:T(1,128)}, u32[]{:S(2)}) copy-start(f32[1,512]{1,0:T(1,128)} %copy-done.25) | copy-start | bytes 6148
  274.4 13.7 %copy-start.28 = (f32[1,512]{1,0:T(1,128)S(1)}, f32[1,512]{1,0:T(1,128)}, u32[]{:S(2)}) copy-start(f32[1,512]{1,0:T(1,128)} %copy-done.27) | copy-start | bytes 6148
  274.4 13.7 %copy-start.46 = (f32[512]{0:T(512)S(1)}, f32[512]{0:T(512)}, u32[]{:S(2)}) copy-start(f32[512]{0:T(512)} %param.48) | copy-start | bytes 6148
  274.4 13.7 %copy-start.51 = (f32[512]{0:T(512)S(1)}, f32[512]{0:T(512)}, u32[]{:S(2)}) copy-start(f32[512]{0:T(512)} %param.49) | copy-start | bytes 6148
  287.5 13.0 %collective-permute-start.9 = (f32[96,128]{1,0:T(8,128)S(1)}, f32[96,128]{1,0:T(8,128)S(1)}, u32[]{:S(2)}, u32[]{:S(2)}) collective-permute-start(f32[96,128]{1,0:T(8,128)S(1)} %pad_bitcast_fusion), channel_id=1, source_target_pairs={{0,2},{2,0},{4,6},{6,4},{8,10},{10,8},{12,14},{14,12},{16,18},{18,... | collective-permute-start | bytes 147464 | tf_op jit(solution)/shard_map/ppermute | solution.py:638
  291.1 40.4 %collective-permute-start.21 = (f32[448,768]{1,0:T(8,128)S(1)}, f32[448,768]{1,0:T(8,128)S(1)}, u32[]{:S(2)}, u32[]{:S(2)}) collective-permute-start(f32[448,768]{1,0:T(8,128)S(1)} %fusion.10), channel_id=1, source_target_pairs={{0,4},{2,6},{4,0},{6,2},{8,12},{10,14},{12,8},{14,10},{16,20},{18,... | collective-permute-start | bytes 4128776 | tf_op jit(solution)/shard_map/ppermute | solution.py:638
  300.5 23.1 %collective-permute-start.10 = (f32[96,128]{1,0:T(8,128)S(1)}, f32[96,128]{1,0:T(8,128)S(1)}, u32[]{:S(2)}, u32[]{:S(2)}) collective-permute-start(f32[96,128]{1,0:T(8,128)S(1)} %fusion.19), channel_id=1, source_target_pairs={{0,4},{2,6},{4,0},{6,2},{8,12},{10,14},{12,8},{14,10},{16,20},{18,... | collective-permute-start | bytes 147464 | tf_op jit(solution)/shard_map/ppermute | solution.py:638
  301.6 29.2 %collective-permute-start.16 = (f32[48,1152]{1,0:T(8,128)S(1)}, f32[48,1152]{1,0:T(8,128)S(1)}, u32[]{:S(2)}, u32[]{:S(2)}) collective-permute-start(f32[48,1152]{1,0:T(8,128)S(1)} %constant_dynamic-slice_fusion.11), channel_id=1, source_target_pairs={{0,16},{2,18},{4,20},{6,22},{8,24},{10,26},{12,28},{14,30},{16,0},... | collective-permute-start | bytes 663560 | tf_op jit(solution)/shard_map/ppermute | solution.py:638
  323.7 4.7 collective-permute-start.11
  327.3 28.9 %collective-permute-start.43 = (f32[384,768]{1,0:T(8,128)S(1)}, f32[384,768]{1,0:T(8,128)S(1)}, u32[]{:S(2)}, u32[]{:S(2)}) collective-permute-start(f32[384,768]{1,0:T(8,128)S(1)} %maximum_select_fusion.9), channel_id=1, source_target_pairs={{0,4},{2,6},{4,0},{6,2},{8,12},{10,14},{12,8},{14,10},{16,20},{18,... | collective-permute-start | bytes 3538952 | tf_op jit(solution)/shard_map/ppermute | solution.py:638
  328.4 31.0 %collective-permute-start.12 = (f32[96,128]{1,0:T(8,128)S(1)}, f32[96,128]{1,0:T(8,128)S(1)}, u32[]{:S(2)}, u32[]{:S(2)}) collective-permute-start(f32[96,128]{1,0:T(8,128)S(1)} %add.211), channel_id=1, source_target_pairs={{0,16},{2,18},{4,20},{6,22},{8,24},{10,26},{12,28},{14,30},{16,0},... | collective-permute-start | bytes 147464 | tf_op jit(solution)/shard_map/ppermute | solution.py:638
  330.8 29.2 %collective-permute-start.17 = (f32[48,1152]{1,0:T(8,128)S(1)}, f32[48,1152]{1,0:T(8,128)S(1)}, u32[]{:S(2)}, u32[]{:S(2)}) collective-permute-start(f32[48,1152]{1,0:T(8,128)S(1)} %dynamic-slice_add_fusion.13), channel_id=1, source_target_pairs={{0,16},{2,18},{4,20},{6,22},{8,24},{10,26},{12,28},{14,30},{16,0},... | collective-permute-start | bytes 663560 | tf_op jit(solution)/shard_map/ppermute | solution.py:638
  332.0 28.5 %collective-permute-start.22 = (f32[224,768]{1,0:T(8,128)S(1)}, f32[224,768]{1,0:T(8,128)S(1)}, u32[]{:S(2)}, u32[]{:S(2)}) collective-permute-start(f32[224,768]{1,0:T(8,128)S(1)} %constant_dynamic-slice_fusion.10), channel_id=1, source_target_pairs={{0,2},{2,0},{4,6},{6,4},{8,10},{10,8},{12,14},{14,12},{16,18},{18,... | collective-permute-start | bytes 2064392 | tf_op jit(solution)/shard_map/ppermute | solution.py:638
  335.5 142.4 %collective-permute-start.36 = (f32[384,1536]{1,0:T(8,128)S(1)}, f32[384,1536]{1,0:T(8,128)}, u32[]{:S(2)}, u32[]{:S(2)}) collective-permute-start(f32[384,1536]{1,0:T(8,128)S(1)} %maximum_select_fusion.4), channel_id=1, source_target_pairs={{0,4},{2,6},{4,0},{6,2},{8,12},{10,14},{12,8},{14,10},{16,20},{18,... | collective-permute-start | bytes 7077896 | tf_op jit(solution)/shard_map/ppermute | solution.py:638
  357.9 125.3 %collective-permute-start.44 = (f32[768,768]{1,0:T(8,128)}, f32[768,768]{1,0:T(8,128)}, u32[]{:S(2)}, u32[]{:S(2)}) collective-permute-start(f32[768,768]{1,0:T(8,128)} %maximum_select_fusion.5), channel_id=1, source_target_pairs={{0,2},{2,0},{4,6},{6,4},{8,10},{10,8},{12,14},{14,12},{16,18},{18,... | collective-permute-start | bytes 7077896 | tf_op jit(solution)/shard_map/ppermute | solution.py:638
  360.1 9.6 %collective-permute-start.18 = (f32[96,1152]{1,0:T(8,128)S(1)}, f32[96,1152]{1,0:T(8,128)S(1)}, u32[]{:S(2)}, u32[]{:S(2)}) collective-permute-start(f32[96,1152]{1,0:T(8,128)S(1)} %maximum_select_fusion.14), channel_id=1, source_target_pairs={{0,8},{2,10},{4,12},{6,14},{8,0},{10,2},{12,4},{14,6},{16,24},{18,... | collective-permute-start | bytes 1327112 | tf_op jit(solution)/shard_map/ppermute | solution.py:638
  360.7 14.5 %collective-permute-start.23 = (f32[112,768]{1,0:T(8,128)S(1)}, f32[112,768]{1,0:T(8,128)S(1)}, u32[]{:S(2)}, u32[]{:S(2)}) collective-permute-start(f32[112,768]{1,0:T(8,128)S(1)} %constant_dynamic-slice_fusion.9), channel_id=1, source_target_pairs={{0,8},{2,10},{4,12},{6,14},{8,0},{10,2},{12,4},{14,6},{16,24},{18,... | collective-permute-start | bytes 1032200 | tf_op jit(solution)/shard_map/ppermute | solution.py:638
  369.8 53.0 %collective-permute-start.19 = (f32[192,1152]{1,0:T(8,128)S(1)}, f32[192,1152]{1,0:T(8,128)S(1)}, u32[]{:S(2)}, u32[]{:S(2)}) collective-permute-start(f32[192,1152]{1,0:T(8,128)S(1)} %maximum_select_fusion.10), channel_id=1, source_target_pairs={{0,4},{2,6},{4,0},{6,2},{8,12},{10,14},{12,8},{14,10},{16,20},{18,... | collective-permute-start | bytes 2654216 | tf_op jit(solution)/shard_map/ppermute | solution.py:638
  375.3 9.1 %collective-permute-start.24 = (f32[56,768]{1,0:T(8,128)S(1)}, f32[56,768]{1,0:T(8,128)S(1)}, u32[]{:S(2)}, u32[]{:S(2)}) collective-permute-start(f32[56,768]{1,0:T(8,128)S(1)} %constant_dynamic-slice_fusion.8), channel_id=1, source_target_pairs={{0,16},{2,18},{4,20},{6,22},{8,24},{10,26},{12,28},{14,30},{16,0},... | collective-permute-start | bytes 516104 | tf_op jit(solution)/shard_map/ppermute | solution.py:638
  384.4 7.7 %collective-permute-start.25 = (f32[56,768]{1,0:T(8,128)S(1)}, f32[56,768]{1,0:T(8,128)S(1)}, u32[]{:S(2)}, u32[]{:S(2)}) collective-permute-start(f32[56,768]{1,0:T(8,128)S(1)} %dynamic-slice_add_fusion.14), channel_id=1, source_target_pairs={{0,16},{2,18},{4,20},{6,22},{8,24},{10,26},{12,28},{14,30},{16,0},... | collective-permute-start | bytes 516104 | tf_op jit(solution)/shard_map/ppermute | solution.py:638
  385.1 45.2 %copy-start.34 = (f32[512]{0:T(512)}, f32[512]{0:T(512)S(1)}, u32[]{:S(2)}) copy-start(f32[512]{0:T(512)S(1)} %get-tuple-element.99) | copy-start | bytes 6148
  392.8 34.7 %collective-permute-start.26 = (f32[112,768]{1,0:T(8,128)}, f32[112,768]{1,0:T(8,128)}, u32[]{:S(2)}, u32[]{:S(2)}) collective-permute-start(f32[112,768]{1,0:T(8,128)} %maximum_select_fusion.15), channel_id=1, source_target_pairs={{0,8},{2,10},{4,12},{6,14},{8,0},{10,2},{12,4},{14,6},{16,24},{18,... | collective-permute-start | bytes 1032200 | tf_op jit(solution)/shard_map/ppermute | solution.py:638
  424.2 65.6 %collective-permute-start.20 = (f32[384,1152]{1,0:T(8,128)}, f32[384,1152]{1,0:T(8,128)}, u32[]{:S(2)}, u32[]{:S(2)}) collective-permute-start(f32[384,1152]{1,0:T(8,128)} %maximum_select_fusion.6), channel_id=1, source_target_pairs={{0,2},{2,0},{4,6},{6,4},{8,10},{10,8},{12,14},{14,12},{16,18},{18,... | collective-permute-start | bytes 5308424 | tf_op jit(solution)/shard_map/ppermute | solution.py:638
  428.9 47.8 %collective-permute-start.27 = (f32[224,768]{1,0:T(8,128)S(1)}, f32[224,768]{1,0:T(8,128)S(1)}, u32[]{:S(2)}, u32[]{:S(2)}) collective-permute-start(f32[224,768]{1,0:T(8,128)S(1)} %maximum_select_fusion.11), channel_id=1, source_target_pairs={{0,2},{2,0},{4,6},{6,4},{8,10},{10,8},{12,14},{14,12},{16,18},{18,... | collective-permute-start | bytes 2064392 | tf_op jit(solution)/shard_map/ppermute | solution.py:638
  476.9 28.4 %collective-permute-start.28 = (f32[448,768]{1,0:T(8,128)S(1)}, f32[448,768]{1,0:T(8,128)S(1)}, u32[]{:S(2)}, u32[]{:S(2)}) collective-permute-start(f32[448,768]{1,0:T(8,128)S(1)} %maximum_select_fusion.7), channel_id=1, source_target_pairs={{0,4},{2,6},{4,0},{6,2},{8,12},{10,14},{12,8},{14,10},{16,20},{18,... | collective-permute-start | bytes 4128776 | tf_op jit(solution)/shard_map/ppermute | solution.py:638
  (33 other events, 141.3 us)

commit v3 on v2

--- a/solution.py
+++ b/solution.py
@@ -17,6 +17,26 @@
 FULL = ((1,), (0,))
 RIGHT = ((1,), (1,))
 LEFT = ((0,), (0,))
+SCHEDULE = " ".join(
+    (
+        "R a R E",
+        "h b R E",
+        "i R H E",
+        "R E R w",
+        "H E o s",
+        "R H s R",
+        "s H E H",
+        "s E R E",
+        "H H p H",
+        "E H",
+    )
+)
+
+
+def cost(micros):
+    return pl.CostEstimate(
+        flops=micros * 10**9, transcendentals=0, bytes_accessed=micros * 3 * 10**6
+    )
 
 
 def mult(left, right, dims=FULL):
@@ -74,6 +94,7 @@
     return pl.pallas_call(
         bias_kernel,
         out_shape=jax.ShapeDtypeStruct((heads, length, length), jnp.float32),
+        cost_estimate=cost(2),
         name="distance_bias",
     )(padded)
 
@@ -200,6 +221,7 @@
             out(width, jnp.bfloat16),
             out(model, jnp.float32),
         ],
+        cost_estimate=cost(15),
         name="attend",
     )(
         patches,
@@ -360,6 +382,7 @@
             jax.ShapeDtypeStruct((1, units), jnp.float32),
             jax.ShapeDtypeStruct((1, model), jnp.float32),
         ],
+        cost_estimate=cost(23),
         name="feed",
     )(
         valid,
@@ -524,6 +547,7 @@
             sums(3 * width),
             jax.ShapeDtypeStruct((heads, 2 * length), jnp.float32),
         ],
+        cost_estimate=cost(24),
         name="attend_back",
     )(
         middle,
@@ -624,6 +648,7 @@
             sums(channels),
             sums(channels),
         ],
+        cost_estimate=cost(10),
         name="stem_back",
     )(patches, hidden, own, other, grad_middle, gain, image, features, mean, inverse)
 
@@ -644,26 +669,100 @@
     return values
 
 
-def sum_by_halving(values, order):
-    rank = lax.axis_index("dp")
-    for bit in order:
-        half = values.shape[0] // 2
-        side = (rank >> bit) & 1
-        sent = lax.dynamic_slice_in_dim(values, (1 - side) * half, half, 0)
-        kept = lax.dynamic_slice_in_dim(values, side * half, half, 0)
-        values = kept + exchange(sent, bit)
-    for bit in reversed(order):
-        side = (rank >> bit) & 1
-        other = exchange(values, bit)
-        values = jnp.where(
-            side == 1, jnp.concatenate([other, values]), jnp.concatenate([values, other])
-        )
-    return values
-
-
-def orders():
-    bits = tuple(range(lax.axis_size("dp").bit_length() - 1))
-    return bits, (bits[1], bits[0]) + bits[2:]
+class Chain:
+    def __init__(self):
+        self.token = ()
+
+    def enter(self, *arrays):
+        held = lax.optimization_barrier((*self.token, *arrays))
+        return held[len(self.token) :]
+
+    def leave(self, *arrays):
+        self.token = arrays
+        return arrays
+
+
+def cut(values, side):
+    half = values.shape[1] // 2
+    return lax.dynamic_slice_in_dim(values, side * half, half, 1)
+
+
+def spread(side, mine, other):
+    return jnp.where(
+        side == 1,
+        jnp.concatenate([other, mine], axis=1),
+        jnp.concatenate([mine, other], axis=1),
+    )
+
+
+def regroup(arrays, count):
+    if len(arrays) == count:
+        return list(arrays)
+    if count == 1:
+        return [jnp.concatenate(arrays, axis=0)]
+    return list(jnp.split(arrays[0], count, axis=0))
+
+
+class Stream:
+    def __init__(self, chain):
+        bits = lax.axis_size("dp").bit_length() - 1
+        self.chain = chain
+        self.rank = lax.axis_index("dp")
+        self.plan = ((0, 1), (1, 0)) + tuple((bit,) for bit in range(2, bits))
+        self.stage = 0
+
+    def bits(self, stage):
+        steps = self.plan + self.plan[::-1]
+        return steps[stage]
+
+    def sides(self, stage):
+        return [(self.rank >> bit) & 1 for bit in self.bits(stage)]
+
+    def send(self, arrays):
+        arrays = self.chain.leave(*arrays)
+        self.flight = [exchange(array, bit) for array, bit in zip(arrays, self.bits(self.stage))]
+
+    def launch(self, *parts):
+        sides = self.sides(0)
+        self.send([part(1 - side) for part, side in zip(parts, sides)])
+        self.kept = [part(side) for part, side in zip(parts, sides)]
+
+    def step(self):
+        steps = len(self.plan)
+        if self.stage == 2 * steps:
+            return
+        held = self.chain.enter(*self.flight)
+        self.stage += 1
+        if self.stage < steps:
+            count = len(self.bits(self.stage))
+            kept, held = regroup(self.kept, count), regroup(held, count)
+            sides = self.sides(self.stage)
+            pairs = list(zip(kept, held, sides))
+            self.send([cut(mine, 1 - side) + cut(other, 1 - side) for mine, other, side in pairs])
+            self.kept = [cut(mine, side) + cut(other, side) for mine, other, side in pairs]
+        elif self.stage == steps:
+            self.values = [mine + other for mine, other in zip(self.kept, held)]
+            self.send(self.values)
+        else:
+            sides = self.sides(self.stage - 1)
+            self.last = list(zip(sides, self.values, held))
+            if self.stage < 2 * steps:
+                values = [spread(*entry) for entry in self.last]
+                self.values = regroup(values, len(self.bits(self.stage)))
+                self.send(self.values)
+            else:
+                self.chain.leave(*held)
+
+    def finish(self):
+        while self.stage < 2 * len(self.plan):
+            self.step()
+        return self.last
+
+
+def piece(entry, start, stop):
+    side, mine, other = entry
+    whole_rows = spread(side, mine[start:stop], other[start:stop])
+    return whole_rows.reshape(-1, whole_rows.shape[2])
 
 
 def pack(arrays):
@@ -774,107 +873,202 @@
         reduce_weight,
         upstream,
     )
-    grad_reduce_weight = mult(active_low, grad_reduced_low, LEFT)
-    grad_expand_weight = mult(second_low, grad_expanded_low, LEFT)
-    block_output = (middle + (reduced + swap_core(reduced)) + reduce_bias).astype(jnp.bfloat16)
+    chain = Chain()
+    reduces, expands, others = Stream(chain), Stream(chain), Stream(chain)
+    streams = {"R": reduces, "E": expands, "H": others}
+    slot = 256
+    state = {}
+
+    def reduce_part(at, size):
+        def part(side):
+            units = lax.dynamic_slice_in_dim(active_low, at + side * (size // 2), size // 2, 1)
+            return mult(units, grad_reduced_low, LEFT)[None]
+
+        return part
+
+    def expand_part(at, size):
+        def part(side):
+            half = second_low.shape[1] // 2
+            columns = lax.dynamic_slice_in_dim(state["second"], side * half, half, 1)
+            return mult(columns, grad_expanded_low[:, at : at + size], LEFT)[None]
+
+        return part
+
+    def launch_reduces():
+        size = active_low.shape[1] // 2
+        reduces.launch(reduce_part(0, size), reduce_part(size, size))
+
+    def launch_expands():
+        (state["second"],) = chain.enter(second_low)
+        size = grad_expanded_low.shape[1] // 2
+        expands.launch(expand_part(0, size), expand_part(size, size))
+
+    def run_attend_back():
+        (other,) = chain.enter(other_second)
+        state["attend"] = attend_back(
+            items,
+            middle,
+            grad_second,
+            other,
+            grad_reduced_low,
+            row(second_gain),
+            merge_weight,
+            mixed,
+            head_gains,
+            probs,
+            heads_low,
+            heads_weight,
+        )
+        grad_first = state["attend"][3]
+        chain.leave(grad_first)
+        state["other_first"] = swap_core(grad_first)
+
+    def run_heads():
+        first, scaled = chain.enter(first_low, scaled_low)
+        grad_branch, grad_heads = state["attend"][1:3]
+        split = lambda array, at, size: array[:, at : at + size]
+        half = grad_branch.shape[1] // 2
+        state["grads"] = chain.leave(
+            *(mult(first, split(grad_heads, k * width, width), LEFT) for k in range(3)),
+            *(mult(scaled, split(grad_branch, k * half, half), LEFT) for k in range(2)),
+        )
+
+    def run_stem_back():
+        (other,) = chain.enter(state["other_first"])
+        grad_middle, grad_first = state["attend"][0], state["attend"][3]
+        state["stem"] = stem_back(
+            patches,
+            hidden,
+            grad_first,
+            other,
+            grad_middle,
+            row(first_gain),
+            image_weight,
+            patch_features,
+            row(stem_mean),
+            row(stem_inverse),
+        )
+        chain.leave(state["stem"][0])
+
+    def run_image():
+        (stem,) = chain.enter(stem_low)
+        grad_embedded = state["stem"][1]
+        half = grad_embedded.shape[1] // 2
+        state["image"] = chain.leave(
+            *(mult(stem, grad_embedded[:, k * half : k * half + half], LEFT) for k in range(2))
+        )
+
+    def launch_others():
+        stack = lambda *arrays: [array.reshape(-1, slot, array.shape[1]) for array in arrays]
+        grads, image = state["grads"], state["image"]
+        left = stack(grads[0], grads[1], image[0])
+        merge = jnp.concatenate([grads[3], grads[4]], axis=0)
+        right = stack(grads[2], merge, image[1])
+        part = lambda pieces: lambda side: jnp.concatenate([cut(p, side) for p in pieces])
+        others.launch(part(left), part(right))
+
+    def small_step():
+        steps = lax.axis_size("dp").bit_length() - 1
+        bit = state.setdefault("bit", 0)
+        if bit == 0:
+            attend_sums, stem_sums = state["attend"][4:], state["stem"][3:]
+            heads_total = jnp.sum(attend_sums[3].reshape(heads, HEAD_DIM), axis=1)
+            table = attend_sums[5][:, : distance_table.shape[1]]
+            state["small"] = (*attend_sums[:3], heads_total, attend_sums[4], table, *stem_sums)
+            state["small"] += (grad_expand_bias, grad_reduce_bias)
+            (packed,) = chain.enter(pack(state["small"]))
+        else:
+            packed, moved = chain.enter(state["packed"], state["moved"])
+            packed = packed + moved
+        (state["packed"],) = chain.leave(packed)
+        if bit < steps:
+            state["moved"] = exchange(packed, bit)
+        state["bit"] = bit + 1
+
+    def swap_reduced():
+        (value,) = chain.enter(reduced)
+        state["reduced"] = value
+        state["other_reduced"] = swap_core(value)
+
+    def run_output():
+        (other,) = chain.enter(state["other_reduced"])
+        block_output = (middle + (state["reduced"] + other) + reduce_bias).astype(jnp.bfloat16)
+        (state["output"],) = chain.leave(block_output)
+
+    def run_patch():
+        while state["bit"] <= lax.axis_size("dp").bit_length() - 1:
+            small_step()
+        state["small"] = unpack(state["packed"], state["small"])
+        stem_gain_sum, stem_shift_sum = state["small"][8:10]
+        (feature,) = chain.enter(patch_features)
+        hat = (feature.astype(jnp.float32) - stem_mean) * stem_inverse
+        patch_grad = (
+            patch_mask[:, None]
+            * stem_inverse
+            * stem_gain
+            * (state["stem"][2] - stem_shift_sum / count - hat * stem_gain_sum / count)
+        )
+        (state["patch"],) = chain.leave(patch_grad)
+
+    other_second = swap_core(grad_second)
+    blocks = {
+        "a": run_attend_back,
+        "h": run_heads,
+        "b": run_stem_back,
+        "i": run_image,
+        "s": small_step,
+        "w": swap_reduced,
+        "o": run_output,
+        "p": run_patch,
+    }
+    starts = {"R": launch_reduces, "E": launch_expands, "H": launch_others}
+    for step in SCHEDULE.split():
+        if step in starts:
+            starts.pop(step)()
+        elif step in streams:
+            streams[step].step()
+        else:
+            blocks[step]()
+    last = {name: stream.finish() for name, stream in streams.items()}
+    grad_reduce_weight = jnp.concatenate([piece(entry, 0, 1) for entry in last["R"]], axis=0)
+    grad_expand_weight = jnp.concatenate([piece(entry, 0, 1) for entry in last["E"]], axis=1)
+    left, right = last["H"]
+    model = layer_input.shape[1]
+    chunk, deep, image_deep = model // slot, merge_weight.shape[0], image_weight.shape[0] // slot
+    grad_query_weight = piece(left, 0, chunk)
+    grad_key_weight = piece(left, chunk, 2 * chunk)
+    grad_value_weight = piece(right, 0, chunk)
+    merge = piece(right, chunk, 2 * chunk)
+    grad_merge_weight = jnp.concatenate([merge[:deep], merge[deep:]], axis=1)
+    grad_image_weight = jnp.concatenate(
+        [
+            piece(left, 2 * chunk, 2 * chunk + image_deep),
+            piece(right, 2 * chunk, 2 * chunk + image_deep),
+        ],
+        axis=1,
+    )
     (
-        grad_middle,
-        grad_branch_low,
-        grad_heads_low,
-        grad_first,
         grad_second_gain,
         grad_second_shift,
         grad_merge_bias,
-        head_sums,
+        grad_head_gain,
         heads_sums,
-        grad_table,
-    ) = attend_back(
-        items,
-        middle,
-        grad_second,
-        swap_core(grad_second),
-        grad_reduced_low,
-        row(second_gain),
-        merge_weight,
-        mixed,
-        head_gains,
-        probs,
-        heads_low,
-        heads_weight,
-    )
-    grad_merge_weight = mult(scaled_low, grad_branch_low, LEFT)
-    grad_heads_weight = mult(first_low, grad_heads_low, LEFT)
-    (
-        input_grad,
-        grad_embedded_low,
-        grad_stem,
-        grad_first_gain,
-        grad_first_shift,
-        gain_local,
-        shift_local,
-    ) = stem_back(
-        patches,
-        hidden,
-        grad_first,
-        swap_core(grad_first),
-        grad_middle,
-        row(first_gain),
-        image_weight,
-        patch_features,
-        row(stem_mean),
-        row(stem_inverse),
-    )
-    grad_image_weight = mult(stem_low, grad_embedded_low, LEFT)
-    first_order, second_order = orders()
-    grad_reduce_weight = sum_by_halving(grad_reduce_weight, first_order)
-    grad_expand_weight = sum_by_halving(grad_expand_weight, second_order)
-    merge_rows = grad_merge_weight.shape[0]
-    row_weights = sum_by_halving(
-        jnp.concatenate([grad_merge_weight, grad_image_weight]), second_order
-    )
-    grad_merge_weight, grad_image_weight = row_weights[:merge_rows], row_weights[merge_rows:]
-    grad_heads_weight = sum_by_halving(grad_heads_weight, first_order)
-    small = (
-        heads_sums,
-        grad_merge_bias,
-        jnp.sum(head_sums.reshape(heads, HEAD_DIM), axis=1),
-        grad_table[:, : distance_table.shape[1]],
-        grad_first_gain,
-        grad_first_shift,
-        grad_second_gain,
-        grad_second_shift,
-        grad_expand_bias,
-        grad_reduce_bias,
-        gain_local,
-        shift_local,
-    )
-    (
-        heads_sums,
-        grad_merge_bias,
-        grad_head_gain,
         grad_distance_table,
         grad_first_gain,
         grad_first_shift,
-        grad_second_gain,
-        grad_second_shift,
+        grad_stem_gain,
+        grad_stem_shift,
         grad_expand_bias,
         grad_reduce_bias,
-        grad_stem_gain,
-        grad_stem_shift,
-    ) = unpack(sum_by_doubling(pack(small)), small)
-    patch_grad = (
-        patch_mask[:, None]
-        * stem_inverse
-        * stem_gain
-        * (grad_stem - grad_stem_shift / count - stem_hat * grad_stem_gain / count)
-    )
+    ) = state["small"]
+    block_output, input_grad, patch_grad = state["output"], state["stem"][0], state["patch"]
     return (
         block_output,
         input_grad,
         patch_grad,
-        grad_heads_weight[:, :width],
-        grad_heads_weight[:, width : 2 * width],
-        grad_heads_weight[:, 2 * width :],
+        grad_query_weight,
+        grad_key_weight,
+        grad_value_weight,
         grad_merge_weight,
         heads_sums[0, :width],
         heads_sums[0, 2 * width :],

time: 516 us -> 455 us (0.88)
  waiting for transfers between devices: 258 us -> 169 us
  other arithmetic: 62.3 us -> 84.7 us
  starting transfers between devices: 52.1 us -> 63.4 us
    ppermute x40 -> x44, waiting for transfers between devices: 255 us -> 166 us  [exchange(): lax.ppermute(values, 'dp', [(rank, rank ^ 1 << bit) for rank in range(cou...]
    ppermute x40 -> x44, starting transfers between devices: 51.3 us -> 62.9 us  [exchange(): lax.ppermute(values, 'dp', [(rank, rank ^ 1 << bit) for rank in range(cou...]
    concatenate x1 -> x9, other arithmetic: 0.41 us -> 11.9 us  [the longest x4 4.08 us: launch_others(): jnp.concatenate([cut(p, side) for p in pieces])]
    add x16 -> x19, other arithmetic: 14.3 us -> 21.3 us  [the longest x7 10.6 us: step(): cut(mine, 1 - side) + cut(other, 1 - side)]
    dynamic_slice x15 -> x4, local copies, waits for them, and re-layouts: 9.51 us -> 3.31 us  [cut(): return lax.dynamic_slice_in_dim(values, side * half, half, 1)]
    select_n x16 -> x26, other arithmetic: 26 us -> 27.8 us  [spread(): jnp.where(side == 1, jnp.concatenate([other, mine], axis=1), jnp.concaten...]
    dot_general x6 -> x16, matrix products: 22.3 us -> 23.2 us  [mult(): lax.dot_general(left, right, (dims, ((), ())), preferred_element_type=jnp...]
    unnamed x109 -> x118, local copies, waits for them, and re-layouts: 11.5 us -> 11.5 us
  transfers between devices with their start and end apart: 45 -> 49, of which waited for: 25 -> 27; matrix products, arithmetic and copies ran while one was open for 18% -> 26% of each run, Pallas kernels for 7% -> 8%
where the time goes in v3:
time: 455 us; the launch traced here: 451 us
  waiting for transfers between devices  169 us (37%)
  other arithmetic  84.7 us (19%)
  Pallas kernels  74.1 us (16%)
  starting transfers between devices  63.4 us (14%)
  local copies, waits for them, and re-layouts  34 us (7%)
  matrix products  23.2 us (5%)
    ppermute x44, waiting for transfers between devices, exchange(): lax.ppermute(values, 'dp', [(rank, rank ^ 1 << bit) for rank in range(cou...  166 us
    ppermute x44, starting transfers between devices, exchange(): lax.ppermute(values, 'dp', [(rank, rank ^ 1 << bit) for rank in range(cou...  62.9 us
    select_n x26, other arithmetic, spread(): jnp.where(side == 1, jnp.concatenate([other, mine], axis=1), jnp.concaten...  27.8 us
    pallas_call x1, Pallas kernels, attend_back(): pl.pallas_call(attend_back_kernel, grid_spec=pltpu.PrefetchScalarGridSpec...  23.6 us
    dot_general x16, matrix products, mult(): lax.dot_general(left, right, (dims, ((), ())), preferred_element_type=jnp...  23.2 us
    pallas_call x1, Pallas kernels, feed(): pl.pallas_call(feed_kernel, grid_spec=pltpu.PrefetchScalarGridSpec(num_sc...  22.7 us
    pallas_call x1, Pallas kernels, attend(): pl.pallas_call(attend_kernel, grid_spec=pltpu.PrefetchScalarGridSpec(num_...  15.1 us
    unnamed x118, local copies, waits for them, and re-layouts  11.5 us
  transfers between devices with their start and end apart: 49, of which 27 were waited for; matrix products, arithmetic and copies ran while one was open for 26% of the time, Pallas kernels for 8%

profile of v3, /device:TPU:0, one launch (start us, length us, event | category | flops | bytes accessed | tf_op | source)
XLA Modules:
  0.0 450.6 jit_solution(1643186295852968209)
XLA Ops:
  5.2 3.0 collective-permute-start
  9.9 2.1 collective-permute-start.1
  13.7 2.1 collective-permute-start.2
  17.4 3.0 collective-permute-start.3
  28.5 1.9 constant_dynamic-update-slice_fusion.2
  32.1 2.3 distance_bias.1.bias_ref
  34.5 15.1 %attend.1 = (f32[1024,768]{1,0:T(8,128)}, bf16[1024,768]{1,0:T(8,128)(2,1)}, bf16[1024,1152]{1,0:T(8,128)(2,1)}, f32[4,6,256,256]{3,2,1,0:T(8,128)}, f32[1024,38...) custom-call(s32[4]{0:T(128)} %copy-done.46, s32[4]{0:T(128)} %get-tuple-element.265.valid_ref, ...), custom_call_target="tpu_custom_call" | custom-call | flops 15000000512 | bytes 45000000 | tf_op jit(solution)/shard_map/attend/pallas_call | solution.py:188
  52.2 3.4 collective-permute-done.5.other_ref
  57.2 22.7 %feed.1 = (f32[1024,768]{1,0:T(8,128)}, bf16[1024,768]{1,0:T(8,128)(2,1)}, bf16[1024,1536]{1,0:T(8,128)(2,1)}, bf16[1024,1536]{1,0:T(8,128)(2,1)}, f32[1024,768]...) custom-call(s32[4]{0:T(128)} %get-tuple-element.265.valid_ref, ...), custom_call_target="tpu_custom_call" | custom-call | flops 23000000512 | bytes 69000000 | tf_op jit(solution)/shard_map/feed/pallas_call | solution.py:345
  80.2 3.6 convolution_bitcast_fusion.3
  83.8 1.9 collective-permute-start.7
  85.6 3.0 convolution_bitcast_fusion.2
  90.1 1.8 fusion.34
  92.8 23.6 %attend_back.1 = (f32[1024,768]{1,0:T(8,128)}, bf16[1024,768]{1,0:T(8,128)(2,1)}, bf16[1024,1152]{1,0:T(8,128)(2,1)}, f32[1024,768]{1,0:T(8,128)}, f32[1,768]{1,...) custom-call(f32[1024,768]{1,0:T(8,128)} %get-tuple-element.112.middl, ...), custom_call_target="tpu_custom_call" | custom-call | flops 24000000000 | bytes 72000000 | tf_op jit(solution)/shard_map/attend_back/pallas_call | solution.py:506
  117.5 2.4 bitcast_add_fusion.6
  122.5 1.8 convolution_bitcast_fusion.1
  125.7 1.8 convolution_bitcast_fusion
  137.1 1.8 fusion.6
  138.9 1.8 fusion.10
  140.8 10.3 %stem_back.1 = (f32[1024,768]{1,0:T(8,128)}, bf16[1024,768]{1,0:T(8,128)(2,1)}, f32[1024,512]{1,0:T(8,128)}, f32[1,768]{1,0:T(1,128)}, f32[1,768]{1,0:T(1,128)}, /*index=5*/f32[1,512]{1,0:T(1,128)}, f32[1,512]{1,0:T(1,128)}) custom-call(s32[4]{0:T(128)} %copy-done.46, f32[1024,768]{1,0:T(8,128)} %get-tuple-element.110.hidden_ref, ...), custom_call_target="tpu_custom_call" | custom-call | flops 10000000000 | bytes 30000000 | tf_op jit(solution)/shard_map/stem_back/pallas_call | solution.py:616
  153.5 7.7 %collective-permute-done.12 = f32[1,384,768]{2,1,0:T(8,128)} collective-permute-done((f32[1,384,768]{2,1,0:T(8,128)}, f32[1,384,768]{2,1,0:T(8,128)}, u32[]{:S(2)}, u32[]{:S(2)}) %collective-permute-start.12) | collective-permute-done | bytes 1179680 | tf_op jit(solution)/shard_map/ppermute | solution.py:663
  173.9 7.5 %collective-permute-done.16 = f32[2,96,768]{2,1,0:T(8,128)S(1)} collective-permute-done((f32[2,96,768]{2,1,0:T(8,128)S(1)}, f32[2,96,768]{2,1,0:T(8,128)S(1)}, u32[]{:S(2)}, u32[]{:S(2)}) %collective-permute-start.16) | collective-permute-done | bytes 589856 | tf_op jit(solution)/shard_map/ppermute | solution.py:663
  182.2 2.5 collective-permute-start.17
  187.7 8.9 %collective-permute-done.17 = f32[2,48,768]{2,1,0:T(8,128)} collective-permute-done((f32[2,48,768]{2,1,0:T(8,128)}, f32[2,48,768]{2,1,0:T(8,128)}, u32[]{:S(2)}, u32[]{:S(2)}) %collective-permute-start.17) | collective-permute-done | bytes 294944 | tf_op jit(solution)/shard_map/ppermute | solution.py:663
  196.5 1.9 add_add_fusion.2
  198.4 8.5 %collective-permute-done.18 = f32[2,96,768]{2,1,0:T(8,128)} collective-permute-done((f32[2,96,768]{2,1,0:T(8,128)}, f32[2,96,768]{2,1,0:T(8,128)}, u32[]{:S(2)}, u32[]{:S(2)}) %collective-permute-start.18) | collective-permute-done | bytes 589856 | tf_op jit(solution)/shard_map/ppermute | solution.py:663
  208.7 5.2 %collective-permute-done.19 = f32[2,48,768]{2,1,0:T(8,128)} collective-permute-done((f32[2,48,768]{2,1,0:T(8,128)}, f32[2,48,768]{2,1,0:T(8,128)}, u32[]{:S(2)}, u32[]{:S(2)}) %collective-permute-start.19) | collective-permute-done | bytes 294944 | tf_op jit(solution)/shard_map/ppermute | solution.py:663
  213.9 2.1 maximum_select_fusion.24
  235.9 3.6 collective-permute-start.24
  239.6 13.6 %collective-permute-done.20 = f32[8,128,384]{2,1,0:T(8,128)} collective-permute-done((f32[8,128,384]{2,1,0:T(8,128)}, f32[8,128,384]{2,1,0:T(8,128)}, u32[]{:S(2)}, u32[]{:S(2)}) %collective-permute-start.20) | collective-permute-done | bytes 1572896 | tf_op jit(solution)/shard_map/ppermute | solution.py:663
  258.4 1.8 collective-permute-start.25
  261.3 4.0 add_convert_fusion
  268.1 8.2 %collective-permute-done.26 = f32[8,64,384]{2,1,0:T(8,128)S(1)} collective-permute-done((f32[8,64,384]{2,1,0:T(8,128)S(1)}, f32[8,64,384]{2,1,0:T(8,128)S(1)}, u32[]{:S(2)}, u32[]{:S(2)}) %collective-permute-start.26) | collective-permute-done | bytes 786464 | tf_op jit(solution)/shard_map/ppermute | solution.py:663
  276.3 2.5 collective-permute-done.25
  281.7 3.4 collective-permute-start.32
  285.1 3.4 collective-permute-done.27
  290.8 2.4 maximum_select_fusion.8
  293.2 2.4 maximum_select_fusion.9
  295.7 7.1 %collective-permute-done.31 = f32[16,32,384]{2,1,0:T(8,128)} collective-permute-done((f32[16,32,384]{2,1,0:T(8,128)}, f32[16,32,384]{2,1,0:T(8,128)}, u32[]{:S(2)}, u32[]{:S(2)}) %collective-permute-start.31) | collective-permute-done | bytes 786464 | tf_op jit(solution)/shard_map/ppermute | solution.py:663
  302.7 1.8 dynamic-slice_add_fusion.4
  306.8 2.5 collective-permute-start.35
  311.9 10.8 %collective-permute-done.33 = f32[16,16,384]{2,1,0:T(8,128)} collective-permute-done((f32[16,16,384]{2,1,0:T(8,128)}, f32[16,16,384]{2,1,0:T(8,128)}, u32[]{:S(2)}, u32[]{:S(2)}) %collective-permute-start.33) | collective-permute-done | bytes 393248 | tf_op jit(solution)/shard_map/ppermute | solution.py:663
  323.9 4.9 %collective-permute-done.34 = f32[96,128]{1,0:T(8,128)S(1)} collective-permute-done((f32[96,128]{1,0:T(8,128)S(1)}, f32[96,128]{1,0:T(8,128)S(1)}, u32[]{:S(2)}, u32[]{:S(2)}) %collective-permute-start.34) | collective-permute-done | bytes 49184 | tf_op jit(solution)/shard_map/ppermute | solution.py:663
  332.2 1.8 collective-permute-start.38
  335.3 2.6 collective-permute-done.37
  337.8 2.0 collective-permute-done.36
  339.8 1.9 maximum_select_fusion.3
  341.7 7.2 %collective-permute-done.39 = f32[1,192,768]{2,1,0:T(8,128)S(1)} collective-permute-done((f32[1,192,768]{2,1,0:T(8,128)S(1)}, f32[1,192,768]{2,1,0:T(8,128)S(1)}, u32[]{:S(2)}, u32[]{:S(2)}) %collective-permute-start.39) | collective-permute-done | bytes 589856 | tf_op jit(solution)/shard_map/ppermute | solution.py:663
  351.1 3.0 collective-permute-done.40
  354.2 1.9 maximum_select_fusion.2
  356.1 2.5 pad_maximum_fusion.1
  359.5 1.8 collective-permute-start.45
  361.6 9.9 %collective-permute-done.41 = f32[16,32,384]{2,1,0:T(8,128)S(1)} collective-permute-done((f32[16,32,384]{2,1,0:T(8,128)S(1)}, f32[16,32,384]{2,1,0:T(8,128)S(1)}, u32[]{:S(2)}, u32[]{:S(2)}) %collective-permute-start.41) | collective-permute-done | bytes 786464 | tf_op jit(solution)/shard_map/ppermute | solution.py:663
  373.0 2.9 collective-permute-start.44
  380.4 3.6 subtract_multiply_fusion
  384.0 19.6 %collective-permute-done.44 = f32[8,64,384]{2,1,0:T(8,128)} collective-permute-done((f32[8,64,384]{2,1,0:T(8,128)}, f32[8,64,384]{2,1,0:T(8,128)}, u32[]{:S(2)}, u32[]{:S(2)}) %collective-permute-start.44) | collective-permute-done | bytes 786464 | tf_op jit(solution)/shard_map/ppermute | solution.py:663
  403.6 2.1 maximum_select_fusion.6
  406.5 2.3 maximum_select_fusion.5
  408.8 1.8 collective-permute-start.47
  411.9 1.9 maximum_select_fusion.1
  413.8 1.9 maximum_select_fusion
  415.8 2.9 pad_maximum_fusion
  418.7 21.6 %collective-permute-done.48 = f32[8,128,384]{2,1,0:T(8,128)S(1)} collective-permute-done((f32[8,128,384]{2,1,0:T(8,128)S(1)}, f32[8,128,384]{2,1,0:T(8,128)S(1)}, u32[]{:S(2)}, u32[]{:S(2)}) %collective-permute-start.48) | collective-permute-done | bytes 1572896 | tf_op jit(solution)/shard_map/ppermute | solution.py:663
  440.3 2.6 collective-permute-done.47
  (299 shorter events, 124.8 us)
Async XLA Ops:
  0.7 22.0 %copy-start.2 = (bf16[1024,512]{1,0:T(8,128)(2,1)S(1)}, bf16[1024,512]{1,0:T(8,128)(2,1)}, u32[]{:S(2)}) copy-start(bf16[1024,512]{1,0:T(8,128)(2,1)} %features_ref.1) | copy-start | bytes 3145732
  1.9 21.8 %copy-start.46 = (s32[4]{0:T(128)}, s32[4]{0:T(128)S(1)}, u32[]{:S(2)}) copy-start(s32[4]{0:T(128)S(1)} %get-tuple-element.264.patches_ref) | copy-start | bytes 52
  3.4 20.4 %copy-start.22 = (bf16[512,768]{1,0:T(8,128)(2,1)S(1)}, bf16[512,768]{1,0:T(8,128)(2,1)}, u32[]{:S(2)}) copy-start(bf16[512,768]{1,0:T(8,128)(2,1)} %image_ref.1) | copy-start | bytes 2359300
  5.2 4.6 %collective-permute-start = (f32[3,512]{1,0:T(4,128)S(1)}, f32[3,512]{1,0:T(4,128)S(1)}, u32[]{:S(2)}, u32[]{:S(2)}) collective-permute-start(f32[3,512]{1,0:T(4,128)S(1)} %maximum_maximum_fusion), channel_id=1, source_target_pairs={{0,2},{2,0},{4,6},{6,4},{8,10},{10,8},{12,14},{14,12},{16,18},{18,... | collective-permute-start | bytes 18440 | tf_op jit(solution)/shard_map/ppermute | solution.py:663
  9.9 3.7 collective-permute-start.1
  13.7 3.7 collective-permute-start.2
  17.4 4.7 %collective-permute-start.3 = (f32[3,512]{1,0:T(4,128)S(1)}, f32[3,512]{1,0:T(4,128)S(1)}, u32[]{:S(2)}, u32[]{:S(2)}) collective-permute-start(f32[3,512]{1,0:T(4,128)S(1)} %add.278), channel_id=1, source_target_pairs={{0,16},{2,18},{4,20},{6,22},{8,24},{10,26},{12,28},{14,30},{16,0},... | collective-permute-start | bytes 18440 | tf_op jit(solution)/shard_map/ppermute | solution.py:663
  24.9 9.6 %collective-permute-start.4 = (f32[1024,768]{1,0:T(8,128)S(1)}, f32[1024,768]{1,0:T(8,128)}, u32[]{:S(2)}, u32[]{:S(2)}) collective-permute-start(f32[1024,768]{1,0:T(8,128)S(1)} %fusion.65.own_ref), channel_id=1, source_target_pairs={{0,1},{1,0},{2,3},{3,2},{4,5},{5,4},{6,7},{7,6},{8,9},{9,8},{10,11... | collective-permute-start | bytes 9437192 | tf_op jit(solution)/shard_map/ppermute | solution.py:658
  34.5 15.3 %copy-start.40 = (f32[768]{0:T(1024)S(1)}, f32[768]{0:T(1024)}, u32[]{:S(2)}) copy-start(f32[768]{0:T(1024)} %param.41) | copy-start | bytes 9220
  34.5 15.9 %copy-start.41 = (f32[768]{0:T(1024)S(1)}, f32[768]{0:T(1024)}, u32[]{:S(2)}) copy-start(f32[768]{0:T(1024)} %param.36) | copy-start | bytes 9220
  34.5 16.5 %copy-start.42 = (f32[768]{0:T(1024)S(1)}, f32[768]{0:T(1024)}, u32[]{:S(2)}) copy-start(f32[768]{0:T(1024)} %param.42) | copy-start | bytes 9220
  34.5 17.1 %copy-start.35 = (f32[1536]{0:T(1024)S(1)}, f32[1536]{0:T(1024)}, u32[]{:S(2)}) copy-start(f32[1536]{0:T(1024)} %param.44) | copy-start | bytes 18436
  49.6 5.9 %collective-permute-start.5 = (f32[1024,768]{1,0:T(8,128)}, f32[1024,768]{1,0:T(8,128)S(1)}, u32[]{:S(2)}, u32[]{:S(2)}) collective-permute-start(f32[1024,768]{1,0:T(8,128)} %get-tuple-element.111.own_ref), channel_id=1, source_target_pairs={{0,1},{1,0},{2,3},{3,2},{4,5},{5,4},{6,7},{7,6},{8,9},{9,8},{10,11... | collective-permute-start | bytes 9437192 | tf_op jit(solution)/shard_map/ppermute | solution.py:658
  79.9 12.8 %collective-permute-start.6 = (f32[1024,768]{1,0:T(8,128)}, f32[1024,768]{1,0:T(8,128)}, u32[]{:S(2)}, u32[]{:S(2)}) collective-permute-start(f32[1024,768]{1,0:T(8,128)} %get-tuple-element.115.own_ref), channel_id=1, source_target_pairs={{0,1},{1,0},{2,3},{3,2},{4,5},{5,4},{6,7},{7,6},{8,9},{9,8},{10,11... | collective-permute-start | bytes 9437192 | tf_op jit(solution)/shard_map/ppermute | solution.py:658
  83.8 32.7 %collective-permute-start.7 = (f32[1,384,768]{2,1,0:T(8,128)}, f32[1,384,768]{2,1,0:T(8,128)S(1)}, u32[]{:S(2)}, u32[]{:S(2)}) collective-permute-start(f32[1,384,768]{2,1,0:T(8,128)} %convolution_bitcast_fusion.3), channel_id=1, source_target_pairs={{0,2},{2,0},{4,6},{6,4},{8,10},{10,8},{12,14},{14,12},{16,18},{18,... | collective-permute-start | bytes 3538952 | tf_op jit(solution)/shard_map/ppermute | solution.py:663
  88.6 28.9 %collective-permute-start.8 = (f32[1,384,768]{2,1,0:T(8,128)}, f32[1,384,768]{2,1,0:T(8,128)}, u32[]{:S(2)}, u32[]{:S(2)}) collective-permute-start(f32[1,384,768]{2,1,0:T(8,128)} %convolution_bitcast_fusion.2), channel_id=1, source_target_pairs={{0,4},{2,6},{4,0},{6,2},{8,12},{10,14},{12,8},{14,10},{16,20},{18,... | collective-permute-start | bytes 3538952 | tf_op jit(solution)/shard_map/ppermute | solution.py:663
  92.8 24.7 %copy-start.6 = (f32[384,768]{1,0:T(8,128)S(1)}, f32[384,768]{1,0:T(8,128)}, u32[]{:S(2)}) copy-start(f32[384,768]{1,0:T(8,128)} %fusion.34) | copy-start | bytes 3538948
  116.4 24.3 %collective-permute-start.9 = (f32[1024,768]{1,0:T(8,128)}, f32[1024,768]{1,0:T(8,128)}, u32[]{:S(2)}, u32[]{:S(2)}) collective-permute-start(f32[1024,768]{1,0:T(8,128)} %get-tuple-element.120.own_ref), channel_id=1, source_target_pairs={{0,1},{1,0},{2,3},{3,2},{4,5},{5,4},{6,7},{7,6},{8,9},{9,8},{10,11... | collective-permute-start | bytes 9437192 | tf_op jit(solution)/shard_map/ppermute | solution.py:658
  119.9 31.1 %collective-permute-start.11 = (f32[1,192,768]{2,1,0:T(8,128)}, f32[1,192,768]{2,1,0:T(8,128)}, u32[]{:S(2)}, u32[]{:S(2)}) collective-permute-start(f32[1,192,768]{2,1,0:T(8,128)} %get-tuple-element.217), channel_id=1, source_target_pairs={{0,2},{2,0},{4,6},{6,4},{8,10},{10,8},{12,14},{14,12},{16,18},{18,... | collective-permute-start | bytes 1769480 | tf_op jit(solution)/shard_map/ppermute | solution.py:663
  121.7 29.3 %collective-permute-start.10 = (f32[1,192,768]{2,1,0:T(8,128)}, f32[1,192,768]{2,1,0:T(8,128)}, u32[]{:S(2)}, u32[]{:S(2)}) collective-permute-start(f32[1,192,768]{2,1,0:T(8,128)} %get-tuple-element.219), channel_id=1, source_target_pairs={{0,4},{2,6},{4,0},{6,2},{8,12},{10,14},{12,8},{14,10},{16,20},{18,... | collective-permute-start | bytes 1769480 | tf_op jit(solution)/shard_map/ppermute | solution.py:663
  124.3 36.9 %collective-permute-start.12 = (f32[1,384,768]{2,1,0:T(8,128)}, f32[1,384,768]{2,1,0:T(8,128)}, u32[]{:S(2)}, u32[]{:S(2)}) collective-permute-start(f32[1,384,768]{2,1,0:T(8,128)} %convolution_bitcast_fusion.1), channel_id=1, source_target_pairs={{0,2},{2,0},{4,6},{6,4},{8,10},{10,8},{12,14},{14,12},{16,18},{18,... | collective-permute-start | bytes 3538952 | tf_op jit(solution)/shard_map/ppermute | solution.py:663
  127.5 35.3 %collective-permute-start.13 = (f32[1,384,768]{2,1,0:T(8,128)}, f32[1,384,768]{2,1,0:T(8,128)}, u32[]{:S(2)}, u32[]{:S(2)}) collective-permute-start(f32[1,384,768]{2,1,0:T(8,128)} %convolution_bitcast_fusion), channel_id=1, source_target_pairs={{0,4},{2,6},{4,0},{6,2},{8,12},{10,14},{12,8},{14,10},{16,20},{18,... | collective-permute-start | bytes 3538952 | tf_op jit(solution)/shard_map/ppermute | solution.py:663
  153.3 9.5 %copy-start.21 = (f32[384,768]{1,0:T(8,128)S(1)}, f32[384,768]{1,0:T(8,128)}, u32[]{:S(2)}) copy-start(f32[384,768]{1,0:T(8,128)} %fusion.6) | copy-start | bytes 3538948
  153.5 27.9 %copy-start.14 = (f32[2,96,768]{2,1,0:T(8,128)}, f32[2,96,768]{2,1,0:T(8,128)S(1)}, u32[]{:S(2)}) copy-start(f32[2,96,768]{2,1,0:T(8,128)S(1)} %get-tuple-element.211) | copy-start | bytes 1769476
  164.3 20.5 %collective-permute-start.15 = (f32[1,192,768]{2,1,0:T(8,128)S(1)}, f32[1,192,768]{2,1,0:T(8,128)S(1)}, u32[]{:S(2)}, u32[]{:S(2)}) collective-permute-start(f32[1,192,768]{2,1,0:T(8,128)S(1)} %get-tuple-element.213), channel_id=1, source_target_pairs={{0,2},{2,0},{4,6},{6,4},{8,10},{10,8},{12,14},{14,12},{16,18},{18,... | collective-permute-start | bytes 1769480 | tf_op jit(solution)/shard_map/ppermute | solution.py:663
  167.0 17.8 %collective-permute-start.14 = (f32[1,192,768]{2,1,0:T(8,128)S(1)}, f32[1,192,768]{2,1,0:T(8,128)S(1)}, u32[]{:S(2)}, u32[]{:S(2)}) collective-permute-start(f32[1,192,768]{2,1,0:T(8,128)S(1)} %get-tuple-element.215), channel_id=1, source_target_pairs={{0,4},{2,6},{4,0},{6,2},{8,12},{10,14},{12,8},{14,10},{16,20},{18,... | collective-permute-start | bytes 1769480 | tf_op jit(solution)/shard_map/ppermute | solution.py:663
  167.5 13.9 %collective-permute-start.16 = (f32[2,96,768]{2,1,0:T(8,128)S(1)}, f32[2,96,768]{2,1,0:T(8,128)S(1)}, u32[]{:S(2)}, u32[]{:S(2)}) collective-permute-start(f32[2,96,768]{2,1,0:T(8,128)S(1)} %get-tuple-element.212), channel_id=1, source_target_pairs={{0,8},{2,10},{4,12},{6,14},{8,0},{10,2},{12,4},{14,6},{16,24},{18,... | collective-permute-start | bytes 1769480 | tf_op jit(solution)/shard_map/ppermute | solution.py:663
  182.2 14.3 %collective-permute-start.17 = (f32[2,48,768]{2,1,0:T(8,128)}, f32[2,48,768]{2,1,0:T(8,128)}, u32[]{:S(2)}, u32[]{:S(2)}) collective-permute-start(f32[2,48,768]{2,1,0:T(8,128)} %dynamic-slice_add_fusion.6), channel_id=1, source_target_pairs={{0,16},{2,18},{4,20},{6,22},{8,24},{10,26},{12,28},{14,30},{16,0},... | collective-permute-start | bytes 884744 | tf_op jit(solution)/shard_map/ppermute | solution.py:663
  186.0 20.9 %collective-permute-start.18 = (f32[2,96,768]{2,1,0:T(8,128)}, f32[2,96,768]{2,1,0:T(8,128)}, u32[]{:S(2)}, u32[]{:S(2)}) collective-permute-start(f32[2,96,768]{2,1,0:T(8,128)} %get-tuple-element.210), channel_id=1, source_target_pairs={{0,8},{2,10},{4,12},{6,14},{8,0},{10,2},{12,4},{14,6},{16,24},{18,... | collective-permute-start | bytes 1769480 | tf_op jit(solution)/shard_map/ppermute | solution.py:663
  187.6 28.4 %copy-start.8 = (f32[1024,768]{1,0:T(8,128)S(1)}, f32[1024,768]{1,0:T(8,128)}, u32[]{:S(2)}) copy-start(f32[1024,768]{1,0:T(8,128)} %get-tuple-element.148) | copy-start | bytes 9437188
  187.7 31.3 %copy-start.43 = (f32[1,768]{1,0:T(1,128)S(1)}, f32[1,768]{1,0:T(1,128)}, u32[]{:S(2)}) copy-start(f32[1,768]{1,0:T(1,128)} %get-tuple-element.165) | copy-start | bytes 9220
  187.7 31.9 %copy-start.36 = (f32[1,1536]{1,0:T(1,128)S(1)}, f32[1,1536]{1,0:T(1,128)}, u32[]{:S(2)}) copy-start(f32[1,1536]{1,0:T(1,128)} %get-tuple-element.164) | copy-start | bytes 18436
  198.4 15.5 %collective-permute-start.19 = (f32[2,48,768]{2,1,0:T(8,128)}, f32[2,48,768]{2,1,0:T(8,128)}, u32[]{:S(2)}, u32[]{:S(2)}) collective-permute-start(f32[2,48,768]{2,1,0:T(8,128)} %add_add_fusion.2), channel_id=1, source_target_pairs={{0,16},{2,18},{4,20},{6,22},{8,24},{10,26},{12,28},{14,30},{16,0},... | collective-permute-start | bytes 884744 | tf_op jit(solution)/shard_map/ppermute | solution.py:663
  216.0 45.2 %collective-permute-start.23 = (f32[1024,768]{1,0:T(8,128)S(1)}, f32[1024,768]{1,0:T(8,128)}, u32[]{:S(2)}, u32[]{:S(2)}) collective-permute-start(f32[1024,768]{1,0:T(8,128)S(1)} %copy-done.8), channel_id=1, source_target_pairs={{0,1},{1,0},{2,3},{3,2},{4,5},{5,4},{6,7},{7,6},{8,9},{9,8},{10,11... | collective-permute-start | bytes 9437192 | tf_op jit(solution)/shard_map/ppermute | solution.py:658
  216.0 37.1 %collective-permute-start.20 = (f32[8,128,384]{2,1,0:T(8,128)}, f32[8,128,384]{2,1,0:T(8,128)}, u32[]{:S(2)}, u32[]{:S(2)}) collective-permute-start(f32[8,128,384]{2,1,0:T(8,128)} %pad_maximum_fusion.2), channel_id=1, source_target_pairs={{0,2},{2,0},{4,6},{6,4},{8,10},{10,8},{12,14},{14,12},{16,18},{18,... | collective-permute-start | bytes 4718600 | tf_op jit(solution)/shard_map/ppermute | solution.py:663
  217.4 36.8 %collective-permute-start.21 = (f32[8,128,384]{2,1,0:T(8,128)}, f32[8,128,384]{2,1,0:T(8,128)}, u32[]{:S(2)}, u32[]{:S(2)}) collective-permute-start(f32[8,128,384]{2,1,0:T(8,128)} %pad_maximum_fusion.3), channel_id=1, source_target_pairs={{0,4},{2,6},{4,0},{6,2},{8,12},{10,14},{12,8},{14,10},{16,20},{18,... | collective-permute-start | bytes 4718600 | tf_op jit(solution)/shard_map/ppermute | solution.py:663
  235.7 24.5 %collective-permute-start.22 = (f32[2,48,768]{2,1,0:T(8,128)S(1)}, f32[2,48,768]{2,1,0:T(8,128)S(1)}, u32[]{:S(2)}, u32[]{:S(2)}) collective-permute-start(f32[2,48,768]{2,1,0:T(8,128)S(1)} %copy-done.26), channel_id=1, source_target_pairs={{0,16},{2,18},{4,20},{6,22},{8,24},{10,26},{12,28},{14,30},{16,0},... | collective-permute-start | bytes 884744 | tf_op jit(solution)/shard_map/ppermute | solution.py:663
  235.9 29.3 %collective-permute-start.24 = (f32[2,96,768]{2,1,0:T(8,128)S(1)}, f32[2,96,768]{2,1,0:T(8,128)S(1)}, u32[]{:S(2)}, u32[]{:S(2)}) collective-permute-start(f32[2,96,768]{2,1,0:T(8,128)S(1)} %copy-done.12), channel_id=1, source_target_pairs={{0,8},{2,10},{4,12},{6,14},{8,0},{10,2},{12,4},{14,6},{16,24},{18,... | collective-permute-start | bytes 1769480 | tf_op jit(solution)/shard_map/ppermute | solution.py:663
  255.8 20.5 %collective-permute-start.26 = (f32[8,64,384]{2,1,0:T(8,128)S(1)}, f32[8,64,384]{2,1,0:T(8,128)S(1)}, u32[]{:S(2)}, u32[]{:S(2)}) collective-permute-start(f32[8,64,384]{2,1,0:T(8,128)S(1)} %get-tuple-element.206), channel_id=1, source_target_pairs={{0,2},{2,0},{4,6},{6,4},{8,10},{10,8},{12,14},{14,12},{16,18},{18,... | collective-permute-start | bytes 2359304 | tf_op jit(solution)/shard_map/ppermute | solution.py:663
  258.4 20.5 %collective-permute-start.25 = (f32[8,64,384]{2,1,0:T(8,128)S(1)}, f32[8,64,384]{2,1,0:T(8,128)S(1)}, u32[]{:S(2)}, u32[]{:S(2)}) collective-permute-start(f32[8,64,384]{2,1,0:T(8,128)S(1)} %get-tuple-element.208), channel_id=1, source_target_pairs={{0,4},{2,6},{4,0},{6,2},{8,12},{10,14},{12,8},{14,10},{16,20},{18,... | collective-permute-start | bytes 2359304 | tf_op jit(solution)/shard_map/ppermute | solution.py:663
  266.6 24.3 %collective-permute-start.29 = (f32[1,192,768]{2,1,0:T(8,128)}, f32[1,192,768]{2,1,0:T(8,128)S(1)}, u32[]{:S(2)}, u32[]{:S(2)}) collective-permute-start(f32[1,192,768]{2,1,0:T(8,128)} %get-tuple-element.233), channel_id=1, source_target_pairs={{0,2},{2,0},{4,6},{6,4},{8,10},{10,8},{12,14},{14,12},{16,18},{18,... | collective-permute-start | bytes 1769480 | tf_op jit(solution)/shard_map/ppermute | solution.py:663
  267.7 23.1 %collective-permute-start.28 = (f32[1,192,768]{2,1,0:T(8,128)}, f32[1,192,768]{2,1,0:T(8,128)S(1)}, u32[]{:S(2)}, u32[]{:S(2)}) collective-permute-start(f32[1,192,768]{2,1,0:T(8,128)} %get-tuple-element.234), channel_id=1, source_target_pairs={{0,4},{2,6},{4,0},{6,2},{8,12},{10,14},{12,8},{14,10},{16,20},{18,... | collective-permute-start | bytes 1769480 | tf_op jit(solution)/shard_map/ppermute | solution.py:663
  280.1 22.6 %collective-permute-start.31 = (f32[16,32,384]{2,1,0:T(8,128)}, f32[16,32,384]{2,1,0:T(8,128)}, u32[]{:S(2)}, u32[]{:S(2)}) collective-permute-start(f32[16,32,384]{2,1,0:T(8,128)} %get-tuple-element.204), channel_id=1, source_target_pairs={{0,8},{2,10},{4,12},{6,14},{8,0},{10,2},{12,4},{14,6},{16,24},{18,... | collective-permute-start | bytes 2359304 | tf_op jit(solution)/shard_map/ppermute | solution.py:663
  280.4 8.0 %collective-permute-start.27 = (f32[96,128]{1,0:T(8,128)}, f32[96,128]{1,0:T(8,128)S(1)}, u32[]{:S(2)}, u32[]{:S(2)}) collective-permute-start(f32[96,128]{1,0:T(8,128)} %pad_bitcast_fusion), channel_id=1, source_target_pairs={{0,2},{2,0},{4,6},{6,4},{8,10},{10,8},{12,14},{14,12},{16,18},{18,... | collective-permute-start | bytes 147464 | tf_op jit(solution)/shard_map/ppermute | solution.py:663
  281.7 24.2 %collective-permute-start.32 = (f32[2,48,768]{2,1,0:T(8,128)S(1)}, f32[2,48,768]{2,1,0:T(8,128)S(1)}, u32[]{:S(2)}, u32[]{:S(2)}) collective-permute-start(f32[2,48,768]{2,1,0:T(8,128)S(1)} %add_add_fusion.1), channel_id=1, source_target_pairs={{0,16},{2,18},{4,20},{6,22},{8,24},{10,26},{12,28},{14,30},{16,0},... | collective-permute-start | bytes 884744 | tf_op jit(solution)/shard_map/ppermute | solution.py:663
  289.2 6.4 %collective-permute-start.30 = (f32[96,128]{1,0:T(8,128)S(1)}, f32[96,128]{1,0:T(8,128)S(1)}, u32[]{:S(2)}, u32[]{:S(2)}) collective-permute-start(f32[96,128]{1,0:T(8,128)S(1)} %add.339), channel_id=1, source_target_pairs={{0,4},{2,6},{4,0},{6,2},{8,12},{10,14},{12,8},{14,10},{16,20},{18,... | collective-permute-start | bytes 147464 | tf_op jit(solution)/shard_map/ppermute | solution.py:663
  304.5 18.2 %collective-permute-start.33 = (f32[16,16,384]{2,1,0:T(8,128)}, f32[16,16,384]{2,1,0:T(8,128)}, u32[]{:S(2)}, u32[]{:S(2)}) collective-permute-start(f32[16,16,384]{2,1,0:T(8,128)} %dynamic-slice_add_fusion.4), channel_id=1, source_target_pairs={{0,16},{2,18},{4,20},{6,22},{8,24},{10,26},{12,28},{14,30},{16,0},... | collective-permute-start | bytes 1179656 | tf_op jit(solution)/shard_map/ppermute | solution.py:663
  306.8 22.0 %collective-permute-start.35 = (f32[2,96,768]{2,1,0:T(8,128)}, f32[2,96,768]{2,1,0:T(8,128)}, u32[]{:S(2)}, u32[]{:S(2)}) collective-permute-start(f32[2,96,768]{2,1,0:T(8,128)} %maximum_select_fusion.25), channel_id=1, source_target_pairs={{0,8},{2,10},{4,12},{6,14},{8,0},{10,2},{12,4},{14,6},{16,24},{18,... | collective-permute-start | bytes 1769480 | tf_op jit(solution)/shard_map/ppermute | solution.py:663
  309.3 28.6 %collective-permute-start.37 = (f32[1,384,768]{2,1,0:T(8,128)}, f32[1,384,768]{2,1,0:T(8,128)}, u32[]{:S(2)}, u32[]{:S(2)}) collective-permute-start(f32[1,384,768]{2,1,0:T(8,128)} %maximum_select_fusion.9), channel_id=1, source_target_pairs={{0,4},{2,6},{4,0},{6,2},{8,12},{10,14},{12,8},{14,10},{16,20},{18,... | collective-permute-start | bytes 3538952 | tf_op jit(solution)/shard_map/ppermute | solution.py:663
  310.7 29.2 %collective-permute-start.36 = (f32[1,384,768]{2,1,0:T(8,128)}, f32[1,384,768]{2,1,0:T(8,128)}, u32[]{:S(2)}, u32[]{:S(2)}) collective-permute-start(f32[1,384,768]{2,1,0:T(8,128)} %maximum_select_fusion.8), channel_id=1, source_target_pairs={{0,2},{2,0},{4,6},{6,4},{8,10},{10,8},{12,14},{14,12},{16,18},{18,... | collective-permute-start | bytes 3538952 | tf_op jit(solution)/shard_map/ppermute | solution.py:663
  311.9 16.9 %collective-permute-start.34 = (f32[96,128]{1,0:T(8,128)S(1)}, f32[96,128]{1,0:T(8,128)S(1)}, u32[]{:S(2)}, u32[]{:S(2)}) collective-permute-start(f32[96,128]{1,0:T(8,128)S(1)} %add.340), channel_id=1, source_target_pairs={{0,8},{2,10},{4,12},{6,14},{8,0},{10,2},{12,4},{14,6},{16,24},{18,... | collective-permute-start | bytes 147464 | tf_op jit(solution)/shard_map/ppermute | solution.py:663
  330.7 18.2 %collective-permute-start.39 = (f32[1,192,768]{2,1,0:T(8,128)S(1)}, f32[1,192,768]{2,1,0:T(8,128)S(1)}, u32[]{:S(2)}, u32[]{:S(2)}) collective-permute-start(f32[1,192,768]{2,1,0:T(8,128)S(1)} %get-tuple-element.237), channel_id=1, source_target_pairs={{0,2},{2,0},{4,6},{6,4},{8,10},{10,8},{12,14},{14,12},{16,18},{18,... | collective-permute-start | bytes 1769480 | tf_op jit(solution)/shard_map/ppermute | solution.py:663
  332.2 16.7 %collective-permute-start.38 = (f32[1,192,768]{2,1,0:T(8,128)S(1)}, f32[1,192,768]{2,1,0:T(8,128)S(1)}, u32[]{:S(2)}, u32[]{:S(2)}) collective-permute-start(f32[1,192,768]{2,1,0:T(8,128)S(1)} %get-tuple-element.238), channel_id=1, source_target_pairs={{0,4},{2,6},{4,0},{6,2},{8,12},{10,14},{12,8},{14,10},{16,20},{18,... | collective-permute-start | bytes 1769480 | tf_op jit(solution)/shard_map/ppermute | solution.py:663
  334.2 42.9 %collective-permute-start.42 = (f32[96,128]{1,0:T(8,128)S(1)}, f32[96,128]{1,0:T(8,128)S(1)}, u32[]{:S(2)}, u32[]{:S(2)}) collective-permute-start(f32[96,128]{1,0:T(8,128)S(1)} %add.345), channel_id=1, source_target_pairs={{0,16},{2,18},{4,20},{6,22},{8,24},{10,26},{12,28},{14,30},{16,0},... | collective-permute-start | bytes 147464 | tf_op jit(solution)/shard_map/ppermute | solution.py:663
  337.8 16.3 %collective-permute-start.40 = (f32[16,16,384]{2,1,0:T(8,128)S(1)}, f32[16,16,384]{2,1,0:T(8,128)S(1)}, u32[]{:S(2)}, u32[]{:S(2)}) collective-permute-start(f32[16,16,384]{2,1,0:T(8,128)S(1)} %add_add_fusion), channel_id=1, source_target_pairs={{0,16},{2,18},{4,20},{6,22},{8,24},{10,26},{12,28},{14,30},{16,0},... | collective-permute-start | bytes 1179656 | tf_op jit(solution)/shard_map/ppermute | solution.py:663
  354.2 17.3 %collective-permute-start.41 = (f32[16,32,384]{2,1,0:T(8,128)S(1)}, f32[16,32,384]{2,1,0:T(8,128)S(1)}, u32[]{:S(2)}, u32[]{:S(2)}) collective-permute-start(f32[16,32,384]{2,1,0:T(8,128)S(1)} %maximum_select_fusion.21), channel_id=1, source_target_pairs={{0,8},{2,10},{4,12},{6,14},{8,0},{10,2},{12,4},{14,6},{16,24},{18,... | collective-permute-start | bytes 2359304 | tf_op jit(solution)/shard_map/ppermute | solution.py:663
  358.6 53.3 %collective-permute-start.46 = (f32[1,384,768]{2,1,0:T(8,128)}, f32[1,384,768]{2,1,0:T(8,128)}, u32[]{:S(2)}, u32[]{:S(2)}) collective-permute-start(f32[1,384,768]{2,1,0:T(8,128)} %maximum_select_fusion.12), channel_id=1, source_target_pairs={{0,4},{2,6},{4,0},{6,2},{8,12},{10,14},{12,8},{14,10},{16,20},{18,... | collective-permute-start | bytes 3538952 | tf_op jit(solution)/shard_map/ppermute | solution.py:663
  359.5 52.4 %collective-permute-start.45 = (f32[1,384,768]{2,1,0:T(8,128)}, f32[1,384,768]{2,1,0:T(8,128)}, u32[]{:S(2)}, u32[]{:S(2)}) collective-permute-start(f32[1,384,768]{2,1,0:T(8,128)} %maximum_select_fusion.11), channel_id=1, source_target_pairs={{0,2},{2,0},{4,6},{6,4},{8,10},{10,8},{12,14},{14,12},{16,18},{18,... | collective-permute-start | bytes 3538952 | tf_op jit(solution)/shard_map/ppermute | solution.py:663
  371.7 8.7 %copy-start.3 = (bf16[1024,512]{1,0:T(8,128)(2,1)S(1)}, bf16[1024,512]{1,0:T(8,128)(2,1)}, u32[]{:S(2)}) copy-start(bf16[1024,512]{1,0:T(8,128)(2,1)} %features_ref.1) | copy-start | bytes 3145732
  371.7 8.7 %copy-start.29 = (f32[1,512]{1,0:T(1,128)S(1)}, f32[1,512]{1,0:T(1,128)}, u32[]{:S(2)}) copy-start(f32[1,512]{1,0:T(1,128)} %copy-done.28) | copy-start | bytes 6148
  373.0 30.7 %collective-permute-start.44 = (f32[8,64,384]{2,1,0:T(8,128)}, f32[8,64,384]{2,1,0:T(8,128)}, u32[]{:S(2)}, u32[]{:S(2)}) collective-permute-start(f32[8,64,384]{2,1,0:T(8,128)} %get-tuple-element.229), channel_id=1, source_target_pairs={{0,2},{2,0},{4,6},{6,4},{8,10},{10,8},{12,14},{14,12},{16,18},{18,... | collective-permute-start | bytes 2359304 | tf_op jit(solution)/shard_map/ppermute | solution.py:663
  375.8 27.8 %collective-permute-start.43 = (f32[8,64,384]{2,1,0:T(8,128)}, f32[8,64,384]{2,1,0:T(8,128)}, u32[]{:S(2)}, u32[]{:S(2)}) collective-permute-start(f32[8,64,384]{2,1,0:T(8,128)} %get-tuple-element.230), channel_id=1, source_target_pairs={{0,4},{2,6},{4,0},{6,2},{8,12},{10,14},{12,8},{14,10},{16,20},{18,... | collective-permute-start | bytes 2359304 | tf_op jit(solution)/shard_map/ppermute | solution.py:663
  405.7 34.6 %collective-permute-start.48 = (f32[8,128,384]{2,1,0:T(8,128)S(1)}, f32[8,128,384]{2,1,0:T(8,128)S(1)}, u32[]{:S(2)}, u32[]{:S(2)}) collective-permute-start(f32[8,128,384]{2,1,0:T(8,128)S(1)} %maximum_select_fusion.6), channel_id=1, source_target_pairs={{0,4},{2,6},{4,0},{6,2},{8,12},{10,14},{12,8},{14,10},{16,20},{18,... | collective-permute-start | bytes 4718600 | tf_op jit(solution)/shard_map/ppermute | solution.py:663
  408.8 34.1 %collective-permute-start.47 = (f32[8,128,384]{2,1,0:T(8,128)S(1)}, f32[8,128,384]{2,1,0:T(8,128)S(1)}, u32[]{:S(2)}, u32[]{:S(2)}) collective-permute-start(f32[8,128,384]{2,1,0:T(8,128)S(1)} %maximum_select_fusion.5), channel_id=1, source_target_pairs={{0,2},{2,0},{4,6},{6,4},{8,10},{10,8},{12,14},{14,12},{16,18},{18,... | collective-permute-start | bytes 4718600 | tf_op jit(solution)/shard_map/ppermute | solution.py:663
  (43 other events, 142.7 us)

commit v4 on v3

--- a/solution.py
+++ b/solution.py
@@ -20,15 +20,16 @@
 SCHEDULE = " ".join(
     (
         "R a R E",
-        "h b R E",
-        "i R H E",
-        "R E R w",
-        "H E o s",
-        "R H s R",
-        "s H E H",
-        "s E R E",
-        "H H p H",
-        "E H",
+        "h b i R",
+        "E H R s",
+        "E R R w",
+        "E H H s",
+        "R E H s",
+        "R H o s",
+        "s E R R",
+        "H E H E",
+        "H p E H",
+        "H",
     )
 )
 
@@ -239,28 +240,15 @@
     )
 
 
-def error_function(values):
-    limited = jnp.clip(values, -3.7439211, 3.7439211)
-    square = limited * limited
-    top = jnp.full_like(square, 2.2905065861350646e-4)
-    for factor in (
-        3.4082910107109506e-3,
-        5.0955695062380861e-2,
-        1.8520832239976145e-1,
-        1.128379143519084,
-    ):
-        top = top * square + factor
-    bottom = jnp.full_like(square, -1.1791602954361697e-7)
-    for factor in (
-        2.3547966471313185e-5,
-        1.0179625278914885e-3,
-        1.4070470171167667e-2,
-        1.1098505178285362e-1,
-        4.9746925110067538e-1,
-        1.0,
-    ):
-        bottom = bottom * square + factor
-    return limited * top / bottom
+def gelu_terms(values):
+    power = jnp.exp(values * values * -0.5)
+    inverse = 1.0 / (1.0 + jnp.abs(values) * 0.23164189)
+    tail = 0.5307027
+    for factor in (-0.7265760, 0.7107069, -0.14224836, 0.12741479):
+        tail = tail * inverse + factor
+    tail = tail * inverse * power
+    cumulative = jnp.where(values < 0.0, tail, 1.0 - tail)
+    return cumulative, cumulative + values * power * 0.3989422804014327
 
 
 def feed_kernel(
@@ -303,10 +291,8 @@
     for at in range(0, hidden_units, part):
         span = slice(at, at + part)
         expanded = mult(second, expand_ref[:, span]) + expand_bias_ref[:, span]
-        cumulative = 0.5 + 0.5 * error_function(expanded * 0.7071067811865476)
+        cumulative, slope = gelu_terms(expanded)
         active = (expanded * cumulative).astype(jnp.bfloat16)
-        density = jnp.exp(expanded * expanded * -0.5) * 0.3989422804014327
-        slope = cumulative + expanded * density
         active_ref[:, span] = active
         grad_active = mult(grad_reduced, reduce_ref[span, :], RIGHT)
         grad_expanded = (grad_active * slope).astype(jnp.bfloat16)
@@ -763,20 +749,6 @@
     side, mine, other = entry
     whole_rows = spread(side, mine[start:stop], other[start:stop])
     return whole_rows.reshape(-1, whole_rows.shape[2])
-
-
-def pack(arrays):
-    flat = jnp.concatenate([entry.reshape(-1) for entry in arrays])
-    short = -flat.shape[0] % 1024
-    return jnp.pad(flat, (0, short)).reshape(-1, 128)
-
-
-def unpack(packed, arrays):
-    flat, at, parts = packed.reshape(-1), 0, []
-    for entry in arrays:
-        parts.append(flat[at : at + entry.size].reshape(entry.shape))
-        at += entry.size
-    return parts
 
 
 def local(
@@ -972,11 +944,10 @@
         bit = state.setdefault("bit", 0)
         if bit == 0:
             attend_sums, stem_sums = state["attend"][4:], state["stem"][3:]
-            heads_total = jnp.sum(attend_sums[3].reshape(heads, HEAD_DIM), axis=1)
-            table = attend_sums[5][:, : distance_table.shape[1]]
-            state["small"] = (*attend_sums[:3], heads_total, attend_sums[4], table, *stem_sums)
-            state["small"] += (grad_expand_bias, grad_reduce_bias)
-            (packed,) = chain.enter(pack(state["small"]))
+            table = [attend_sums[5][head : head + 1] for head in range(heads)]
+            state["small"] = (*attend_sums[:5], *stem_sums, grad_expand_bias, grad_reduce_bias)
+            state["small"] += tuple(table)
+            (packed,) = chain.enter(jnp.concatenate(state["small"], axis=1))
         else:
             packed, moved = chain.enter(state["packed"], state["moved"])
             packed = packed + moved
@@ -998,8 +969,12 @@
     def run_patch():
         while state["bit"] <= lax.axis_size("dp").bit_length() - 1:
             small_step()
-        state["small"] = unpack(state["packed"], state["small"])
-        stem_gain_sum, stem_shift_sum = state["small"][8:10]
+        at, parts = 0, []
+        for entry in state["small"]:
+            parts.append(state["packed"][:, at : at + entry.shape[1]])
+            at += entry.shape[1]
+        state["small"] = parts
+        stem_gain_sum, stem_shift_sum = state["small"][7:9]
         (feature,) = chain.enter(patch_features)
         hat = (feature.astype(jnp.float32) - stem_mean) * stem_inverse
         patch_grad = (
@@ -1051,16 +1026,18 @@
         grad_second_gain,
         grad_second_shift,
         grad_merge_bias,
-        grad_head_gain,
+        head_sums,
         heads_sums,
-        grad_distance_table,
         grad_first_gain,
         grad_first_shift,
         grad_stem_gain,
         grad_stem_shift,
         grad_expand_bias,
         grad_reduce_bias,
+        *table,
     ) = state["small"]
+    grad_head_gain = jnp.sum(head_sums.reshape(heads, HEAD_DIM), axis=1)
+    grad_distance_table = jnp.concatenate(table, axis=0)[:, : distance_table.shape[1]]
     block_output, input_grad, patch_grad = state["output"], state["stem"][0], state["patch"]
     return (
         block_output,

time: 455 us -> 435 us (0.956)
  other arithmetic: 84.7 us -> 61.8 us
  Pallas kernels: 74.1 us -> 80.8 us
  starting transfers between devices: 63.4 us -> 56.8 us
    pallas_call x9 -> x0, other arithmetic: 9.63 us -> none  [the longest x5 5.84 us: attend_back(): pl.pallas_call(attend_back_kernel, grid_spec=pltpu.PrefetchScalarGridSpec...]
    pallas_call x1, Pallas kernels: 10.3 us -> 19.7 us  [stem_back(): pl.pallas_call(stem_back_kernel, grid_spec=pltpu.PrefetchScalarGridSpec(n...]
    ppermute x44, starting transfers between devices: 62.9 us -> 56.3 us  [exchange(): lax.ppermute(values, 'dp', [(rank, rank ^ 1 << bit) for rank in range(cou...]
    select_n x26, other arithmetic: 27.8 us -> 23 us  [spread(): jnp.where(side == 1, jnp.concatenate([other, mine], axis=1), jnp.concaten...]
    unnamed x118 -> x170, local copies, waits for them, and re-layouts: 11.5 us -> 15.8 us
    add x7 -> x9, other arithmetic: 10.6 us -> 10.4 us  [step(): cut(mine, 1 - side) + cut(other, 1 - side)]
  transfers between devices with their start and end apart: 49 -> 49, of which waited for: 27 -> 26; matrix products, arithmetic and copies ran while one was open for 26% -> 22% of each run, Pallas kernels for 8% -> 11%
where the time goes in v4:
time: 435 us; the launch traced here: 429 us
  waiting for transfers between devices  171 us (39%)
  Pallas kernels  80.8 us (19%)
  other arithmetic  61.8 us (14%)
  starting transfers between devices  56.8 us (13%)
  local copies, waits for them, and re-layouts  33.3 us (8%)
  matrix products  23.5 us (5%)
    ppermute x44, waiting for transfers between devices, exchange(): lax.ppermute(values, 'dp', [(rank, rank ^ 1 << bit) for rank in range(cou...  168 us
    ppermute x44, starting transfers between devices, exchange(): lax.ppermute(values, 'dp', [(rank, rank ^ 1 << bit) for rank in range(cou...  56.3 us
    pallas_call x1, Pallas kernels, attend_back(): pl.pallas_call(attend_back_kernel, grid_spec=pltpu.PrefetchScalarGridSpec...  23.7 us
    dot_general x16, matrix products, mult(): lax.dot_general(left, right, (dims, ((), ())), preferred_element_type=jnp...  23.5 us
    select_n x26, other arithmetic, spread(): jnp.where(side == 1, jnp.concatenate([other, mine], axis=1), jnp.concaten...  23 us
    pallas_call x1, Pallas kernels, feed(): pl.pallas_call(feed_kernel, grid_spec=pltpu.PrefetchScalarGridSpec(num_sc...  20.2 us
    pallas_call x1, Pallas kernels, stem_back(): pl.pallas_call(stem_back_kernel, grid_spec=pltpu.PrefetchScalarGridSpec(n...  19.7 us
    unnamed x170, local copies, waits for them, and re-layouts  15.8 us
  transfers between devices with their start and end apart: 49, of which 26 were waited for; matrix products, arithmetic and copies ran while one was open for 22% of the time, Pallas kernels for 11%

profile of v4, /device:TPU:0, one launch (start us, length us, event | category | flops | bytes accessed | tf_op | source)
XLA Modules:
  0.0 429.2 jit_solution(13841647077104150215)
XLA Ops:
  3.4 1.7 fusion
  5.2 3.0 collective-permute-start
  8.2 1.6 collective-permute-done
  9.9 2.1 collective-permute-start.1
  12.0 1.6 collective-permute-done.1
  13.7 2.1 collective-permute-start.2
  15.7 1.6 collective-permute-done.2
  17.4 3.0 collective-permute-start.3
  20.4 1.6 collective-permute-done.3
  27.9 1.9 constant_dynamic-update-slice_fusion.2
  31.6 2.3 distance_bias.1.bias_ref
  34.0 14.9 %attend.1 = (f32[1024,768]{1,0:T(8,128)}, bf16[1024,768]{1,0:T(8,128)(2,1)}, bf16[1024,1152]{1,0:T(8,128)(2,1)}, f32[4,6,256,256]{3,2,1,0:T(8,128)}, f32[1024,38...) custom-call(s32[4]{0:T(128)} %copy-done.62, s32[4]{0:T(128)} %get-tuple-element.271.valid_ref, ...), custom_call_target="tpu_custom_call" | custom-call | flops 15000000512 | bytes 45000000 | tf_op jit(solution)/shard_map/attend/pallas_call | solution.py:189
  51.5 3.4 collective-permute-done.5.other_ref
  54.8 1.7 copy-done.66
  56.5 20.2 %feed.1 = (f32[1024,768]{1,0:T(8,128)}, bf16[1024,768]{1,0:T(8,128)(2,1)}, bf16[1024,1536]{1,0:T(8,128)(2,1)}, bf16[1024,1536]{1,0:T(8,128)(2,1)}, f32[1024,768]...) custom-call(s32[4]{0:T(128)} %get-tuple-element.271.valid_ref, ...), custom_call_target="tpu_custom_call" | custom-call | flops 23000000512 | bytes 69000000 | tf_op jit(solution)/shard_map/feed/pallas_call | solution.py:331
  76.9 3.6 convolution_bitcast_fusion.3
  80.5 1.9 collective-permute-start.7
  82.4 3.0 convolution_bitcast_fusion.2
  88.5 23.7 %attend_back.1 = (f32[1024,768]{1,0:T(8,128)}, bf16[1024,768]{1,0:T(8,128)(2,1)}, bf16[1024,1152]{1,0:T(8,128)(2,1)}, f32[1024,768]{1,0:T(8,128)}, f32[1,768]{1,...) custom-call(f32[1024,768]{1,0:T(8,128)} %get-tuple-element.112.middl, ...), custom_call_target="tpu_custom_call" | custom-call | flops 24000000000 | bytes 72000000 | tf_op jit(solution)/shard_map/attend_back/pallas_call | solution.py:492
  113.6 2.5 bitcast_add_fusion.4
  117.7 1.7 collective-permute-start.10
  119.5 1.8 convolution_bitcast_fusion
  121.3 1.9 convolution_bitcast_fusion.1
  133.5 1.8 fusion.6
  135.3 1.8 fusion.9
  137.2 1.6 copy-done.65
  138.8 19.7 %stem_back.1 = (f32[1024,768]{1,0:T(8,128)}, bf16[1024,768]{1,0:T(8,128)(2,1)}, f32[1024,512]{1,0:T(8,128)}, f32[1,768]{1,0:T(1,128)}, f32[1,768]{1,0:T(1,128)}, /*index=5*/f32[1,512]{1,0:T(1,128)}, f32[1,512]{1,0:T(1,128)}) custom-call(s32[4]{0:T(128)} %copy-done.62, f32[1024,768]{1,0:T(8,128)} %get-tuple-element.110.hidden_ref, ...), custom_call_target="tpu_custom_call" | custom-call | flops 10000000000 | bytes 30000000 | tf_op jit(solution)/shard_map/stem_back/pallas_call | solution.py:602
  158.6 2.0 fusion.18
  174.4 2.9 collective-permute-done.12
  177.4 2.8 collective-permute-start.17
  180.1 3.4 collective-permute-done.16
  183.5 2.2 collective-permute-done.15
  186.8 4.1 collective-permute-done.17
  191.3 14.9 %collective-permute-done.18 = f32[2,48,768]{2,1,0:T(8,128)S(1)} collective-permute-done((f32[2,48,768]{2,1,0:T(8,128)S(1)}, f32[2,48,768]{2,1,0:T(8,128)S(1)}, u32[]{:S(2)}, u32[]{:S(2)}) %collective-permute-start.18) | collective-permute-done | bytes 294944 | tf_op jit(solution)/shard_map/ppermute | solution.py:649
  207.5 6.6 %collective-permute-done.20 = f32[8,128,384]{2,1,0:T(8,128)S(1)} collective-permute-done((f32[8,128,384]{2,1,0:T(8,128)S(1)}, f32[8,128,384]{2,1,0:T(8,128)S(1)}, u32[]{:S(2)}, u32[]{:S(2)}) %collective-permute-start.20) | collective-permute-done | bytes 1572896 | tf_op jit(solution)/shard_map/ppermute | solution.py:649
  214.1 2.4 collective-permute-done.21
  222.1 11.4 %collective-permute-done.22 = f32[8,64,384]{2,1,0:T(8,128)} collective-permute-done((f32[8,64,384]{2,1,0:T(8,128)S(1)}, f32[8,64,384]{2,1,0:T(8,128)}, u32[]{:S(2)}, u32[]{:S(2)}) %collective-permute-start.22) | collective-permute-done | bytes 786464 | tf_op jit(solution)/shard_map/ppermute | solution.py:649
  233.5 2.7 collective-permute-start.26
  246.7 1.9 add_add_fusion.1
  248.6 11.5 %collective-permute-done.27 = f32[16,32,384]{2,1,0:T(8,128)} collective-permute-done((f32[16,32,384]{2,1,0:T(8,128)}, f32[16,32,384]{2,1,0:T(8,128)}, u32[]{:S(2)}, u32[]{:S(2)}) %collective-permute-start.27) | collective-permute-done | bytes 786464 | tf_op jit(solution)/shard_map/ppermute | solution.py:649
  260.1 1.8 dynamic-slice_add_fusion.4
  264.7 2.6 maximum_select_fusion.9
  271.7 1.9 maximum_select_fusion.19
  273.6 13.3 %collective-permute-done.31 = f32[16,16,384]{2,1,0:T(8,128)S(1)} collective-permute-done((f32[16,16,384]{2,1,0:T(8,128)}, f32[16,16,384]{2,1,0:T(8,128)S(1)}, u32[]{:S(2)}, u32[]{:S(2)}) %collective-permute-start.31) | collective-permute-done | bytes 393248 | tf_op jit(solution)/shard_map/ppermute | solution.py:649
  288.9 4.9 %add_convert_fusion = bf16[1024,768]{1,0:T(8,128)(2,1)} fusion(f32[1024,768]{1,0:T(8,128)S(1)} %copy-done.6, f32[1024,768]{1,0:T(8,128)} %get-tuple-element.160, f32[1024,768]{1,0:T(8,128)} %collective-permute-done.32, f32[768]{0:T(1024)S(1)} %copy-done.46), kind=kLoop, calls=%fused_computation.2 | loop fusion | flops 3145728 | bytes 11013120 | tf_op jit(solution)/shard_map/convert_element_type | solution.py:966
  294.0 2.2 collective-permute-start.34
  299.2 1.9 maximum_select_fusion.25
  301.2 1.9 collective-permute-start.39
  304.3 13.1 %collective-permute-done.38 = f32[16,16,384]{2,1,0:T(8,128)S(1)} collective-permute-done((f32[16,16,384]{2,1,0:T(8,128)S(1)}, f32[16,16,384]{2,1,0:T(8,128)S(1)}, u32[]{:S(2)}, u32[]{:S(2)}) %collective-permute-start.38) | collective-permute-done | bytes 393248 | tf_op jit(solution)/shard_map/ppermute | solution.py:649
  319.0 2.9 maximum_select_fusion.3
  323.3 1.9 maximum_select_fusion.2
  325.2 2.5 pad_maximum_fusion.1
  327.7 1.8 maximum_select_fusion.10
  330.2 2.0 collective-permute-start.41
  332.2 8.6 %collective-permute-done.40 = f32[16,32,384]{2,1,0:T(8,128)} collective-permute-done((f32[16,32,384]{2,1,0:T(8,128)}, f32[16,32,384]{2,1,0:T(8,128)}, u32[]{:S(2)}, u32[]{:S(2)}) %collective-permute-start.40) | collective-permute-done | bytes 786464 | tf_op jit(solution)/shard_map/ppermute | solution.py:649
  340.7 2.0 maximum_select_fusion.4
  343.1 1.9 collective-permute-start.43
  346.5 2.0 collective-permute-start.46
  349.0 14.4 %collective-permute-done.44 = f32[8,64,384]{2,1,0:T(8,128)S(1)} collective-permute-done((f32[8,64,384]{2,1,0:T(8,128)S(1)}, f32[8,64,384]{2,1,0:T(8,128)S(1)}, u32[]{:S(2)}, u32[]{:S(2)}) %collective-permute-start.44) | collective-permute-done | bytes 786464 | tf_op jit(solution)/shard_map/ppermute | solution.py:649
  363.7 2.0 collective-permute-start.48
  368.0 2.0 subtract_multiply_fusion
  370.1 18.8 %collective-permute-done.46 = f32[1,384,768]{2,1,0:T(8,128)S(1)} collective-permute-done((f32[1,384,768]{2,1,0:T(8,128)S(1)}, f32[1,384,768]{2,1,0:T(8,128)S(1)}, u32[]{:S(2)}, u32[]{:S(2)}) %collective-permute-start.46) | collective-permute-done | bytes 1179680 | tf_op jit(solution)/shard_map/ppermute | solution.py:649
  389.3 2.9 pad_maximum_fusion
  392.2 29.0 %collective-permute-done.48 = f32[8,128,384]{2,1,0:T(8,128)S(1)} collective-permute-done((f32[8,128,384]{2,1,0:T(8,128)S(1)}, f32[8,128,384]{2,1,0:T(8,128)S(1)}, u32[]{:S(2)}, u32[]{:S(2)}) %collective-permute-start.48) | collective-permute-done | bytes 1572896 | tf_op jit(solution)/shard_map/ppermute | solution.py:649
  (335 shorter events, 92.2 us)
Async XLA Ops:
  0.7 21.4 %copy-start.2 = (bf16[1024,512]{1,0:T(8,128)(2,1)S(1)}, bf16[1024,512]{1,0:T(8,128)(2,1)}, u32[]{:S(2)}) copy-start(bf16[1024,512]{1,0:T(8,128)(2,1)} %features_ref.1) | copy-start | bytes 3145732
  1.9 21.3 %copy-start.62 = (s32[4]{0:T(128)}, s32[4]{0:T(128)S(1)}, u32[]{:S(2)}) copy-start(s32[4]{0:T(128)S(1)} %get-tuple-element.270.patches_ref) | copy-start | bytes 52
  3.4 19.8 %copy-start.21 = (bf16[512,768]{1,0:T(8,128)(2,1)S(1)}, bf16[512,768]{1,0:T(8,128)(2,1)}, u32[]{:S(2)}) copy-start(bf16[512,768]{1,0:T(8,128)(2,1)} %image_ref.1) | copy-start | bytes 2359300
  5.2 4.6 %collective-permute-start = (f32[3,512]{1,0:T(4,128)S(1)}, f32[3,512]{1,0:T(4,128)S(1)}, u32[]{:S(2)}, u32[]{:S(2)}) collective-permute-start(f32[3,512]{1,0:T(4,128)S(1)} %maximum_maximum_fusion), channel_id=1, source_target_pairs={{0,2},{2,0},{4,6},{6,4},{8,10},{10,8},{12,14},{14,12},{16,18},{18,... | collective-permute-start | bytes 18440 | tf_op jit(solution)/shard_map/ppermute | solution.py:649
  9.9 3.7 collective-permute-start.1
  13.7 3.7 collective-permute-start.2
  17.4 4.7 %collective-permute-start.3 = (f32[3,512]{1,0:T(4,128)S(1)}, f32[3,512]{1,0:T(4,128)S(1)}, u32[]{:S(2)}, u32[]{:S(2)}) collective-permute-start(f32[3,512]{1,0:T(4,128)S(1)} %add.276), channel_id=1, source_target_pairs={{0,16},{2,18},{4,20},{6,22},{8,24},{10,26},{12,28},{14,30},{16,0},... | collective-permute-start | bytes 18440 | tf_op jit(solution)/shard_map/ppermute | solution.py:649
  24.3 9.6 %collective-permute-start.4 = (f32[1024,768]{1,0:T(8,128)S(1)}, f32[1024,768]{1,0:T(8,128)}, u32[]{:S(2)}, u32[]{:S(2)}) collective-permute-start(f32[1024,768]{1,0:T(8,128)S(1)} %fusion.66.own_ref), channel_id=1, source_target_pairs={{0,1},{1,0},{2,3},{3,2},{4,5},{5,4},{6,7},{7,6},{8,9},{9,8},{10,11... | collective-permute-start | bytes 9437192 | tf_op jit(solution)/shard_map/ppermute | solution.py:644
  33.9 15.2 %copy-start.49 = (f32[768]{0:T(1024)S(1)}, f32[768]{0:T(1024)}, u32[]{:S(2)}) copy-start(f32[768]{0:T(1024)} %param.41) | copy-start | bytes 9220
  33.9 15.7 %copy-start.50 = (f32[768]{0:T(1024)S(1)}, f32[768]{0:T(1024)}, u32[]{:S(2)}) copy-start(f32[768]{0:T(1024)} %param.36) | copy-start | bytes 9220
  34.0 16.3 %copy-start.51 = (f32[768]{0:T(1024)S(1)}, f32[768]{0:T(1024)}, u32[]{:S(2)}) copy-start(f32[768]{0:T(1024)} %param.42) | copy-start | bytes 9220
  34.0 16.9 %copy-start.43 = (f32[1536]{0:T(1024)S(1)}, f32[1536]{0:T(1024)}, u32[]{:S(2)}) copy-start(f32[1536]{0:T(1024)} %param.44) | copy-start | bytes 18436
  48.9 5.9 %collective-permute-start.5 = (f32[1024,768]{1,0:T(8,128)}, f32[1024,768]{1,0:T(8,128)S(1)}, u32[]{:S(2)}, u32[]{:S(2)}) collective-permute-start(f32[1024,768]{1,0:T(8,128)} %get-tuple-element.111.own_ref), channel_id=1, source_target_pairs={{0,1},{1,0},{2,3},{3,2},{4,5},{5,4},{6,7},{7,6},{8,9},{9,8},{10,11... | collective-permute-start | bytes 9437192 | tf_op jit(solution)/shard_map/ppermute | solution.py:644
  76.7 11.8 %collective-permute-start.6 = (f32[1024,768]{1,0:T(8,128)}, f32[1024,768]{1,0:T(8,128)}, u32[]{:S(2)}, u32[]{:S(2)}) collective-permute-start(f32[1024,768]{1,0:T(8,128)} %get-tuple-element.115.own_ref), channel_id=1, source_target_pairs={{0,1},{1,0},{2,3},{3,2},{4,5},{5,4},{6,7},{7,6},{8,9},{9,8},{10,11... | collective-permute-start | bytes 9437192 | tf_op jit(solution)/shard_map/ppermute | solution.py:644
  80.5 31.8 %collective-permute-start.7 = (f32[1,384,768]{2,1,0:T(8,128)}, f32[1,384,768]{2,1,0:T(8,128)S(1)}, u32[]{:S(2)}, u32[]{:S(2)}) collective-permute-start(f32[1,384,768]{2,1,0:T(8,128)} %convolution_bitcast_fusion.3), channel_id=1, source_target_pairs={{0,2},{2,0},{4,6},{6,4},{8,10},{10,8},{12,14},{14,12},{16,18},{18,... | collective-permute-start | bytes 3538952 | tf_op jit(solution)/shard_map/ppermute | solution.py:649
  85.3 28.3 %collective-permute-start.8 = (f32[1,384,768]{2,1,0:T(8,128)}, f32[1,384,768]{2,1,0:T(8,128)}, u32[]{:S(2)}, u32[]{:S(2)}) collective-permute-start(f32[1,384,768]{2,1,0:T(8,128)} %convolution_bitcast_fusion.2), channel_id=1, source_target_pairs={{0,4},{2,6},{4,0},{6,2},{8,12},{10,14},{12,8},{14,10},{16,20},{18,... | collective-permute-start | bytes 3538952 | tf_op jit(solution)/shard_map/ppermute | solution.py:649
  112.2 25.0 %collective-permute-start.9 = (f32[1024,768]{1,0:T(8,128)}, f32[1024,768]{1,0:T(8,128)S(1)}, u32[]{:S(2)}, u32[]{:S(2)}) collective-permute-start(f32[1024,768]{1,0:T(8,128)} %get-tuple-element.120.own_ref), channel_id=1, source_target_pairs={{0,1},{1,0},{2,3},{3,2},{4,5},{5,4},{6,7},{7,6},{8,9},{9,8},{10,11... | collective-permute-start | bytes 9437192 | tf_op jit(solution)/shard_map/ppermute | solution.py:644
  116.1 45.2 %collective-permute-start.11 = (f32[1,192,768]{2,1,0:T(8,128)}, f32[1,192,768]{2,1,0:T(8,128)}, u32[]{:S(2)}, u32[]{:S(2)}) collective-permute-start(f32[1,192,768]{2,1,0:T(8,128)} %get-tuple-element.224), channel_id=1, source_target_pairs={{0,2},{2,0},{4,6},{6,4},{8,10},{10,8},{12,14},{14,12},{16,18},{18,... | collective-permute-start | bytes 1769480 | tf_op jit(solution)/shard_map/ppermute | solution.py:649
  117.7 43.6 %collective-permute-start.10 = (f32[1,192,768]{2,1,0:T(8,128)}, f32[1,192,768]{2,1,0:T(8,128)}, u32[]{:S(2)}, u32[]{:S(2)}) collective-permute-start(f32[1,192,768]{2,1,0:T(8,128)} %get-tuple-element.226), channel_id=1, source_target_pairs={{0,4},{2,6},{4,0},{6,2},{8,12},{10,14},{12,8},{14,10},{16,20},{18,... | collective-permute-start | bytes 1769480 | tf_op jit(solution)/shard_map/ppermute | solution.py:649
  123.2 42.5 %collective-permute-start.13 = (f32[1,384,768]{2,1,0:T(8,128)}, f32[1,384,768]{2,1,0:T(8,128)}, u32[]{:S(2)}, u32[]{:S(2)}) collective-permute-start(f32[1,384,768]{2,1,0:T(8,128)} %convolution_bitcast_fusion.1), channel_id=1, source_target_pairs={{0,2},{2,0},{4,6},{6,4},{8,10},{10,8},{12,14},{14,12},{16,18},{18,... | collective-permute-start | bytes 3538952 | tf_op jit(solution)/shard_map/ppermute | solution.py:649
  124.5 41.2 %collective-permute-start.14 = (f32[1,384,768]{2,1,0:T(8,128)}, f32[1,384,768]{2,1,0:T(8,128)}, u32[]{:S(2)}, u32[]{:S(2)}) collective-permute-start(f32[1,384,768]{2,1,0:T(8,128)} %convolution_bitcast_fusion), channel_id=1, source_target_pairs={{0,4},{2,6},{4,0},{6,2},{8,12},{10,14},{12,8},{14,10},{16,20},{18,... | collective-permute-start | bytes 3538952 | tf_op jit(solution)/shard_map/ppermute | solution.py:649
  138.8 19.7 %copy-start.5 = (bf16[1024,512]{1,0:T(8,128)(2,1)S(1)}, bf16[1024,512]{1,0:T(8,128)(2,1)}, u32[]{:S(2)}) copy-start(bf16[1024,512]{1,0:T(8,128)(2,1)} %copy-done.4) | copy-start | bytes 3145732
  163.9 13.4 %collective-permute-start.12 = (f32[2,96,768]{2,1,0:T(8,128)S(1)}, f32[2,96,768]{2,1,0:T(8,128)S(1)}, u32[]{:S(2)}, u32[]{:S(2)}) collective-permute-start(f32[2,96,768]{2,1,0:T(8,128)S(1)} %get-tuple-element.223), channel_id=1, source_target_pairs={{0,8},{2,10},{4,12},{6,14},{8,0},{10,2},{12,4},{14,6},{16,24},{18,... | collective-permute-start | bytes 1769480 | tf_op jit(solution)/shard_map/ppermute | solution.py:649
  167.2 16.3 %collective-permute-start.16 = (f32[1,192,768]{2,1,0:T(8,128)S(1)}, f32[1,192,768]{2,1,0:T(8,128)S(1)}, u32[]{:S(2)}, u32[]{:S(2)}) collective-permute-start(f32[1,192,768]{2,1,0:T(8,128)S(1)} %get-tuple-element.218), channel_id=1, source_target_pairs={{0,2},{2,0},{4,6},{6,4},{8,10},{10,8},{12,14},{14,12},{16,18},{18,... | collective-permute-start | bytes 1769480 | tf_op jit(solution)/shard_map/ppermute | solution.py:649
  169.4 16.3 %collective-permute-start.15 = (f32[1,192,768]{2,1,0:T(8,128)S(1)}, f32[1,192,768]{2,1,0:T(8,128)S(1)}, u32[]{:S(2)}, u32[]{:S(2)}) collective-permute-start(f32[1,192,768]{2,1,0:T(8,128)S(1)} %get-tuple-element.220), channel_id=1, source_target_pairs={{0,4},{2,6},{4,0},{6,2},{8,12},{10,14},{12,8},{14,10},{16,20},{18,... | collective-permute-start | bytes 1769480 | tf_op jit(solution)/shard_map/ppermute | solution.py:649
  172.4 41.7 %collective-permute-start.20 = (f32[8,128,384]{2,1,0:T(8,128)S(1)}, f32[8,128,384]{2,1,0:T(8,128)S(1)}, u32[]{:S(2)}, u32[]{:S(2)}) collective-permute-start(f32[8,128,384]{2,1,0:T(8,128)S(1)} %pad_maximum_fusion.2), channel_id=1, source_target_pairs={{0,2},{2,0},{4,6},{6,4},{8,10},{10,8},{12,14},{14,12},{16,18},{18,... | collective-permute-start | bytes 4718600 | tf_op jit(solution)/shard_map/ppermute | solution.py:649
  173.9 42.6 %collective-permute-start.21 = (f32[8,128,384]{2,1,0:T(8,128)S(1)}, f32[8,128,384]{2,1,0:T(8,128)S(1)}, u32[]{:S(2)}, u32[]{:S(2)}) collective-permute-start(f32[8,128,384]{2,1,0:T(8,128)S(1)} %pad_maximum_fusion.3), channel_id=1, source_target_pairs={{0,4},{2,6},{4,0},{6,2},{8,12},{10,14},{12,8},{14,10},{16,20},{18,... | collective-permute-start | bytes 4718600 | tf_op jit(solution)/shard_map/ppermute | solution.py:649
  174.4 11.3 %copy-start.29 = (f32[1,11776]{1,0:T(1,128)}, f32[1,11776]{1,0:T(1,128)S(1)}, u32[]{:S(2)}) copy-start(f32[1,11776]{1,0:T(1,128)S(1)} %constant_dynamic-update-slice_fusion.5) | copy-start | bytes 141316
  177.4 13.6 %collective-permute-start.17 = (f32[2,48,768]{2,1,0:T(8,128)S(1)}, f32[2,48,768]{2,1,0:T(8,128)S(1)}, u32[]{:S(2)}, u32[]{:S(2)}) collective-permute-start(f32[2,48,768]{2,1,0:T(8,128)S(1)} %dynamic-slice_add_fusion.6), channel_id=1, source_target_pairs={{0,16},{2,18},{4,20},{6,22},{8,24},{10,26},{12,28},{14,30},{16,0},... | collective-permute-start | bytes 884744 | tf_op jit(solution)/shard_map/ppermute | solution.py:649
  186.0 21.5 %copy-start.13 = (f32[2,96,768]{2,1,0:T(8,128)}, f32[2,96,768]{2,1,0:T(8,128)S(1)}, u32[]{:S(2)}) copy-start(f32[2,96,768]{2,1,0:T(8,128)S(1)} %get-tuple-element.216) | copy-start | bytes 1769476
  186.0 20.7 %collective-permute-start.19 = (f32[2,96,768]{2,1,0:T(8,128)S(1)}, f32[2,96,768]{2,1,0:T(8,128)S(1)}, u32[]{:S(2)}, u32[]{:S(2)}) collective-permute-start(f32[2,96,768]{2,1,0:T(8,128)S(1)} %get-tuple-element.217), channel_id=1, source_target_pairs={{0,8},{2,10},{4,12},{6,14},{8,0},{10,2},{12,4},{14,6},{16,24},{18,... | collective-permute-start | bytes 1769480 | tf_op jit(solution)/shard_map/ppermute | solution.py:649
  191.0 15.2 %collective-permute-start.18 = (f32[2,48,768]{2,1,0:T(8,128)S(1)}, f32[2,48,768]{2,1,0:T(8,128)S(1)}, u32[]{:S(2)}, u32[]{:S(2)}) collective-permute-start(f32[2,48,768]{2,1,0:T(8,128)S(1)} %add_add_fusion.2), channel_id=1, source_target_pairs={{0,16},{2,18},{4,20},{6,22},{8,24},{10,26},{12,28},{14,30},{16,0},... | collective-permute-start | bytes 884744 | tf_op jit(solution)/shard_map/ppermute | solution.py:649
  206.7 10.0 %copy-start.24 = (f32[2,96,768]{2,1,0:T(8,128)}, f32[2,96,768]{2,1,0:T(8,128)S(1)}, u32[]{:S(2)}) copy-start(f32[2,96,768]{2,1,0:T(8,128)S(1)} %collective-permute-done.19) | copy-start | bytes 1769476
  206.7 82.2 %collective-permute-start.32 = (f32[1024,768]{1,0:T(8,128)}, f32[1024,768]{1,0:T(8,128)}, u32[]{:S(2)}, u32[]{:S(2)}) collective-permute-start(f32[1024,768]{1,0:T(8,128)} %get-tuple-element.160), channel_id=1, source_target_pairs={{0,1},{1,0},{2,3},{3,2},{4,5},{5,4},{6,7},{7,6},{8,9},{9,8},{10,11... | collective-permute-start | bytes 9437192 | tf_op jit(solution)/shard_map/ppermute | solution.py:644
  216.7 16.8 %collective-permute-start.22 = (f32[8,64,384]{2,1,0:T(8,128)S(1)}, f32[8,64,384]{2,1,0:T(8,128)}, u32[]{:S(2)}, u32[]{:S(2)}) collective-permute-start(f32[8,64,384]{2,1,0:T(8,128)S(1)} %get-tuple-element.214), channel_id=1, source_target_pairs={{0,4},{2,6},{4,0},{6,2},{8,12},{10,14},{12,8},{14,10},{16,20},{18,... | collective-permute-start | bytes 2359304 | tf_op jit(solution)/shard_map/ppermute | solution.py:649
  219.3 16.9 %collective-permute-start.23 = (f32[8,64,384]{2,1,0:T(8,128)}, f32[8,64,384]{2,1,0:T(8,128)}, u32[]{:S(2)}, u32[]{:S(2)}) collective-permute-start(f32[8,64,384]{2,1,0:T(8,128)} %get-tuple-element.212), channel_id=1, source_target_pairs={{0,2},{2,0},{4,6},{6,4},{8,10},{10,8},{12,14},{14,12},{16,18},{18,... | collective-permute-start | bytes 2359304 | tf_op jit(solution)/shard_map/ppermute | solution.py:649
  220.6 21.1 %collective-permute-start.25 = (f32[2,96,768]{2,1,0:T(8,128)S(1)}, f32[2,96,768]{2,1,0:T(8,128)S(1)}, u32[]{:S(2)}, u32[]{:S(2)}) collective-permute-start(f32[2,96,768]{2,1,0:T(8,128)S(1)} %maximum_select_fusion.24), channel_id=1, source_target_pairs={{0,8},{2,10},{4,12},{6,14},{8,0},{10,2},{12,4},{14,6},{16,24},{18,... | collective-permute-start | bytes 1769480 | tf_op jit(solution)/shard_map/ppermute | solution.py:649
  221.3 19.7 %collective-permute-start.24 = (f32[1,11776]{1,0:T(1,128)}, f32[1,11776]{1,0:T(1,128)S(1)}, u32[]{:S(2)}, u32[]{:S(2)}) collective-permute-start(f32[1,11776]{1,0:T(1,128)} %copy-done.29), channel_id=1, source_target_pairs={{0,2},{2,0},{4,6},{6,4},{8,10},{10,8},{12,14},{14,12},{16,18},{18,... | collective-permute-start | bytes 141320 | tf_op jit(solution)/shard_map/ppermute | solution.py:649
  233.5 12.8 %collective-permute-start.26 = (f32[2,48,768]{2,1,0:T(8,128)}, f32[2,48,768]{2,1,0:T(8,128)}, u32[]{:S(2)}, u32[]{:S(2)}) collective-permute-start(f32[2,48,768]{2,1,0:T(8,128)} %dynamic-slice_add_fusion.5), channel_id=1, source_target_pairs={{0,16},{2,18},{4,20},{6,22},{8,24},{10,26},{12,28},{14,30},{16,0},... | collective-permute-start | bytes 884744 | tf_op jit(solution)/shard_map/ppermute | solution.py:649
  239.7 20.3 %collective-permute-start.27 = (f32[16,32,384]{2,1,0:T(8,128)}, f32[16,32,384]{2,1,0:T(8,128)}, u32[]{:S(2)}, u32[]{:S(2)}) collective-permute-start(f32[16,32,384]{2,1,0:T(8,128)} %get-tuple-element.211), channel_id=1, source_target_pairs={{0,8},{2,10},{4,12},{6,14},{8,0},{10,2},{12,4},{14,6},{16,24},{18,... | collective-permute-start | bytes 2359304 | tf_op jit(solution)/shard_map/ppermute | solution.py:649
  243.0 21.6 %collective-permute-start.30 = (f32[1,192,768]{2,1,0:T(8,128)}, f32[1,192,768]{2,1,0:T(8,128)S(1)}, u32[]{:S(2)}, u32[]{:S(2)}) collective-permute-start(f32[1,192,768]{2,1,0:T(8,128)} %get-tuple-element.240), channel_id=1, source_target_pairs={{0,2},{2,0},{4,6},{6,4},{8,10},{10,8},{12,14},{14,12},{16,18},{18,... | collective-permute-start | bytes 1769480 | tf_op jit(solution)/shard_map/ppermute | solution.py:649
  243.7 21.0 %collective-permute-start.29 = (f32[1,192,768]{2,1,0:T(8,128)S(1)}, f32[1,192,768]{2,1,0:T(8,128)S(1)}, u32[]{:S(2)}, u32[]{:S(2)}) collective-permute-start(f32[1,192,768]{2,1,0:T(8,128)S(1)} %get-tuple-element.241), channel_id=1, source_target_pairs={{0,4},{2,6},{4,0},{6,2},{8,12},{10,14},{12,8},{14,10},{16,20},{18,... | collective-permute-start | bytes 1769480 | tf_op jit(solution)/shard_map/ppermute | solution.py:649
  246.4 16.8 %collective-permute-start.28 = (f32[1,11776]{1,0:T(1,128)}, f32[1,11776]{1,0:T(1,128)S(1)}, u32[]{:S(2)}, u32[]{:S(2)}) collective-permute-start(f32[1,11776]{1,0:T(1,128)} %add.332), channel_id=1, source_target_pairs={{0,4},{2,6},{4,0},{6,2},{8,12},{10,14},{12,8},{14,10},{16,20},{18,... | collective-permute-start | bytes 141320 | tf_op jit(solution)/shard_map/ppermute | solution.py:649
  261.9 25.1 %collective-permute-start.31 = (f32[16,16,384]{2,1,0:T(8,128)}, f32[16,16,384]{2,1,0:T(8,128)S(1)}, u32[]{:S(2)}, u32[]{:S(2)}) collective-permute-start(f32[16,16,384]{2,1,0:T(8,128)} %dynamic-slice_add_fusion.4), channel_id=1, source_target_pairs={{0,16},{2,18},{4,20},{6,22},{8,24},{10,26},{12,28},{14,30},{16,0},... | collective-permute-start | bytes 1179656 | tf_op jit(solution)/shard_map/ppermute | solution.py:649
  267.2 35.8 %collective-permute-start.37 = (f32[1,384,768]{2,1,0:T(8,128)}, f32[1,384,768]{2,1,0:T(8,128)}, u32[]{:S(2)}, u32[]{:S(2)}) collective-permute-start(f32[1,384,768]{2,1,0:T(8,128)} %maximum_select_fusion.9), channel_id=1, source_target_pairs={{0,4},{2,6},{4,0},{6,2},{8,12},{10,14},{12,8},{14,10},{16,20},{18,... | collective-permute-start | bytes 3538952 | tf_op jit(solution)/shard_map/ppermute | solution.py:649
  268.7 34.3 %collective-permute-start.36 = (f32[1,384,768]{2,1,0:T(8,128)}, f32[1,384,768]{2,1,0:T(8,128)}, u32[]{:S(2)}, u32[]{:S(2)}) collective-permute-start(f32[1,384,768]{2,1,0:T(8,128)} %maximum_select_fusion.8), channel_id=1, source_target_pairs={{0,2},{2,0},{4,6},{6,4},{8,10},{10,8},{12,14},{14,12},{16,18},{18,... | collective-permute-start | bytes 3538952 | tf_op jit(solution)/shard_map/ppermute | solution.py:649
  270.2 29.0 %collective-permute-start.35 = (f32[2,48,768]{2,1,0:T(8,128)}, f32[2,48,768]{2,1,0:T(8,128)S(1)}, u32[]{:S(2)}, u32[]{:S(2)}) collective-permute-start(f32[2,48,768]{2,1,0:T(8,128)} %add_add_fusion.1), channel_id=1, source_target_pairs={{0,16},{2,18},{4,20},{6,22},{8,24},{10,26},{12,28},{14,30},{16,0},... | collective-permute-start | bytes 884744 | tf_op jit(solution)/shard_map/ppermute | solution.py:649
  271.7 17.2 %copy-start.6 = (f32[1024,768]{1,0:T(8,128)S(1)}, f32[1024,768]{1,0:T(8,128)}, u32[]{:S(2)}) copy-start(f32[1024,768]{1,0:T(8,128)} %get-tuple-element.112.middle_ref) | copy-start | bytes 9437188
  271.7 17.2 %copy-start.46 = (f32[768]{0:T(1024)S(1)}, f32[768]{0:T(1024)}, u32[]{:S(2)}) copy-start(f32[768]{0:T(1024)} %param.46) | copy-start | bytes 9220
  287.7 6.2 %collective-permute-start.33 = (f32[1,11776]{1,0:T(1,128)}, f32[1,11776]{1,0:T(1,128)S(1)}, u32[]{:S(2)}, u32[]{:S(2)}) collective-permute-start(f32[1,11776]{1,0:T(1,128)} %add.337), channel_id=1, source_target_pairs={{0,8},{2,10},{4,12},{6,14},{8,0},{10,2},{12,4},{14,6},{16,24},{18,... | collective-permute-start | bytes 141320 | tf_op jit(solution)/shard_map/ppermute | solution.py:649
  294.0 5.2 %collective-permute-start.34 = (f32[1,11776]{1,0:T(1,128)S(1)}, f32[1,11776]{1,0:T(1,128)S(1)}, u32[]{:S(2)}, u32[]{:S(2)}) collective-permute-start(f32[1,11776]{1,0:T(1,128)S(1)} %add.343), channel_id=1, source_target_pairs={{0,16},{2,18},{4,20},{6,22},{8,24},{10,26},{12,28},{14,30},{16,0},... | collective-permute-start | bytes 141320 | tf_op jit(solution)/shard_map/ppermute | solution.py:649
  297.3 20.1 %collective-permute-start.38 = (f32[16,16,384]{2,1,0:T(8,128)S(1)}, f32[16,16,384]{2,1,0:T(8,128)S(1)}, u32[]{:S(2)}, u32[]{:S(2)}) collective-permute-start(f32[16,16,384]{2,1,0:T(8,128)S(1)} %add_add_fusion), channel_id=1, source_target_pairs={{0,16},{2,18},{4,20},{6,22},{8,24},{10,26},{12,28},{14,30},{16,0},... | collective-permute-start | bytes 1179656 | tf_op jit(solution)/shard_map/ppermute | solution.py:649
  299.2 19.8 %copy-start.27 = (f32[1,11776]{1,0:T(1,128)}, f32[1,11776]{1,0:T(1,128)S(1)}, u32[]{:S(2)}) copy-start(f32[1,11776]{1,0:T(1,128)S(1)} %add.344) | copy-start | bytes 141316
  301.2 26.5 %collective-permute-start.39 = (f32[2,96,768]{2,1,0:T(8,128)}, f32[2,96,768]{2,1,0:T(8,128)}, u32[]{:S(2)}, u32[]{:S(2)}) collective-permute-start(f32[2,96,768]{2,1,0:T(8,128)} %maximum_select_fusion.25), channel_id=1, source_target_pairs={{0,8},{2,10},{4,12},{6,14},{8,0},{10,2},{12,4},{14,6},{16,24},{18,... | collective-permute-start | bytes 1769480 | tf_op jit(solution)/shard_map/ppermute | solution.py:649
  304.3 62.0 %copy-start.37 = (f32[1,512]{1,0:T(1,128)}, f32[1,512]{1,0:T(1,128)S(1)}, u32[]{:S(2)}) copy-start(f32[1,512]{1,0:T(1,128)S(1)} %get-tuple-element.268) | copy-start | bytes 6148
  319.0 21.7 %collective-permute-start.40 = (f32[16,32,384]{2,1,0:T(8,128)}, f32[16,32,384]{2,1,0:T(8,128)}, u32[]{:S(2)}, u32[]{:S(2)}) collective-permute-start(f32[16,32,384]{2,1,0:T(8,128)} %maximum_select_fusion.21), channel_id=1, source_target_pairs={{0,8},{2,10},{4,12},{6,14},{8,0},{10,2},{12,4},{14,6},{16,24},{18,... | collective-permute-start | bytes 2359304 | tf_op jit(solution)/shard_map/ppermute | solution.py:649
  329.7 16.7 %collective-permute-start.42 = (f32[1,192,768]{2,1,0:T(8,128)S(1)}, f32[1,192,768]{2,1,0:T(8,128)S(1)}, u32[]{:S(2)}, u32[]{:S(2)}) collective-permute-start(f32[1,192,768]{2,1,0:T(8,128)S(1)} %get-tuple-element.244), channel_id=1, source_target_pairs={{0,2},{2,0},{4,6},{6,4},{8,10},{10,8},{12,14},{14,12},{16,18},{18,... | collective-permute-start | bytes 1769480 | tf_op jit(solution)/shard_map/ppermute | solution.py:649
  330.2 16.2 %collective-permute-start.41 = (f32[1,192,768]{2,1,0:T(8,128)S(1)}, f32[1,192,768]{2,1,0:T(8,128)S(1)}, u32[]{:S(2)}, u32[]{:S(2)}) collective-permute-start(f32[1,192,768]{2,1,0:T(8,128)S(1)} %get-tuple-element.245), channel_id=1, source_target_pairs={{0,4},{2,6},{4,0},{6,2},{8,12},{10,14},{12,8},{14,10},{16,20},{18,... | collective-permute-start | bytes 1769480 | tf_op jit(solution)/shard_map/ppermute | solution.py:649
  342.9 20.5 %collective-permute-start.44 = (f32[8,64,384]{2,1,0:T(8,128)S(1)}, f32[8,64,384]{2,1,0:T(8,128)S(1)}, u32[]{:S(2)}, u32[]{:S(2)}) collective-permute-start(f32[8,64,384]{2,1,0:T(8,128)S(1)} %get-tuple-element.236), channel_id=1, source_target_pairs={{0,2},{2,0},{4,6},{6,4},{8,10},{10,8},{12,14},{14,12},{16,18},{18,... | collective-permute-start | bytes 2359304 | tf_op jit(solution)/shard_map/ppermute | solution.py:649
  343.1 20.4 %collective-permute-start.43 = (f32[8,64,384]{2,1,0:T(8,128)S(1)}, f32[8,64,384]{2,1,0:T(8,128)S(1)}, u32[]{:S(2)}, u32[]{:S(2)}) collective-permute-start(f32[8,64,384]{2,1,0:T(8,128)S(1)} %get-tuple-element.237), channel_id=1, source_target_pairs={{0,4},{2,6},{4,0},{6,2},{8,12},{10,14},{12,8},{14,10},{16,20},{18,... | collective-permute-start | bytes 2359304 | tf_op jit(solution)/shard_map/ppermute | solution.py:649
  346.5 42.3 %collective-permute-start.46 = (f32[1,384,768]{2,1,0:T(8,128)S(1)}, f32[1,384,768]{2,1,0:T(8,128)S(1)}, u32[]{:S(2)}, u32[]{:S(2)}) collective-permute-start(f32[1,384,768]{2,1,0:T(8,128)S(1)} %maximum_select_fusion.12), channel_id=1, source_target_pairs={{0,4},{2,6},{4,0},{6,2},{8,12},{10,14},{12,8},{14,10},{16,20},{18,... | collective-permute-start | bytes 3538952 | tf_op jit(solution)/shard_map/ppermute | solution.py:649
  348.6 40.2 %collective-permute-start.45 = (f32[1,384,768]{2,1,0:T(8,128)S(1)}, f32[1,384,768]{2,1,0:T(8,128)S(1)}, u32[]{:S(2)}, u32[]{:S(2)}) collective-permute-start(f32[1,384,768]{2,1,0:T(8,128)S(1)} %maximum_select_fusion.11), channel_id=1, source_target_pairs={{0,2},{2,0},{4,6},{6,4},{8,10},{10,8},{12,14},{14,12},{16,18},{18,... | collective-permute-start | bytes 3538952 | tf_op jit(solution)/shard_map/ppermute | solution.py:649
  363.7 57.5 %collective-permute-start.48 = (f32[8,128,384]{2,1,0:T(8,128)S(1)}, f32[8,128,384]{2,1,0:T(8,128)S(1)}, u32[]{:S(2)}, u32[]{:S(2)}) collective-permute-start(f32[8,128,384]{2,1,0:T(8,128)S(1)} %maximum_select_fusion.6), channel_id=1, source_target_pairs={{0,4},{2,6},{4,0},{6,2},{8,12},{10,14},{12,8},{14,10},{16,20},{18,... | collective-permute-start | bytes 4718600 | tf_op jit(solution)/shard_map/ppermute | solution.py:649
  365.8 55.4 %collective-permute-start.47 = (f32[8,128,384]{2,1,0:T(8,128)S(1)}, f32[8,128,384]{2,1,0:T(8,128)S(1)}, u32[]{:S(2)}, u32[]{:S(2)}) collective-permute-start(f32[8,128,384]{2,1,0:T(8,128)S(1)} %maximum_select_fusion.5), channel_id=1, source_target_pairs={{0,2},{2,0},{4,6},{6,4},{8,10},{10,8},{12,14},{14,12},{16,18},{18,... | collective-permute-start | bytes 4718600 | tf_op jit(solution)/shard_map/ppermute | solution.py:649
  (61 other events, 156.1 us)

commit v5 on v4

--- a/solution.py
+++ b/solution.py
@@ -17,19 +17,19 @@
 FULL = ((1,), (0,))
 RIGHT = ((1,), (1,))
 LEFT = ((0,), (0,))
+PAIRED = (True, True, True)
 SCHEDULE = " ".join(
     (
         "R a R E",
-        "h b i R",
-        "E H R s",
-        "E R R w",
+        "h R b i",
+        "R E R s",
+        "E E R H",
+        "w H E R",
         "E H H s",
-        "R E H s",
-        "R H o s",
-        "s E R R",
-        "H E H E",
-        "H p E H",
-        "H",
+        "R E R H",
+        "s E H H",
+        "s E s p",
+        "H o E H",
     )
 )
 
@@ -690,11 +690,14 @@
 
 
 class Stream:
-    def __init__(self, chain):
+    def __init__(self, chain, paired):
         bits = lax.axis_size("dp").bit_length() - 1
         self.chain = chain
         self.rank = lax.axis_index("dp")
-        self.plan = ((0, 1), (1, 0)) + tuple((bit,) for bit in range(2, bits))
+        far = tuple((bit,) for bit in range(2, bits))
+        if paired:
+            far = tuple((bit, min(bit ^ 1, bits - 1)) for bit in range(2, bits))
+        self.plan = ((0, 1), (1, 0)) + far
         self.stage = 0
 
     def bits(self, stage):
@@ -846,7 +849,7 @@
         upstream,
     )
     chain = Chain()
-    reduces, expands, others = Stream(chain), Stream(chain), Stream(chain)
+    reduces, expands, others = (Stream(chain, paired) for paired in PAIRED)
     streams = {"R": reduces, "E": expands, "H": others}
     slot = 256
     state = {}

time: 435 us -> 408 us (0.938)
  waiting for transfers between devices: 171 us -> 118 us
  starting transfers between devices: 56.8 us -> 82.9 us
  local copies, waits for them, and re-layouts: 33.3 us -> 25.8 us
  other arithmetic: 61.8 us -> 68.8 us
    ppermute x44 -> x56, waiting for transfers between devices: 168 us -> 115 us  [exchange(): lax.ppermute(values, 'dp', [(rank, rank ^ 1 << bit) for rank in range(cou...]
    ppermute x44 -> x56, starting transfers between devices: 56.3 us -> 82.3 us  [exchange(): lax.ppermute(values, 'dp', [(rank, rank ^ 1 << bit) for rank in range(cou...]
    add x3 -> x12, other arithmetic: 1.45 us -> 8.53 us  [step(): cut(mine, side) + cut(other, side)]
    select_n x26 -> x40, other arithmetic: 23 us -> 29.5 us  [spread(): jnp.where(side == 1, jnp.concatenate([other, mine], axis=1), jnp.concaten...]
    add x9 -> x6, other arithmetic: 10.4 us -> 5.18 us  [step(): cut(mine, 1 - side) + cut(other, 1 - side)]
    unnamed x170 -> x161, local copies, waits for them, and re-layouts: 15.8 us -> 12.8 us
  transfers between devices with their start and end apart: 49 -> 61, of which waited for: 26 -> 25; matrix products, arithmetic and copies ran while one was open for 22% -> 23% of each run, Pallas kernels for 11% -> 11%
where the time goes in v5:
time: 408 us; the launch traced here: 403 us
  waiting for transfers between devices  118 us (29%)
  starting transfers between devices  82.9 us (20%)
  Pallas kernels  80.9 us (20%)
  other arithmetic  68.8 us (17%)
  local copies, waits for them, and re-layouts  25.8 us (6%)
  matrix products  24.5 us (6%)
    ppermute x56, waiting for transfers between devices, exchange(): lax.ppermute(values, 'dp', [(rank, rank ^ 1 << bit) for rank in range(cou...  115 us
    ppermute x56, starting transfers between devices, exchange(): lax.ppermute(values, 'dp', [(rank, rank ^ 1 << bit) for rank in range(cou...  82.3 us
    select_n x40, other arithmetic, spread(): jnp.where(side == 1, jnp.concatenate([other, mine], axis=1), jnp.concaten...  29.5 us
    dot_general x16, matrix products, mult(): lax.dot_general(left, right, (dims, ((), ())), preferred_element_type=jnp...  24.5 us
    pallas_call x1, Pallas kernels, attend_back(): pl.pallas_call(attend_back_kernel, grid_spec=pltpu.PrefetchScalarGridSpec...  23.6 us
    pallas_call x1, Pallas kernels, feed(): pl.pallas_call(feed_kernel, grid_spec=pltpu.PrefetchScalarGridSpec(num_sc...  20.2 us
    pallas_call x1, Pallas kernels, stem_back(): pl.pallas_call(stem_back_kernel, grid_spec=pltpu.PrefetchScalarGridSpec(n...  19.8 us
    pallas_call x1, Pallas kernels, attend(): pl.pallas_call(attend_kernel, grid_spec=pltpu.PrefetchScalarGridSpec(num_...  14.9 us
  transfers between devices with their start and end apart: 61, of which 25 were waited for; matrix products, arithmetic and copies ran while one was open for 23% of the time, Pallas kernels for 11%

profile of v5, /device:TPU:0, one launch (start us, length us, event | category | flops | bytes accessed | tf_op | source)
XLA Modules:
  0.0 403.4 jit_solution(502537510490393942)
XLA Ops:
  3.4 1.7 fusion
  5.2 3.0 collective-permute-start
  9.9 2.1 collective-permute-start.1
  13.7 2.1 collective-permute-start.2
  17.4 3.0 collective-permute-start.3
  27.9 1.9 constant_dynamic-update-slice_fusion.2
  31.6 2.3 distance_bias.1.bias_ref
  34.0 14.9 %attend.1 = (f32[1024,768]{1,0:T(8,128)}, bf16[1024,768]{1,0:T(8,128)(2,1)}, bf16[1024,1152]{1,0:T(8,128)(2,1)}, f32[4,6,256,256]{3,2,1,0:T(8,128)}, f32[1024,38...) custom-call(s32[4]{0:T(128)} %copy-done.59, s32[4]{0:T(128)} %get-tuple-element.291.valid_ref, ...), custom_call_target="tpu_custom_call" | custom-call | flops 15000000512 | bytes 45000000 | tf_op jit(solution)/shard_map/attend/pallas_call | solution.py:189
  51.5 3.4 collective-permute-done.5.other_ref
  56.5 20.2 %feed.1 = (f32[1024,768]{1,0:T(8,128)}, bf16[1024,768]{1,0:T(8,128)(2,1)}, bf16[1024,1536]{1,0:T(8,128)(2,1)}, bf16[1024,1536]{1,0:T(8,128)(2,1)}, f32[1024,768]...) custom-call(s32[4]{0:T(128)} %get-tuple-element.291.valid_ref, ...), custom_call_target="tpu_custom_call" | custom-call | flops 23000000512 | bytes 69000000 | tf_op jit(solution)/shard_map/feed/pallas_call | solution.py:331
  76.9 3.6 convolution_bitcast_fusion.3
  80.5 1.9 collective-permute-start.7
  82.4 3.0 convolution_bitcast_fusion.2
  86.8 1.8 fusion.30
  89.5 23.6 %attend_back.1 = (f32[1024,768]{1,0:T(8,128)}, bf16[1024,768]{1,0:T(8,128)(2,1)}, bf16[1024,1152]{1,0:T(8,128)(2,1)}, f32[1024,768]{1,0:T(8,128)}, f32[1,768]{1,...) custom-call(f32[1024,768]{1,0:T(8,128)} %get-tuple-element.124.middl, ...), custom_call_target="tpu_custom_call" | custom-call | flops 24000000000 | bytes 72000000 | tf_op jit(solution)/shard_map/attend_back/pallas_call | solution.py:492
  115.8 1.8 collective-permute-start.9
  117.6 1.9 convolution_bitcast_fusion
  119.5 1.9 convolution_bitcast_fusion.1
  131.7 1.8 fusion.6
  133.5 1.8 fusion.9
  136.3 2.5 collective-permute-start.15
  143.0 19.8 %stem_back.1 = (f32[1024,768]{1,0:T(8,128)}, bf16[1024,768]{1,0:T(8,128)(2,1)}, f32[1024,512]{1,0:T(8,128)}, f32[1,768]{1,0:T(1,128)}, f32[1,768]{1,0:T(1,128)}, /*index=5*/f32[1,512]{1,0:T(1,128)}, f32[1,512]{1,0:T(1,128)}) custom-call(s32[4]{0:T(128)} %copy-done.59, f32[1024,768]{1,0:T(8,128)} %get-tuple-element.122.hidden_ref, ...), custom_call_target="tpu_custom_call" | custom-call | flops 10000000000 | bytes 30000000 | tf_op jit(solution)/shard_map/stem_back/pallas_call | solution.py:602
  162.8 2.0 fusion.14
  179.6 7.0 %collective-permute-done.21 = f32[1,192,768]{2,1,0:T(8,128)S(1)} collective-permute-done((f32[1,192,768]{2,1,0:T(8,128)S(1)}, f32[1,192,768]{2,1,0:T(8,128)S(1)}, u32[]{:S(2)}, u32[]{:S(2)}) %collective-permute-start.21) | collective-permute-done | bytes 589856 | tf_op jit(solution)/shard_map/ppermute | solution.py:649
  186.6 2.6 collective-permute-done.20
  189.3 2.6 collective-permute-start.23
  194.2 7.6 %collective-permute-done.23 = f32[1,96,768]{2,1,0:T(8,128)S(1)} collective-permute-done((f32[1,96,768]{2,1,0:T(8,128)S(1)}, f32[1,96,768]{2,1,0:T(8,128)S(1)}, u32[]{:S(2)}, u32[]{:S(2)}) %collective-permute-start.23) | collective-permute-done | bytes 294944 | tf_op jit(solution)/shard_map/ppermute | solution.py:649
  201.9 2.0 collective-permute-start.27
  203.9 4.7 %collective-permute-done.22 = f32[1,96,768]{2,1,0:T(8,128)S(1)} collective-permute-done((f32[1,96,768]{2,1,0:T(8,128)S(1)}, f32[1,96,768]{2,1,0:T(8,128)S(1)}, u32[]{:S(2)}, u32[]{:S(2)}) %collective-permute-start.22) | collective-permute-done | bytes 294944 | tf_op jit(solution)/shard_map/ppermute | solution.py:649
  208.7 2.7 collective-permute-start.24
  212.8 4.4 %collective-permute-done.12 = f32[8,128,384]{2,1,0:T(8,128)S(1)} collective-permute-done((f32[8,128,384]{2,1,0:T(8,128)S(1)}, f32[8,128,384]{2,1,0:T(8,128)S(1)}, u32[]{:S(2)}, u32[]{:S(2)}) %collective-permute-start.12) | collective-permute-done | bytes 1572896 | tf_op jit(solution)/shard_map/ppermute | solution.py:649
  217.2 2.5 collective-permute-start.29
  222.6 2.9 collective-permute-start.30
  225.6 1.7 collective-permute-start.31
  227.3 8.0 %collective-permute-done.29 = f32[1,96,768]{2,1,0:T(8,128)S(1)} collective-permute-done((f32[1,96,768]{2,1,0:T(8,128)S(1)}, f32[1,96,768]{2,1,0:T(8,128)S(1)}, u32[]{:S(2)}, u32[]{:S(2)}) %collective-permute-start.29) | collective-permute-done | bytes 294944 | tf_op jit(solution)/shard_map/ppermute | solution.py:649
  240.8 3.4 collective-permute-start.35
  244.6 1.8 collective-permute-start.38
  247.8 8.7 %collective-permute-done.34 = f32[8,32,384]{2,1,0:T(8,128)} collective-permute-done((f32[8,32,384]{2,1,0:T(8,128)}, f32[8,32,384]{2,1,0:T(8,128)}, u32[]{:S(2)}, u32[]{:S(2)}) %collective-permute-start.34) | collective-permute-done | bytes 393248 | tf_op jit(solution)/shard_map/ppermute | solution.py:649
  256.5 5.1 %collective-permute-done.35 = f32[8,32,384]{2,1,0:T(8,128)} collective-permute-done((f32[8,32,384]{2,1,0:T(8,128)}, f32[8,32,384]{2,1,0:T(8,128)}, u32[]{:S(2)}, u32[]{:S(2)}) %collective-permute-start.35) | collective-permute-done | bytes 393248 | tf_op jit(solution)/shard_map/ppermute | solution.py:649
  267.2 2.0 collective-permute-start.41
  269.2 2.9 collective-permute-start.40
  274.3 9.6 %collective-permute-done.39 = f32[1,96,768]{2,1,0:T(8,128)} collective-permute-done((f32[1,96,768]{2,1,0:T(8,128)}, f32[1,96,768]{2,1,0:T(8,128)}, u32[]{:S(2)}, u32[]{:S(2)}) %collective-permute-start.39) | collective-permute-done | bytes 294944 | tf_op jit(solution)/shard_map/ppermute | solution.py:649
  288.4 4.1 %collective-permute-done.42 = f32[1,384,768]{2,1,0:T(8,128)} collective-permute-done((f32[1,384,768]{2,1,0:T(8,128)}, f32[1,384,768]{2,1,0:T(8,128)}, u32[]{:S(2)}, u32[]{:S(2)}) %collective-permute-start.42) | collective-permute-done | bytes 1179680 | tf_op jit(solution)/shard_map/ppermute | solution.py:649
  295.8 3.3 collective-permute-start.48
  300.1 1.9 collective-permute-done.45
  302.0 4.4 %collective-permute-start.49 = (f32[8,16,384]{2,1,0:T(8,128)S(1)}, f32[8,16,384]{2,1,0:T(8,128)S(1)}, u32[]{:S(2)}, u32[]{:S(2)}) collective-permute-start(f32[8,16,384]{2,1,0:T(8,128)S(1)} %add_add_fusion), channel_id=1, source_target_pairs={{0,8},{2,10},{4,12},{6,14},{8,0},{10,2},{12,4},{14,6},{16,24},{18,... | collective-permute-start | bytes 589832 | tf_op jit(solution)/shard_map/ppermute | solution.py:649
  308.6 1.9 maximum_select_fusion.3
  310.4 1.9 maximum_select_fusion.2
  312.4 3.3 collective-permute-start.51
  317.2 2.5 pad_maximum_fusion.1
  319.7 12.2 %collective-permute-done.51 = f32[8,32,384]{2,1,0:T(8,128)S(1)} collective-permute-done((f32[8,32,384]{2,1,0:T(8,128)S(1)}, f32[8,32,384]{2,1,0:T(8,128)S(1)}, u32[]{:S(2)}, u32[]{:S(2)}) %collective-permute-start.51) | collective-permute-done | bytes 393248 | tf_op jit(solution)/shard_map/ppermute | solution.py:649
  333.5 2.4 collective-permute-done.52
  336.0 2.1 collective-permute-start.55
  338.8 1.7 collective-permute-start.56
  344.9 2.0 maximum_select_fusion.1
  347.5 2.0 subtract_multiply_fusion
  349.5 7.4 %collective-permute-done.57 = f32[8,64,384]{2,1,0:T(8,128)} collective-permute-done((f32[8,64,384]{2,1,0:T(8,128)}, f32[8,64,384]{2,1,0:T(8,128)}, u32[]{:S(2)}, u32[]{:S(2)}) %collective-permute-start.57) | collective-permute-done | bytes 786464 | tf_op jit(solution)/shard_map/ppermute | solution.py:649
  356.9 2.0 maximum_select_fusion.5
  358.9 1.8 collective-permute-start.60
  362.8 1.9 maximum_select_fusion
  364.6 2.9 pad_maximum_fusion
  369.5 4.9 %add_convert_fusion = bf16[1024,768]{1,0:T(8,128)(2,1)} fusion(f32[1024,768]{1,0:T(8,128)S(1)} %copy-done.7, f32[1024,768]{1,0:T(8,128)} %get-tuple-element.152, f32[1024,768]{1,0:T(8,128)} %collective-permute-done.58, f32[768]{0:T(1024)S(1)} %copy-done.43), kind=kLoop, calls=%fused_computation.2 | loop fusion | flops 3145728 | bytes 11013120 | tf_op jit(solution)/shard_map/convert_element_type | solution.py:969
  374.5 18.7 %collective-permute-done.60 = f32[8,128,384]{2,1,0:T(8,128)S(1)} collective-permute-done((f32[8,128,384]{2,1,0:T(8,128)S(1)}, f32[8,128,384]{2,1,0:T(8,128)S(1)}, u32[]{:S(2)}, u32[]{:S(2)}) %collective-permute-start.60) | collective-permute-done | bytes 1572896 | tf_op jit(solution)/shard_map/ppermute | solution.py:649
  393.2 2.8 collective-permute-done.59
  (367 shorter events, 108.8 us)
Async XLA Ops:
  0.7 21.4 %copy-start.2 = (bf16[1024,512]{1,0:T(8,128)(2,1)S(1)}, bf16[1024,512]{1,0:T(8,128)(2,1)}, u32[]{:S(2)}) copy-start(bf16[1024,512]{1,0:T(8,128)(2,1)} %features_ref.1) | copy-start | bytes 3145732
  1.9 21.3 %copy-start.59 = (s32[4]{0:T(128)}, s32[4]{0:T(128)S(1)}, u32[]{:S(2)}) copy-start(s32[4]{0:T(128)S(1)} %get-tuple-element.290.patches_ref) | copy-start | bytes 52
  5.2 4.6 %collective-permute-start = (f32[3,512]{1,0:T(4,128)S(1)}, f32[3,512]{1,0:T(4,128)S(1)}, u32[]{:S(2)}, u32[]{:S(2)}) collective-permute-start(f32[3,512]{1,0:T(4,128)S(1)} %maximum_maximum_fusion), channel_id=1, source_target_pairs={{0,2},{2,0},{4,6},{6,4},{8,10},{10,8},{12,14},{14,12},{16,18},{18,... | collective-permute-start | bytes 18440 | tf_op jit(solution)/shard_map/ppermute | solution.py:649
  9.9 3.7 collective-permute-start.1
  13.7 3.7 collective-permute-start.2
  17.4 4.7 %collective-permute-start.3 = (f32[3,512]{1,0:T(4,128)S(1)}, f32[3,512]{1,0:T(4,128)S(1)}, u32[]{:S(2)}, u32[]{:S(2)}) collective-permute-start(f32[3,512]{1,0:T(4,128)S(1)} %add.361), channel_id=1, source_target_pairs={{0,16},{2,18},{4,20},{6,22},{8,24},{10,26},{12,28},{14,30},{16,0},... | collective-permute-start | bytes 18440 | tf_op jit(solution)/shard_map/ppermute | solution.py:649
  24.3 9.6 %collective-permute-start.4 = (f32[1024,768]{1,0:T(8,128)S(1)}, f32[1024,768]{1,0:T(8,128)}, u32[]{:S(2)}, u32[]{:S(2)}) collective-permute-start(f32[1024,768]{1,0:T(8,128)S(1)} %fusion.53.own_ref), channel_id=1, source_target_pairs={{0,1},{1,0},{2,3},{3,2},{4,5},{5,4},{6,7},{7,6},{8,9},{9,8},{10,11... | collective-permute-start | bytes 9437192 | tf_op jit(solution)/shard_map/ppermute | solution.py:644
  48.9 5.9 %collective-permute-start.5 = (f32[1024,768]{1,0:T(8,128)}, f32[1024,768]{1,0:T(8,128)S(1)}, u32[]{:S(2)}, u32[]{:S(2)}) collective-permute-start(f32[1024,768]{1,0:T(8,128)} %get-tuple-element.123.own_ref), channel_id=1, source_target_pairs={{0,1},{1,0},{2,3},{3,2},{4,5},{5,4},{6,7},{7,6},{8,9},{9,8},{10,11... | collective-permute-start | bytes 9437192 | tf_op jit(solution)/shard_map/ppermute | solution.py:644
  76.7 12.8 %collective-permute-start.6 = (f32[1024,768]{1,0:T(8,128)}, f32[1024,768]{1,0:T(8,128)}, u32[]{:S(2)}, u32[]{:S(2)}) collective-permute-start(f32[1024,768]{1,0:T(8,128)} %get-tuple-element.127.own_ref), channel_id=1, source_target_pairs={{0,1},{1,0},{2,3},{3,2},{4,5},{5,4},{6,7},{7,6},{8,9},{9,8},{10,11... | collective-permute-start | bytes 9437192 | tf_op jit(solution)/shard_map/ppermute | solution.py:644
  80.5 32.8 %collective-permute-start.7 = (f32[1,384,768]{2,1,0:T(8,128)}, f32[1,384,768]{2,1,0:T(8,128)S(1)}, u32[]{:S(2)}, u32[]{:S(2)}) collective-permute-start(f32[1,384,768]{2,1,0:T(8,128)} %convolution_bitcast_fusion.3), channel_id=1, source_target_pairs={{0,2},{2,0},{4,6},{6,4},{8,10},{10,8},{12,14},{14,12},{16,18},{18,... | collective-permute-start | bytes 3538952 | tf_op jit(solution)/shard_map/ppermute | solution.py:649
  85.3 28.3 %collective-permute-start.8 = (f32[1,384,768]{2,1,0:T(8,128)}, f32[1,384,768]{2,1,0:T(8,128)}, u32[]{:S(2)}, u32[]{:S(2)}) collective-permute-start(f32[1,384,768]{2,1,0:T(8,128)} %convolution_bitcast_fusion.2), channel_id=1, source_target_pairs={{0,4},{2,6},{4,0},{6,2},{8,12},{10,14},{12,8},{14,10},{16,20},{18,... | collective-permute-start | bytes 3538952 | tf_op jit(solution)/shard_map/ppermute | solution.py:649
  89.5 24.1 %copy-start.6 = (f32[384,768]{1,0:T(8,128)S(1)}, f32[384,768]{1,0:T(8,128)}, u32[]{:S(2)}) copy-start(f32[384,768]{1,0:T(8,128)} %fusion.30) | copy-start | bytes 3538948
  113.1 28.2 %collective-permute-start.11 = (f32[1024,768]{1,0:T(8,128)}, f32[1024,768]{1,0:T(8,128)S(1)}, u32[]{:S(2)}, u32[]{:S(2)}) collective-permute-start(f32[1024,768]{1,0:T(8,128)} %get-tuple-element.132.own_ref), channel_id=1, source_target_pairs={{0,1},{1,0},{2,3},{3,2},{4,5},{5,4},{6,7},{7,6},{8,9},{9,8},{10,11... | collective-permute-start | bytes 9437192 | tf_op jit(solution)/shard_map/ppermute | solution.py:644
  115.1 20.2 %collective-permute-start.10 = (f32[1,192,768]{2,1,0:T(8,128)S(1)}, f32[1,192,768]{2,1,0:T(8,128)S(1)}, u32[]{:S(2)}, u32[]{:S(2)}) collective-permute-start(f32[1,192,768]{2,1,0:T(8,128)S(1)} %get-tuple-element.243), channel_id=1, source_target_pairs={{0,2},{2,0},{4,6},{6,4},{8,10},{10,8},{12,14},{14,12},{16,18},{18,... | collective-permute-start | bytes 1769480 | tf_op jit(solution)/shard_map/ppermute | solution.py:649
  115.8 19.5 %collective-permute-start.9 = (f32[1,192,768]{2,1,0:T(8,128)S(1)}, f32[1,192,768]{2,1,0:T(8,128)S(1)}, u32[]{:S(2)}, u32[]{:S(2)}) collective-permute-start(f32[1,192,768]{2,1,0:T(8,128)S(1)} %get-tuple-element.245), channel_id=1, source_target_pairs={{0,4},{2,6},{4,0},{6,2},{8,12},{10,14},{12,8},{14,10},{16,20},{18,... | collective-permute-start | bytes 1769480 | tf_op jit(solution)/shard_map/ppermute | solution.py:649
  121.4 47.4 %collective-permute-start.16 = (f32[1,384,768]{2,1,0:T(8,128)}, f32[1,384,768]{2,1,0:T(8,128)}, u32[]{:S(2)}, u32[]{:S(2)}) collective-permute-start(f32[1,384,768]{2,1,0:T(8,128)} %convolution_bitcast_fusion.1), channel_id=1, source_target_pairs={{0,2},{2,0},{4,6},{6,4},{8,10},{10,8},{12,14},{14,12},{16,18},{18,... | collective-permute-start | bytes 3538952 | tf_op jit(solution)/shard_map/ppermute | solution.py:649
  122.7 46.1 %collective-permute-start.17 = (f32[1,384,768]{2,1,0:T(8,128)}, f32[1,384,768]{2,1,0:T(8,128)}, u32[]{:S(2)}, u32[]{:S(2)}) collective-permute-start(f32[1,384,768]{2,1,0:T(8,128)} %convolution_bitcast_fusion), channel_id=1, source_target_pairs={{0,4},{2,6},{4,0},{6,2},{8,12},{10,14},{12,8},{14,10},{16,20},{18,... | collective-permute-start | bytes 3538952 | tf_op jit(solution)/shard_map/ppermute | solution.py:649
  136.3 29.4 %collective-permute-start.15 = (f32[1,96,768]{2,1,0:T(8,128)}, f32[1,96,768]{2,1,0:T(8,128)}, u32[]{:S(2)}, u32[]{:S(2)}) collective-permute-start(f32[1,96,768]{2,1,0:T(8,128)} %get-tuple-element.265), channel_id=1, source_target_pairs={{0,16},{2,18},{4,20},{6,22},{8,24},{10,26},{12,28},{14,30},{16,0},... | collective-permute-start | bytes 884744 | tf_op jit(solution)/shard_map/ppermute | solution.py:649
  139.7 26.0 %collective-permute-start.14 = (f32[1,96,768]{2,1,0:T(8,128)}, f32[1,96,768]{2,1,0:T(8,128)}, u32[]{:S(2)}, u32[]{:S(2)}) collective-permute-start(f32[1,96,768]{2,1,0:T(8,128)} %get-tuple-element.267), channel_id=1, source_target_pairs={{0,8},{2,10},{4,12},{6,14},{8,0},{10,2},{12,4},{14,6},{16,24},{18,... | collective-permute-start | bytes 884744 | tf_op jit(solution)/shard_map/ppermute | solution.py:649
  166.7 10.2 %collective-permute-start.19 = (f32[1,48,768]{2,1,0:T(8,128)S(1)}, f32[1,48,768]{2,1,0:T(8,128)S(1)}, u32[]{:S(2)}, u32[]{:S(2)}) collective-permute-start(f32[1,48,768]{2,1,0:T(8,128)S(1)} %dynamic-slice_add_fusion.20), channel_id=1, source_target_pairs={{0,8},{2,10},{4,12},{6,14},{8,0},{10,2},{12,4},{14,6},{16,24},{18,... | collective-permute-start | bytes 442376 | tf_op jit(solution)/shard_map/ppermute | solution.py:649
  168.1 9.6 %collective-permute-start.18 = (f32[1,48,768]{2,1,0:T(8,128)S(1)}, f32[1,48,768]{2,1,0:T(8,128)S(1)}, u32[]{:S(2)}, u32[]{:S(2)}) collective-permute-start(f32[1,48,768]{2,1,0:T(8,128)S(1)} %dynamic-slice_add_fusion.21), channel_id=1, source_target_pairs={{0,16},{2,18},{4,20},{6,22},{8,24},{10,26},{12,28},{14,30},{16,0},... | collective-permute-start | bytes 442376 | tf_op jit(solution)/shard_map/ppermute | solution.py:649
  170.3 16.3 %collective-permute-start.21 = (f32[1,192,768]{2,1,0:T(8,128)S(1)}, f32[1,192,768]{2,1,0:T(8,128)S(1)}, u32[]{:S(2)}, u32[]{:S(2)}) collective-permute-start(f32[1,192,768]{2,1,0:T(8,128)S(1)} %get-tuple-element.239), channel_id=1, source_target_pairs={{0,2},{2,0},{4,6},{6,4},{8,10},{10,8},{12,14},{14,12},{16,18},{18,... | collective-permute-start | bytes 1769480 | tf_op jit(solution)/shard_map/ppermute | solution.py:649
  173.0 16.3 %collective-permute-start.20 = (f32[1,192,768]{2,1,0:T(8,128)S(1)}, f32[1,192,768]{2,1,0:T(8,128)S(1)}, u32[]{:S(2)}, u32[]{:S(2)}) collective-permute-start(f32[1,192,768]{2,1,0:T(8,128)S(1)} %get-tuple-element.241), channel_id=1, source_target_pairs={{0,4},{2,6},{4,0},{6,2},{8,12},{10,14},{12,8},{14,10},{16,20},{18,... | collective-permute-start | bytes 1769480 | tf_op jit(solution)/shard_map/ppermute | solution.py:649
  175.5 41.7 %collective-permute-start.12 = (f32[8,128,384]{2,1,0:T(8,128)S(1)}, f32[8,128,384]{2,1,0:T(8,128)S(1)}, u32[]{:S(2)}, u32[]{:S(2)}) collective-permute-start(f32[8,128,384]{2,1,0:T(8,128)S(1)} %pad_maximum_fusion.2), channel_id=1, source_target_pairs={{0,2},{2,0},{4,6},{6,4},{8,10},{10,8},{12,14},{14,12},{16,18},{18,... | collective-permute-start | bytes 4718600 | tf_op jit(solution)/shard_map/ppermute | solution.py:649
  177.0 42.8 %collective-permute-start.13 = (f32[8,128,384]{2,1,0:T(8,128)S(1)}, f32[8,128,384]{2,1,0:T(8,128)S(1)}, u32[]{:S(2)}, u32[]{:S(2)}) collective-permute-start(f32[8,128,384]{2,1,0:T(8,128)S(1)} %pad_maximum_fusion.3), channel_id=1, source_target_pairs={{0,4},{2,6},{4,0},{6,2},{8,12},{10,14},{12,8},{14,10},{16,20},{18,... | collective-permute-start | bytes 4718600 | tf_op jit(solution)/shard_map/ppermute | solution.py:649
  189.3 12.6 %collective-permute-start.23 = (f32[1,96,768]{2,1,0:T(8,128)S(1)}, f32[1,96,768]{2,1,0:T(8,128)S(1)}, u32[]{:S(2)}, u32[]{:S(2)}) collective-permute-start(f32[1,96,768]{2,1,0:T(8,128)S(1)} %get-tuple-element.261), channel_id=1, source_target_pairs={{0,16},{2,18},{4,20},{6,22},{8,24},{10,26},{12,28},{14,30},{16,0},... | collective-permute-start | bytes 884744 | tf_op jit(solution)/shard_map/ppermute | solution.py:649
  192.0 16.6 %collective-permute-start.22 = (f32[1,96,768]{2,1,0:T(8,128)S(1)}, f32[1,96,768]{2,1,0:T(8,128)S(1)}, u32[]{:S(2)}, u32[]{:S(2)}) collective-permute-start(f32[1,96,768]{2,1,0:T(8,128)S(1)} %get-tuple-element.263), channel_id=1, source_target_pairs={{0,8},{2,10},{4,12},{6,14},{8,0},{10,2},{12,4},{14,6},{16,24},{18,... | collective-permute-start | bytes 884744 | tf_op jit(solution)/shard_map/ppermute | solution.py:649
  193.9 14.9 %collective-permute-start.26 = (f32[1,48,768]{2,1,0:T(8,128)S(1)}, f32[1,48,768]{2,1,0:T(8,128)S(1)}, u32[]{:S(2)}, u32[]{:S(2)}) collective-permute-start(f32[1,48,768]{2,1,0:T(8,128)S(1)} %add_add_fusion.5), channel_id=1, source_target_pairs={{0,16},{2,18},{4,20},{6,22},{8,24},{10,26},{12,28},{14,30},{16,0},... | collective-permute-start | bytes 442376 | tf_op jit(solution)/shard_map/ppermute | solution.py:649
  201.9 9.9 %collective-permute-start.27 = (f32[1,48,768]{2,1,0:T(8,128)S(1)}, f32[1,48,768]{2,1,0:T(8,128)S(1)}, u32[]{:S(2)}, u32[]{:S(2)}) collective-permute-start(f32[1,48,768]{2,1,0:T(8,128)S(1)} %add_add_fusion.4), channel_id=1, source_target_pairs={{0,8},{2,10},{4,12},{6,14},{8,0},{10,2},{12,4},{14,6},{16,24},{18,... | collective-permute-start | bytes 442376 | tf_op jit(solution)/shard_map/ppermute | solution.py:649
  208.6 12.9 %collective-permute-start.25 = (f32[1,48,768]{2,1,0:T(8,128)S(1)}, f32[1,48,768]{2,1,0:T(8,128)S(1)}, u32[]{:S(2)}, u32[]{:S(2)}) collective-permute-start(f32[1,48,768]{2,1,0:T(8,128)S(1)} %dynamic-slice_add_fusion.18), channel_id=1, source_target_pairs={{0,8},{2,10},{4,12},{6,14},{8,0},{10,2},{12,4},{14,6},{16,24},{18,... | collective-permute-start | bytes 442376 | tf_op jit(solution)/shard_map/ppermute | solution.py:649
  208.7 13.8 %collective-permute-start.24 = (f32[1,48,768]{2,1,0:T(8,128)S(1)}, f32[1,48,768]{2,1,0:T(8,128)S(1)}, u32[]{:S(2)}, u32[]{:S(2)}) collective-permute-start(f32[1,48,768]{2,1,0:T(8,128)S(1)} %dynamic-slice_add_fusion.19), channel_id=1, source_target_pairs={{0,16},{2,18},{4,20},{6,22},{8,24},{10,26},{12,28},{14,30},{16,0},... | collective-permute-start | bytes 442376 | tf_op jit(solution)/shard_map/ppermute | solution.py:649
  211.8 13.8 %collective-permute-start.28 = (f32[1,96,768]{2,1,0:T(8,128)S(1)}, f32[1,96,768]{2,1,0:T(8,128)S(1)}, u32[]{:S(2)}, u32[]{:S(2)}) collective-permute-start(f32[1,96,768]{2,1,0:T(8,128)S(1)} %maximum_select_fusion.32), channel_id=1, source_target_pairs={{0,8},{2,10},{4,12},{6,14},{8,0},{10,2},{12,4},{14,6},{16,24},{18,... | collective-permute-start | bytes 884744 | tf_op jit(solution)/shard_map/ppermute | solution.py:649
  217.2 18.1 %collective-permute-start.29 = (f32[1,96,768]{2,1,0:T(8,128)S(1)}, f32[1,96,768]{2,1,0:T(8,128)S(1)}, u32[]{:S(2)}, u32[]{:S(2)}) collective-permute-start(f32[1,96,768]{2,1,0:T(8,128)S(1)} %maximum_select_fusion.33), channel_id=1, source_target_pairs={{0,16},{2,18},{4,20},{6,22},{8,24},{10,26},{12,28},{14,30},{16,0},... | collective-permute-start | bytes 884744 | tf_op jit(solution)/shard_map/ppermute | solution.py:649
  220.0 18.8 %collective-permute-start.32 = (f32[8,64,384]{2,1,0:T(8,128)S(1)}, f32[8,64,384]{2,1,0:T(8,128)S(1)}, u32[]{:S(2)}, u32[]{:S(2)}) collective-permute-start(f32[8,64,384]{2,1,0:T(8,128)S(1)} %get-tuple-element.237), channel_id=1, source_target_pairs={{0,4},{2,6},{4,0},{6,2},{8,12},{10,14},{12,8},{14,10},{16,20},{18,... | collective-permute-start | bytes 2359304 | tf_op jit(solution)/shard_map/ppermute | solution.py:649
  221.5 17.2 %collective-permute-start.33 = (f32[8,64,384]{2,1,0:T(8,128)S(1)}, f32[8,64,384]{2,1,0:T(8,128)S(1)}, u32[]{:S(2)}, u32[]{:S(2)}) collective-permute-start(f32[8,64,384]{2,1,0:T(8,128)S(1)} %get-tuple-element.235), channel_id=1, source_target_pairs={{0,2},{2,0},{4,6},{6,4},{8,10},{10,8},{12,14},{14,12},{16,18},{18,... | collective-permute-start | bytes 2359304 | tf_op jit(solution)/shard_map/ppermute | solution.py:649
  222.6 14.4 %collective-permute-start.30 = (f32[1,48,768]{2,1,0:T(8,128)S(1)}, f32[1,48,768]{2,1,0:T(8,128)S(1)}, u32[]{:S(2)}, u32[]{:S(2)}) collective-permute-start(f32[1,48,768]{2,1,0:T(8,128)S(1)} %add_add_fusion.3), channel_id=1, source_target_pairs={{0,16},{2,18},{4,20},{6,22},{8,24},{10,26},{12,28},{14,30},{16,0},... | collective-permute-start | bytes 442376 | tf_op jit(solution)/shard_map/ppermute | solution.py:649
  225.6 11.6 %collective-permute-start.31 = (f32[1,48,768]{2,1,0:T(8,128)S(1)}, f32[1,48,768]{2,1,0:T(8,128)S(1)}, u32[]{:S(2)}, u32[]{:S(2)}) collective-permute-start(f32[1,48,768]{2,1,0:T(8,128)S(1)} %add_add_fusion.2), channel_id=1, source_target_pairs={{0,8},{2,10},{4,12},{6,14},{8,0},{10,2},{12,4},{14,6},{16,24},{18,... | collective-permute-start | bytes 442376 | tf_op jit(solution)/shard_map/ppermute | solution.py:649
  239.6 16.9 %collective-permute-start.34 = (f32[8,32,384]{2,1,0:T(8,128)}, f32[8,32,384]{2,1,0:T(8,128)}, u32[]{:S(2)}, u32[]{:S(2)}) collective-permute-start(f32[8,32,384]{2,1,0:T(8,128)} %get-tuple-element.257), channel_id=1, source_target_pairs={{0,8},{2,10},{4,12},{6,14},{8,0},{10,2},{12,4},{14,6},{16,24},{18,... | collective-permute-start | bytes 1179656 | tf_op jit(solution)/shard_map/ppermute | solution.py:649
  240.8 20.9 %collective-permute-start.35 = (f32[8,32,384]{2,1,0:T(8,128)}, f32[8,32,384]{2,1,0:T(8,128)}, u32[]{:S(2)}, u32[]{:S(2)}) collective-permute-start(f32[8,32,384]{2,1,0:T(8,128)} %get-tuple-element.255), channel_id=1, source_target_pairs={{0,16},{2,18},{4,20},{6,22},{8,24},{10,26},{12,28},{14,30},{16,0},... | collective-permute-start | bytes 1179656 | tf_op jit(solution)/shard_map/ppermute | solution.py:649
  244.1 20.8 %collective-permute-start.37 = (f32[1,192,768]{2,1,0:T(8,128)}, f32[1,192,768]{2,1,0:T(8,128)S(1)}, u32[]{:S(2)}, u32[]{:S(2)}) collective-permute-start(f32[1,192,768]{2,1,0:T(8,128)} %maximum_select_fusion.22), channel_id=1, source_target_pairs={{0,4},{2,6},{4,0},{6,2},{8,12},{10,14},{12,8},{14,10},{16,20},{18,... | collective-permute-start | bytes 1769480 | tf_op jit(solution)/shard_map/ppermute | solution.py:649
  244.6 20.3 %collective-permute-start.38 = (f32[1,192,768]{2,1,0:T(8,128)}, f32[1,192,768]{2,1,0:T(8,128)S(1)}, u32[]{:S(2)}, u32[]{:S(2)}) collective-permute-start(f32[1,192,768]{2,1,0:T(8,128)} %maximum_select_fusion.23), channel_id=1, source_target_pairs={{0,2},{2,0},{4,6},{6,4},{8,10},{10,8},{12,14},{14,12},{16,18},{18,... | collective-permute-start | bytes 1769480 | tf_op jit(solution)/shard_map/ppermute | solution.py:649
  246.4 18.5 %collective-permute-start.36 = (f32[1,11776]{1,0:T(1,128)S(1)}, f32[1,11776]{1,0:T(1,128)S(1)}, u32[]{:S(2)}, u32[]{:S(2)}) collective-permute-start(f32[1,11776]{1,0:T(1,128)S(1)} %constant_dynamic-update-slice_fusion.3), channel_id=1, source_target_pairs={{0,2},{2,0},{4,6},{6,4},{8,10},{10,8},{12,14},{14,12},{16,18},{18,... | collective-permute-start | bytes 141320 | tf_op jit(solution)/shard_map/ppermute | solution.py:649
  266.1 26.4 %collective-permute-start.42 = (f32[1,384,768]{2,1,0:T(8,128)}, f32[1,384,768]{2,1,0:T(8,128)}, u32[]{:S(2)}, u32[]{:S(2)}) collective-permute-start(f32[1,384,768]{2,1,0:T(8,128)} %maximum_select_fusion.7), channel_id=1, source_target_pairs={{0,4},{2,6},{4,0},{6,2},{8,12},{10,14},{12,8},{14,10},{16,20},{18,... | collective-permute-start | bytes 3538952 | tf_op jit(solution)/shard_map/ppermute | solution.py:649
  267.2 26.4 %collective-permute-start.41 = (f32[1,384,768]{2,1,0:T(8,128)}, f32[1,384,768]{2,1,0:T(8,128)}, u32[]{:S(2)}, u32[]{:S(2)}) collective-permute-start(f32[1,384,768]{2,1,0:T(8,128)} %maximum_select_fusion.6), channel_id=1, source_target_pairs={{0,2},{2,0},{4,6},{6,4},{8,10},{10,8},{12,14},{14,12},{16,18},{18,... | collective-permute-start | bytes 3538952 | tf_op jit(solution)/shard_map/ppermute | solution.py:649
  269.2 14.6 %collective-permute-start.39 = (f32[1,96,768]{2,1,0:T(8,128)}, f32[1,96,768]{2,1,0:T(8,128)}, u32[]{:S(2)}, u32[]{:S(2)}) collective-permute-start(f32[1,96,768]{2,1,0:T(8,128)} %maximum_select_fusion.36), channel_id=1, source_target_pairs={{0,8},{2,10},{4,12},{6,14},{8,0},{10,2},{12,4},{14,6},{16,24},{18,... | collective-permute-start | bytes 884744 | tf_op jit(solution)/shard_map/ppermute | solution.py:649
  269.2 15.4 %collective-permute-start.40 = (f32[1,96,768]{2,1,0:T(8,128)}, f32[1,96,768]{2,1,0:T(8,128)}, u32[]{:S(2)}, u32[]{:S(2)}) collective-permute-start(f32[1,96,768]{2,1,0:T(8,128)} %maximum_select_fusion.37), channel_id=1, source_target_pairs={{0,16},{2,18},{4,20},{6,22},{8,24},{10,26},{12,28},{14,30},{16,0},... | collective-permute-start | bytes 884744 | tf_op jit(solution)/shard_map/ppermute | solution.py:649
  274.2 19.5 %collective-permute-start.44 = (f32[8,16,384]{2,1,0:T(8,128)}, f32[8,16,384]{2,1,0:T(8,128)S(1)}, u32[]{:S(2)}, u32[]{:S(2)}) collective-permute-start(f32[8,16,384]{2,1,0:T(8,128)} %dynamic-slice_add_fusion.16), channel_id=1, source_target_pairs={{0,8},{2,10},{4,12},{6,14},{8,0},{10,2},{12,4},{14,6},{16,24},{18,... | collective-permute-start | bytes 589832 | tf_op jit(solution)/shard_map/ppermute | solution.py:649
  283.9 11.0 %collective-permute-start.43 = (f32[8,16,384]{2,1,0:T(8,128)}, f32[8,16,384]{2,1,0:T(8,128)S(1)}, u32[]{:S(2)}, u32[]{:S(2)}) collective-permute-start(f32[8,16,384]{2,1,0:T(8,128)} %dynamic-slice_add_fusion.17), channel_id=1, source_target_pairs={{0,16},{2,18},{4,20},{6,22},{8,24},{10,26},{12,28},{14,30},{16,0},... | collective-permute-start | bytes 589832 | tf_op jit(solution)/shard_map/ppermute | solution.py:649
  285.7 20.7 %collective-permute-start.46 = (f32[1,192,768]{2,1,0:T(8,128)S(1)}, f32[1,192,768]{2,1,0:T(8,128)S(1)}, u32[]{:S(2)}, u32[]{:S(2)}) collective-permute-start(f32[1,192,768]{2,1,0:T(8,128)S(1)} %maximum_select_fusion.26), channel_id=1, source_target_pairs={{0,4},{2,6},{4,0},{6,2},{8,12},{10,14},{12,8},{14,10},{16,20},{18,... | collective-permute-start | bytes 1769480 | tf_op jit(solution)/shard_map/ppermute | solution.py:649
  292.5 13.9 %collective-permute-start.47 = (f32[1,192,768]{2,1,0:T(8,128)S(1)}, f32[1,192,768]{2,1,0:T(8,128)S(1)}, u32[]{:S(2)}, u32[]{:S(2)}) collective-permute-start(f32[1,192,768]{2,1,0:T(8,128)S(1)} %maximum_select_fusion.27), channel_id=1, source_target_pairs={{0,2},{2,0},{4,6},{6,4},{8,10},{10,8},{12,14},{14,12},{16,18},{18,... | collective-permute-start | bytes 1769480 | tf_op jit(solution)/shard_map/ppermute | solution.py:649
  293.6 74.0 %collective-permute-start.58 = (f32[1024,768]{1,0:T(8,128)}, f32[1024,768]{1,0:T(8,128)}, u32[]{:S(2)}, u32[]{:S(2)}) collective-permute-start(f32[1024,768]{1,0:T(8,128)} %get-tuple-element.152), channel_id=1, source_target_pairs={{0,1},{1,0},{2,3},{3,2},{4,5},{5,4},{6,7},{7,6},{8,9},{9,8},{10,11... | collective-permute-start | bytes 9437192 | tf_op jit(solution)/shard_map/ppermute | solution.py:644
  293.7 8.3 %collective-permute-start.45 = (f32[1,11776]{1,0:T(1,128)S(1)}, f32[1,11776]{1,0:T(1,128)S(1)}, u32[]{:S(2)}, u32[]{:S(2)}) collective-permute-start(f32[1,11776]{1,0:T(1,128)S(1)} %add.441), channel_id=1, source_target_pairs={{0,4},{2,6},{4,0},{6,2},{8,12},{10,14},{12,8},{14,10},{16,20},{18,... | collective-permute-start | bytes 141320 | tf_op jit(solution)/shard_map/ppermute | solution.py:649
  295.8 16.5 %collective-permute-start.48 = (f32[8,16,384]{2,1,0:T(8,128)S(1)}, f32[8,16,384]{2,1,0:T(8,128)S(1)}, u32[]{:S(2)}, u32[]{:S(2)}) collective-permute-start(f32[8,16,384]{2,1,0:T(8,128)S(1)} %add_add_fusion.1), channel_id=1, source_target_pairs={{0,16},{2,18},{4,20},{6,22},{8,24},{10,26},{12,28},{14,30},{16,0},... | collective-permute-start | bytes 589832 | tf_op jit(solution)/shard_map/ppermute | solution.py:649
  302.0 10.4 %collective-permute-start.49 = (f32[8,16,384]{2,1,0:T(8,128)S(1)}, f32[8,16,384]{2,1,0:T(8,128)S(1)}, u32[]{:S(2)}, u32[]{:S(2)}) collective-permute-start(f32[8,16,384]{2,1,0:T(8,128)S(1)} %add_add_fusion), channel_id=1, source_target_pairs={{0,8},{2,10},{4,12},{6,14},{8,0},{10,2},{12,4},{14,6},{16,24},{18,... | collective-permute-start | bytes 589832 | tf_op jit(solution)/shard_map/ppermute | solution.py:649
  306.6 32.3 %collective-permute-start.54 = (f32[1,384,768]{2,1,0:T(8,128)S(1)}, f32[1,384,768]{2,1,0:T(8,128)}, u32[]{:S(2)}, u32[]{:S(2)}) collective-permute-start(f32[1,384,768]{2,1,0:T(8,128)S(1)} %maximum_select_fusion.9), channel_id=1, source_target_pairs={{0,4},{2,6},{4,0},{6,2},{8,12},{10,14},{12,8},{14,10},{16,20},{18,... | collective-permute-start | bytes 3538952 | tf_op jit(solution)/shard_map/ppermute | solution.py:649
  307.0 33.5 %collective-permute-start.53 = (f32[1,384,768]{2,1,0:T(8,128)S(1)}, f32[1,384,768]{2,1,0:T(8,128)}, u32[]{:S(2)}, u32[]{:S(2)}) collective-permute-start(f32[1,384,768]{2,1,0:T(8,128)S(1)} %maximum_select_fusion.8), channel_id=1, source_target_pairs={{0,2},{2,0},{4,6},{6,4},{8,10},{10,8},{12,14},{14,12},{16,18},{18,... | collective-permute-start | bytes 3538952 | tf_op jit(solution)/shard_map/ppermute | solution.py:649
  312.4 19.5 %collective-permute-start.51 = (f32[8,32,384]{2,1,0:T(8,128)S(1)}, f32[8,32,384]{2,1,0:T(8,128)S(1)}, u32[]{:S(2)}, u32[]{:S(2)}) collective-permute-start(f32[8,32,384]{2,1,0:T(8,128)S(1)} %maximum_select_fusion.31), channel_id=1, source_target_pairs={{0,16},{2,18},{4,20},{6,22},{8,24},{10,26},{12,28},{14,30},{16,0},... | collective-permute-start | bytes 1179656 | tf_op jit(solution)/shard_map/ppermute | solution.py:649
  315.8 16.7 %collective-permute-start.50 = (f32[8,32,384]{2,1,0:T(8,128)S(1)}, f32[8,32,384]{2,1,0:T(8,128)S(1)}, u32[]{:S(2)}, u32[]{:S(2)}) collective-permute-start(f32[8,32,384]{2,1,0:T(8,128)S(1)} %maximum_select_fusion.30), channel_id=1, source_target_pairs={{0,8},{2,10},{4,12},{6,14},{8,0},{10,2},{12,4},{14,6},{16,24},{18,... | collective-permute-start | bytes 1179656 | tf_op jit(solution)/shard_map/ppermute | solution.py:649
  331.8 4.1 %collective-permute-start.52 = (f32[1,11776]{1,0:T(1,128)S(1)}, f32[1,11776]{1,0:T(1,128)S(1)}, u32[]{:S(2)}, u32[]{:S(2)}) collective-permute-start(f32[1,11776]{1,0:T(1,128)S(1)} %add.446), channel_id=1, source_target_pairs={{0,8},{2,10},{4,12},{6,14},{8,0},{10,2},{12,4},{14,6},{16,24},{18,... | collective-permute-start | bytes 141320 | tf_op jit(solution)/shard_map/ppermute | solution.py:649
  336.0 5.0 %collective-permute-start.55 = (f32[1,11776]{1,0:T(1,128)S(1)}, f32[1,11776]{1,0:T(1,128)S(1)}, u32[]{:S(2)}, u32[]{:S(2)}) collective-permute-start(f32[1,11776]{1,0:T(1,128)S(1)} %add.447), channel_id=1, source_target_pairs={{0,16},{2,18},{4,20},{6,22},{8,24},{10,26},{12,28},{14,30},{16,0},... | collective-permute-start | bytes 141320 | tf_op jit(solution)/shard_map/ppermute | solution.py:649
  338.2 18.6 %collective-permute-start.57 = (f32[8,64,384]{2,1,0:T(8,128)}, f32[8,64,384]{2,1,0:T(8,128)}, u32[]{:S(2)}, u32[]{:S(2)}) collective-permute-start(f32[8,64,384]{2,1,0:T(8,128)} %maximum_select_fusion.19), channel_id=1, source_target_pairs={{0,2},{2,0},{4,6},{6,4},{8,10},{10,8},{12,14},{14,12},{16,18},{18,... | collective-permute-start | bytes 2359304 | tf_op jit(solution)/shard_map/ppermute | solution.py:649
  338.8 18.1 %collective-permute-start.56 = (f32[8,64,384]{2,1,0:T(8,128)S(1)}, f32[8,64,384]{2,1,0:T(8,128)}, u32[]{:S(2)}, u32[]{:S(2)}) collective-permute-start(f32[8,64,384]{2,1,0:T(8,128)S(1)} %maximum_select_fusion.18), channel_id=1, source_target_pairs={{0,4},{2,6},{4,0},{6,2},{8,12},{10,14},{12,8},{14,10},{16,20},{18,... | collective-permute-start | bytes 2359304 | tf_op jit(solution)/shard_map/ppermute | solution.py:649
  358.9 34.3 %collective-permute-start.60 = (f32[8,128,384]{2,1,0:T(8,128)S(1)}, f32[8,128,384]{2,1,0:T(8,128)S(1)}, u32[]{:S(2)}, u32[]{:S(2)}) collective-permute-start(f32[8,128,384]{2,1,0:T(8,128)S(1)} %maximum_select_fusion.5), channel_id=1, source_target_pairs={{0,4},{2,6},{4,0},{6,2},{8,12},{10,14},{12,8},{14,10},{16,20},{18,... | collective-permute-start | bytes 4718600 | tf_op jit(solution)/shard_map/ppermute | solution.py:649
  362.2 33.8 %collective-permute-start.59 = (f32[8,128,384]{2,1,0:T(8,128)S(1)}, f32[8,128,384]{2,1,0:T(8,128)S(1)}, u32[]{:S(2)}, u32[]{:S(2)}) collective-permute-start(f32[8,128,384]{2,1,0:T(8,128)S(1)} %maximum_select_fusion.4), channel_id=1, source_target_pairs={{0,2},{2,0},{4,6},{6,4},{8,10},{10,8},{12,14},{14,12},{16,18},{18,... | collective-permute-start | bytes 4718600 | tf_op jit(solution)/shard_map/ppermute | solution.py:649
  (70 other events, 329.5 us)

commit v6 on v5

--- a/solution.py
+++ b/solution.py
@@ -22,13 +22,13 @@
     (
         "R a R E",
         "h R b i",
-        "R E R s",
-        "E E R H",
-        "w H E R",
-        "E H H s",
-        "R E R H",
-        "s E H H",
-        "s E s p",
+        "E R E R",
+        "s E R H",
+        "w H R E",
+        "H H s R",
+        "E s E R",
+        "H s E H",
+        "H s E p",
         "H o E H",
     )
 )

time: 408 us -> 399 us (0.978)
  waiting for transfers between devices: 118 us -> 147 us
  starting transfers between devices: 82.9 us -> 54.8 us
  other arithmetic: 68.8 us -> 55.2 us
  local copies, waits for them, and re-layouts: 25.8 us -> 30.4 us
    ppermute x56, waiting for transfers between devices: 115 us -> 143 us  [exchange(): lax.ppermute(values, 'dp', [(rank, rank ^ 1 << bit) for rank in range(cou...]
    ppermute x56, starting transfers between devices: 82.3 us -> 54.2 us  [exchange(): lax.ppermute(values, 'dp', [(rank, rank ^ 1 << bit) for rank in range(cou...]
    select_n x40, other arithmetic: 29.5 us -> 17.4 us  [spread(): jnp.where(side == 1, jnp.concatenate([other, mine], axis=1), jnp.concaten...]
    unnamed x161 -> x135, local copies, waits for them, and re-layouts: 12.8 us -> 18.3 us
  transfers between devices with their start and end apart: 61 -> 61, of which waited for: 25 -> 35; matrix products, arithmetic and copies ran while one was open for 23% -> 21% of each run, Pallas kernels for 11% -> 12%
where the time goes in v6:
time: 399 us; the launch traced here: 394 us
  waiting for transfers between devices  147 us (37%)
  Pallas kernels  80.7 us (20%)
  other arithmetic  55.2 us (14%)
  starting transfers between devices  54.8 us (14%)
  local copies, waits for them, and re-layouts  30.4 us (8%)
  matrix products  24.5 us (6%)
    ppermute x56, waiting for transfers between devices, exchange(): lax.ppermute(values, 'dp', [(rank, rank ^ 1 << bit) for rank in range(cou...  143 us
    ppermute x56, starting transfers between devices, exchange(): lax.ppermute(values, 'dp', [(rank, rank ^ 1 << bit) for rank in range(cou...  54.2 us
    dot_general x16, matrix products, mult(): lax.dot_general(left, right, (dims, ((), ())), preferred_element_type=jnp...  24.5 us
    pallas_call x1, Pallas kernels, attend_back(): pl.pallas_call(attend_back_kernel, grid_spec=pltpu.PrefetchScalarGridSpec...  23.6 us
    pallas_call x1, Pallas kernels, feed(): pl.pallas_call(feed_kernel, grid_spec=pltpu.PrefetchScalarGridSpec(num_sc...  20.2 us
    pallas_call x1, Pallas kernels, stem_back(): pl.pallas_call(stem_back_kernel, grid_spec=pltpu.PrefetchScalarGridSpec(n...  19.6 us
    unnamed x135, local copies, waits for them, and re-layouts  18.3 us
    select_n x40, other arithmetic, spread(): jnp.where(side == 1, jnp.concatenate([other, mine], axis=1), jnp.concaten...  17.4 us
  transfers between devices with their start and end apart: 61, of which 35 were waited for; matrix products, arithmetic and copies ran while one was open for 21% of the time, Pallas kernels for 12%

profile of v6, /device:TPU:0, one launch (start us, length us, event | category | flops | bytes accessed | tf_op | source)
XLA Modules:
  0.0 394.3 jit_solution(12621092293887707788)
XLA Ops:
  3.4 1.7 fusion
  5.2 3.0 collective-permute-start
  8.2 1.6 collective-permute-done
  9.9 2.1 collective-permute-start.1
  12.0 1.6 collective-permute-done.1
  13.7 2.1 collective-permute-start.2
  15.7 1.6 collective-permute-done.2
  17.4 3.0 collective-permute-start.3
  20.4 1.6 collective-permute-done.3
  27.9 1.9 constant_dynamic-update-slice_fusion.2
  31.6 2.3 distance_bias.1.bias_ref
  34.0 14.9 %attend.1 = (f32[1024,768]{1,0:T(8,128)}, bf16[1024,768]{1,0:T(8,128)(2,1)}, bf16[1024,1152]{1,0:T(8,128)(2,1)}, f32[4,6,256,256]{3,2,1,0:T(8,128)}, f32[1024,38...) custom-call(s32[4]{0:T(128)} %copy-done.46, s32[4]{0:T(128)} %get-tuple-element.291.valid_ref, ...), custom_call_target="tpu_custom_call" | custom-call | flops 15000000512 | bytes 45000000 | tf_op jit(solution)/shard_map/attend/pallas_call | solution.py:189
  51.5 3.4 collective-permute-done.5.other_ref
  54.8 1.7 copy-done.50
  56.5 20.2 %feed.1 = (f32[1024,768]{1,0:T(8,128)}, bf16[1024,768]{1,0:T(8,128)(2,1)}, bf16[1024,1536]{1,0:T(8,128)(2,1)}, bf16[1024,1536]{1,0:T(8,128)(2,1)}, f32[1024,768]...) custom-call(s32[4]{0:T(128)} %get-tuple-element.291.valid_ref, ...), custom_call_target="tpu_custom_call" | custom-call | flops 23000000512 | bytes 69000000 | tf_op jit(solution)/shard_map/feed/pallas_call | solution.py:331
  76.9 3.6 convolution_bitcast_fusion.3
  80.5 1.9 collective-permute-start.7
  82.4 3.0 convolution_bitcast_fusion.2
  86.8 1.8 fusion.30
  89.5 23.6 %attend_back.1 = (f32[1024,768]{1,0:T(8,128)}, bf16[1024,768]{1,0:T(8,128)(2,1)}, bf16[1024,1152]{1,0:T(8,128)(2,1)}, f32[1024,768]{1,0:T(8,128)}, f32[1,768]{1,...) custom-call(f32[1024,768]{1,0:T(8,128)} %get-tuple-element.124.middl, ...), custom_call_target="tpu_custom_call" | custom-call | flops 24000000000 | bytes 72000000 | tf_op jit(solution)/shard_map/attend_back/pallas_call | solution.py:492
  115.8 1.8 collective-permute-start.9
  117.6 1.9 convolution_bitcast_fusion
  119.5 1.9 convolution_bitcast_fusion.1
  131.4 1.8 fusion.6
  133.2 1.8 fusion.9
  135.9 2.5 collective-permute-start.17
  139.4 1.6 collective-permute-start.16
  141.0 1.6 copy-done.49
  142.7 19.6 %stem_back.1 = (f32[1024,768]{1,0:T(8,128)}, bf16[1024,768]{1,0:T(8,128)(2,1)}, f32[1024,512]{1,0:T(8,128)}, f32[1,768]{1,0:T(1,128)}, f32[1,768]{1,0:T(1,128)}, /*index=5*/f32[1,512]{1,0:T(1,128)}, f32[1,512]{1,0:T(1,128)}) custom-call(s32[4]{0:T(128)} %copy-done.46, f32[1024,768]{1,0:T(8,128)} %get-tuple-element.122.hidden_ref, ...), custom_call_target="tpu_custom_call" | custom-call | flops 10000000000 | bytes 30000000 | tf_op jit(solution)/shard_map/stem_back/pallas_call | solution.py:602
  165.2 2.0 fusion.14
  181.6 4.5 %collective-permute-done.19 = f32[1,192,768]{2,1,0:T(8,128)S(1)} collective-permute-done((f32[1,192,768]{2,1,0:T(8,128)S(1)}, f32[1,192,768]{2,1,0:T(8,128)S(1)}, u32[]{:S(2)}, u32[]{:S(2)}) %collective-permute-start.19) | collective-permute-done | bytes 589856 | tf_op jit(solution)/shard_map/ppermute | solution.py:649
  186.4 2.4 collective-permute-done.18
  189.8 9.2 %collective-permute-done.20 = f32[1,48,768]{2,1,0:T(8,128)S(1)} collective-permute-done((f32[1,48,768]{2,1,0:T(8,128)S(1)}, f32[1,48,768]{2,1,0:T(8,128)S(1)}, u32[]{:S(2)}, u32[]{:S(2)}) %collective-permute-start.20) | collective-permute-done | bytes 147488 | tf_op jit(solution)/shard_map/ppermute | solution.py:649
  200.9 1.8 collective-permute-done.22
  202.9 6.0 %collective-permute-done.23 = f32[1,96,768]{2,1,0:T(8,128)S(1)} collective-permute-done((f32[1,96,768]{2,1,0:T(8,128)S(1)}, f32[1,96,768]{2,1,0:T(8,128)S(1)}, u32[]{:S(2)}, u32[]{:S(2)}) %collective-permute-start.23) | collective-permute-done | bytes 294944 | tf_op jit(solution)/shard_map/ppermute | solution.py:649
  209.1 3.5 collective-permute-done.24
  212.6 2.6 collective-permute-done.25
  215.4 1.9 collective-permute-done.12
  217.3 2.2 collective-permute-done.13
  223.5 7.4 %collective-permute-done.27 = f32[1,96,768]{2,1,0:T(8,128)S(1)} collective-permute-done((f32[1,96,768]{2,1,0:T(8,128)S(1)}, f32[1,96,768]{2,1,0:T(8,128)S(1)}, u32[]{:S(2)}, u32[]{:S(2)}) %collective-permute-start.27) | collective-permute-done | bytes 294944 | tf_op jit(solution)/shard_map/ppermute | solution.py:649
  232.7 3.5 collective-permute-done.30
  242.7 12.7 %collective-permute-done.33 = f32[8,32,384]{2,1,0:T(8,128)} collective-permute-done((f32[8,32,384]{2,1,0:T(8,128)}, f32[8,32,384]{2,1,0:T(8,128)}, u32[]{:S(2)}, u32[]{:S(2)}) %collective-permute-start.33) | collective-permute-done | bytes 393248 | tf_op jit(solution)/shard_map/ppermute | solution.py:649
  258.8 1.7 collective-permute-start.43
  262.1 1.7 collective-permute-done.38
  266.3 12.3 %collective-permute-done.40 = f32[1,96,768]{2,1,0:T(8,128)S(1)} collective-permute-done((f32[1,96,768]{2,1,0:T(8,128)S(1)}, f32[1,96,768]{2,1,0:T(8,128)S(1)}, u32[]{:S(2)}, u32[]{:S(2)}) %collective-permute-start.40) | collective-permute-done | bytes 294944 | tf_op jit(solution)/shard_map/ppermute | solution.py:649
  279.4 1.9 collective-permute-done.41
  281.5 6.7 %collective-permute-done.43 = f32[1,384,768]{2,1,0:T(8,128)S(1)} collective-permute-done((f32[1,384,768]{2,1,0:T(8,128)S(1)}, f32[1,384,768]{2,1,0:T(8,128)S(1)}, u32[]{:S(2)}, u32[]{:S(2)}) %collective-permute-start.43) | collective-permute-done | bytes 1179680 | tf_op jit(solution)/shard_map/ppermute | solution.py:649
  291.6 2.9 collective-permute-start.49
  295.6 2.8 collective-permute-done.47
  304.1 2.0 collective-permute-done.50
  308.5 2.5 pad_maximum_fusion.1
  311.0 13.8 %collective-permute-done.52 = f32[8,32,384]{2,1,0:T(8,128)S(1)} collective-permute-done((f32[8,32,384]{2,1,0:T(8,128)S(1)}, f32[8,32,384]{2,1,0:T(8,128)S(1)}, u32[]{:S(2)}, u32[]{:S(2)}) %collective-permute-start.52) | collective-permute-done | bytes 393248 | tf_op jit(solution)/shard_map/ppermute | solution.py:649
  327.2 2.6 collective-permute-done.53
  334.5 2.0 maximum_select_fusion.1
  337.1 2.0 subtract_multiply_fusion
  339.2 6.5 %collective-permute-done.57 = f32[8,64,384]{2,1,0:T(8,128)} collective-permute-done((f32[8,64,384]{2,1,0:T(8,128)}, f32[8,64,384]{2,1,0:T(8,128)}, u32[]{:S(2)}, u32[]{:S(2)}) %collective-permute-start.57) | collective-permute-done | bytes 786464 | tf_op jit(solution)/shard_map/ppermute | solution.py:649
  345.7 2.6 collective-permute-done.56
  348.3 2.0 maximum_select_fusion.5
  354.2 1.9 maximum_select_fusion
  356.1 2.9 pad_maximum_fusion
  359.3 1.7 copy-done.7
  361.0 4.9 %add_convert_fusion = bf16[1024,768]{1,0:T(8,128)(2,1)} fusion(f32[1024,768]{1,0:T(8,128)S(1)} %copy-done.7, f32[1024,768]{1,0:T(8,128)} %get-tuple-element.152, f32[1024,768]{1,0:T(8,128)} %collective-permute-done.58, f32[768]{0:T(1024)S(1)} %copy-done.34), kind=kLoop, calls=%fused_computation.2 | loop fusion | flops 3145728 | bytes 11013120 | tf_op jit(solution)/shard_map/convert_element_type | solution.py:969
  365.9 18.8 %collective-permute-done.60 = f32[8,128,384]{2,1,0:T(8,128)S(1)} collective-permute-done((f32[8,128,384]{2,1,0:T(8,128)S(1)}, f32[8,128,384]{2,1,0:T(8,128)S(1)}, u32[]{:S(2)}, u32[]{:S(2)}) %collective-permute-start.60) | collective-permute-done | bytes 1572896 | tf_op jit(solution)/shard_map/ppermute | solution.py:649
  384.7 2.1 collective-permute-done.59
  (341 shorter events, 103.0 us)
Async XLA Ops:
  5.2 4.6 %collective-permute-start = (f32[3,512]{1,0:T(4,128)S(1)}, f32[3,512]{1,0:T(4,128)S(1)}, u32[]{:S(2)}, u32[]{:S(2)}) collective-permute-start(f32[3,512]{1,0:T(4,128)S(1)} %maximum_maximum_fusion), channel_id=1, source_target_pairs={{0,2},{2,0},{4,6},{6,4},{8,10},{10,8},{12,14},{14,12},{16,18},{18,... | collective-permute-start | bytes 18440 | tf_op jit(solution)/shard_map/ppermute | solution.py:649
  9.9 3.7 collective-permute-start.1
  13.7 3.7 collective-permute-start.2
  17.4 4.7 %collective-permute-start.3 = (f32[3,512]{1,0:T(4,128)S(1)}, f32[3,512]{1,0:T(4,128)S(1)}, u32[]{:S(2)}, u32[]{:S(2)}) collective-permute-start(f32[3,512]{1,0:T(4,128)S(1)} %add.361), channel_id=1, source_target_pairs={{0,16},{2,18},{4,20},{6,22},{8,24},{10,26},{12,28},{14,30},{16,0},... | collective-permute-start | bytes 18440 | tf_op jit(solution)/shard_map/ppermute | solution.py:649
  24.3 9.6 %collective-permute-start.4 = (f32[1024,768]{1,0:T(8,128)S(1)}, f32[1024,768]{1,0:T(8,128)}, u32[]{:S(2)}, u32[]{:S(2)}) collective-permute-start(f32[1024,768]{1,0:T(8,128)S(1)} %fusion.53.own_ref), channel_id=1, source_target_pairs={{0,1},{1,0},{2,3},{3,2},{4,5},{5,4},{6,7},{7,6},{8,9},{9,8},{10,11... | collective-permute-start | bytes 9437192 | tf_op jit(solution)/shard_map/ppermute | solution.py:644
  48.9 5.9 %collective-permute-start.5 = (f32[1024,768]{1,0:T(8,128)}, f32[1024,768]{1,0:T(8,128)S(1)}, u32[]{:S(2)}, u32[]{:S(2)}) collective-permute-start(f32[1024,768]{1,0:T(8,128)} %get-tuple-element.123.own_ref), channel_id=1, source_target_pairs={{0,1},{1,0},{2,3},{3,2},{4,5},{5,4},{6,7},{7,6},{8,9},{9,8},{10,11... | collective-permute-start | bytes 9437192 | tf_op jit(solution)/shard_map/ppermute | solution.py:644
  76.7 12.8 %collective-permute-start.6 = (f32[1024,768]{1,0:T(8,128)}, f32[1024,768]{1,0:T(8,128)}, u32[]{:S(2)}, u32[]{:S(2)}) collective-permute-start(f32[1024,768]{1,0:T(8,128)} %get-tuple-element.127.own_ref), channel_id=1, source_target_pairs={{0,1},{1,0},{2,3},{3,2},{4,5},{5,4},{6,7},{7,6},{8,9},{9,8},{10,11... | collective-permute-start | bytes 9437192 | tf_op jit(solution)/shard_map/ppermute | solution.py:644
  80.5 32.8 %collective-permute-start.7 = (f32[1,384,768]{2,1,0:T(8,128)}, f32[1,384,768]{2,1,0:T(8,128)S(1)}, u32[]{:S(2)}, u32[]{:S(2)}) collective-permute-start(f32[1,384,768]{2,1,0:T(8,128)} %convolution_bitcast_fusion.3), channel_id=1, source_target_pairs={{0,2},{2,0},{4,6},{6,4},{8,10},{10,8},{12,14},{14,12},{16,18},{18,... | collective-permute-start | bytes 3538952 | tf_op jit(solution)/shard_map/ppermute | solution.py:649
  85.3 28.3 %collective-permute-start.8 = (f32[1,384,768]{2,1,0:T(8,128)}, f32[1,384,768]{2,1,0:T(8,128)}, u32[]{:S(2)}, u32[]{:S(2)}) collective-permute-start(f32[1,384,768]{2,1,0:T(8,128)} %convolution_bitcast_fusion.2), channel_id=1, source_target_pairs={{0,4},{2,6},{4,0},{6,2},{8,12},{10,14},{12,8},{14,10},{16,20},{18,... | collective-permute-start | bytes 3538952 | tf_op jit(solution)/shard_map/ppermute | solution.py:649
  89.5 24.1 %copy-start.6 = (f32[384,768]{1,0:T(8,128)S(1)}, f32[384,768]{1,0:T(8,128)}, u32[]{:S(2)}) copy-start(f32[384,768]{1,0:T(8,128)} %fusion.30) | copy-start | bytes 3538948
  113.1 27.9 %collective-permute-start.11 = (f32[1024,768]{1,0:T(8,128)}, f32[1024,768]{1,0:T(8,128)S(1)}, u32[]{:S(2)}, u32[]{:S(2)}) collective-permute-start(f32[1024,768]{1,0:T(8,128)} %get-tuple-element.132.own_ref), channel_id=1, source_target_pairs={{0,1},{1,0},{2,3},{3,2},{4,5},{5,4},{6,7},{7,6},{8,9},{9,8},{10,11... | collective-permute-start | bytes 9437192 | tf_op jit(solution)/shard_map/ppermute | solution.py:644
  115.1 19.9 %collective-permute-start.10 = (f32[1,192,768]{2,1,0:T(8,128)S(1)}, f32[1,192,768]{2,1,0:T(8,128)S(1)}, u32[]{:S(2)}, u32[]{:S(2)}) collective-permute-start(f32[1,192,768]{2,1,0:T(8,128)S(1)} %get-tuple-element.243), channel_id=1, source_target_pairs={{0,2},{2,0},{4,6},{6,4},{8,10},{10,8},{12,14},{14,12},{16,18},{18,... | collective-permute-start | bytes 1769480 | tf_op jit(solution)/shard_map/ppermute | solution.py:649
  115.8 19.2 %collective-permute-start.9 = (f32[1,192,768]{2,1,0:T(8,128)S(1)}, f32[1,192,768]{2,1,0:T(8,128)S(1)}, u32[]{:S(2)}, u32[]{:S(2)}) collective-permute-start(f32[1,192,768]{2,1,0:T(8,128)S(1)} %get-tuple-element.245), channel_id=1, source_target_pairs={{0,4},{2,6},{4,0},{6,2},{8,12},{10,14},{12,8},{14,10},{16,20},{18,... | collective-permute-start | bytes 1769480 | tf_op jit(solution)/shard_map/ppermute | solution.py:649
  121.4 46.6 %collective-permute-start.14 = (f32[1,384,768]{2,1,0:T(8,128)}, f32[1,384,768]{2,1,0:T(8,128)}, u32[]{:S(2)}, u32[]{:S(2)}) collective-permute-start(f32[1,384,768]{2,1,0:T(8,128)} %convolution_bitcast_fusion.1), channel_id=1, source_target_pairs={{0,2},{2,0},{4,6},{6,4},{8,10},{10,8},{12,14},{14,12},{16,18},{18,... | collective-permute-start | bytes 3538952 | tf_op jit(solution)/shard_map/ppermute | solution.py:649
  122.7 45.3 %collective-permute-start.15 = (f32[1,384,768]{2,1,0:T(8,128)}, f32[1,384,768]{2,1,0:T(8,128)}, u32[]{:S(2)}, u32[]{:S(2)}) collective-permute-start(f32[1,384,768]{2,1,0:T(8,128)} %convolution_bitcast_fusion), channel_id=1, source_target_pairs={{0,4},{2,6},{4,0},{6,2},{8,12},{10,14},{12,8},{14,10},{16,20},{18,... | collective-permute-start | bytes 3538952 | tf_op jit(solution)/shard_map/ppermute | solution.py:649
  135.9 37.7 %collective-permute-start.17 = (f32[1,96,768]{2,1,0:T(8,128)}, f32[1,96,768]{2,1,0:T(8,128)}, u32[]{:S(2)}, u32[]{:S(2)}) collective-permute-start(f32[1,96,768]{2,1,0:T(8,128)} %get-tuple-element.273), channel_id=1, source_target_pairs={{0,16},{2,18},{4,20},{6,22},{8,24},{10,26},{12,28},{14,30},{16,0},... | collective-permute-start | bytes 884744 | tf_op jit(solution)/shard_map/ppermute | solution.py:649
  139.4 34.3 %collective-permute-start.16 = (f32[1,96,768]{2,1,0:T(8,128)}, f32[1,96,768]{2,1,0:T(8,128)}, u32[]{:S(2)}, u32[]{:S(2)}) collective-permute-start(f32[1,96,768]{2,1,0:T(8,128)} %get-tuple-element.275), channel_id=1, source_target_pairs={{0,8},{2,10},{4,12},{6,14},{8,0},{10,2},{12,4},{14,6},{16,24},{18,... | collective-permute-start | bytes 884744 | tf_op jit(solution)/shard_map/ppermute | solution.py:649
  142.7 22.4 %copy-start.28 = (f32[6,512]{1,0:T(8,128)S(1)}, f32[6,512]{1,0:T(8,128)}, u32[]{:S(2)}) copy-start(f32[6,512]{1,0:T(8,128)} %get-tuple-element.174) | copy-start | bytes 36868
  142.7 22.5 %copy-start.5 = (bf16[1024,512]{1,0:T(8,128)(2,1)S(1)}, bf16[1024,512]{1,0:T(8,128)(2,1)}, u32[]{:S(2)}) copy-start(bf16[1024,512]{1,0:T(8,128)(2,1)} %copy-done.4) | copy-start | bytes 3145732
  169.8 16.3 %collective-permute-start.19 = (f32[1,192,768]{2,1,0:T(8,128)S(1)}, f32[1,192,768]{2,1,0:T(8,128)S(1)}, u32[]{:S(2)}, u32[]{:S(2)}) collective-permute-start(f32[1,192,768]{2,1,0:T(8,128)S(1)} %get-tuple-element.239), channel_id=1, source_target_pairs={{0,2},{2,0},{4,6},{6,4},{8,10},{10,8},{12,14},{14,12},{16,18},{18,... | collective-permute-start | bytes 1769480 | tf_op jit(solution)/shard_map/ppermute | solution.py:649
  172.5 16.3 %collective-permute-start.18 = (f32[1,192,768]{2,1,0:T(8,128)S(1)}, f32[1,192,768]{2,1,0:T(8,128)S(1)}, u32[]{:S(2)}, u32[]{:S(2)}) collective-permute-start(f32[1,192,768]{2,1,0:T(8,128)S(1)} %get-tuple-element.241), channel_id=1, source_target_pairs={{0,4},{2,6},{4,0},{6,2},{8,12},{10,14},{12,8},{14,10},{16,20},{18,... | collective-permute-start | bytes 1769480 | tf_op jit(solution)/shard_map/ppermute | solution.py:649
  174.6 14.7 %collective-permute-start.21 = (f32[1,48,768]{2,1,0:T(8,128)S(1)}, f32[1,48,768]{2,1,0:T(8,128)S(1)}, u32[]{:S(2)}, u32[]{:S(2)}) collective-permute-start(f32[1,48,768]{2,1,0:T(8,128)S(1)} %dynamic-slice_add_fusion.20), channel_id=1, source_target_pairs={{0,8},{2,10},{4,12},{6,14},{8,0},{10,2},{12,4},{14,6},{16,24},{18,... | collective-permute-start | bytes 442376 | tf_op jit(solution)/shard_map/ppermute | solution.py:649
  176.4 40.9 %collective-permute-start.12 = (f32[8,128,384]{2,1,0:T(8,128)S(1)}, f32[8,128,384]{2,1,0:T(8,128)S(1)}, u32[]{:S(2)}, u32[]{:S(2)}) collective-permute-start(f32[8,128,384]{2,1,0:T(8,128)S(1)} %pad_maximum_fusion.2), channel_id=1, source_target_pairs={{0,2},{2,0},{4,6},{6,4},{8,10},{10,8},{12,14},{14,12},{16,18},{18,... | collective-permute-start | bytes 4718600 | tf_op jit(solution)/shard_map/ppermute | solution.py:649
  177.9 41.6 %collective-permute-start.13 = (f32[8,128,384]{2,1,0:T(8,128)S(1)}, f32[8,128,384]{2,1,0:T(8,128)S(1)}, u32[]{:S(2)}, u32[]{:S(2)}) collective-permute-start(f32[8,128,384]{2,1,0:T(8,128)S(1)} %pad_maximum_fusion.3), channel_id=1, source_target_pairs={{0,4},{2,6},{4,0},{6,2},{8,12},{10,14},{12,8},{14,10},{16,20},{18,... | collective-permute-start | bytes 4718600 | tf_op jit(solution)/shard_map/ppermute | solution.py:649
  186.1 12.8 %collective-permute-start.20 = (f32[1,48,768]{2,1,0:T(8,128)S(1)}, f32[1,48,768]{2,1,0:T(8,128)S(1)}, u32[]{:S(2)}, u32[]{:S(2)}) collective-permute-start(f32[1,48,768]{2,1,0:T(8,128)S(1)} %dynamic-slice_add_fusion.21), channel_id=1, source_target_pairs={{0,16},{2,18},{4,20},{6,22},{8,24},{10,26},{12,28},{14,30},{16,0},... | collective-permute-start | bytes 442376 | tf_op jit(solution)/shard_map/ppermute | solution.py:649
  188.8 13.9 %collective-permute-start.22 = (f32[1,96,768]{2,1,0:T(8,128)S(1)}, f32[1,96,768]{2,1,0:T(8,128)S(1)}, u32[]{:S(2)}, u32[]{:S(2)}) collective-permute-start(f32[1,96,768]{2,1,0:T(8,128)S(1)} %get-tuple-element.271), channel_id=1, source_target_pairs={{0,8},{2,10},{4,12},{6,14},{8,0},{10,2},{12,4},{14,6},{16,24},{18,... | collective-permute-start | bytes 884744 | tf_op jit(solution)/shard_map/ppermute | solution.py:649
  189.3 19.6 %collective-permute-start.23 = (f32[1,96,768]{2,1,0:T(8,128)S(1)}, f32[1,96,768]{2,1,0:T(8,128)S(1)}, u32[]{:S(2)}, u32[]{:S(2)}) collective-permute-start(f32[1,96,768]{2,1,0:T(8,128)S(1)} %get-tuple-element.269), channel_id=1, source_target_pairs={{0,16},{2,18},{4,20},{6,22},{8,24},{10,26},{12,28},{14,30},{16,0},... | collective-permute-start | bytes 884744 | tf_op jit(solution)/shard_map/ppermute | solution.py:649
  199.9 12.7 %collective-permute-start.24 = (f32[1,48,768]{2,1,0:T(8,128)S(1)}, f32[1,48,768]{2,1,0:T(8,128)S(1)}, u32[]{:S(2)}, u32[]{:S(2)}) collective-permute-start(f32[1,48,768]{2,1,0:T(8,128)S(1)} %add_add_fusion.5), channel_id=1, source_target_pairs={{0,16},{2,18},{4,20},{6,22},{8,24},{10,26},{12,28},{14,30},{16,0},... | collective-permute-start | bytes 442376 | tf_op jit(solution)/shard_map/ppermute | solution.py:649
  202.7 12.5 %collective-permute-start.25 = (f32[1,48,768]{2,1,0:T(8,128)S(1)}, f32[1,48,768]{2,1,0:T(8,128)S(1)}, u32[]{:S(2)}, u32[]{:S(2)}) collective-permute-start(f32[1,48,768]{2,1,0:T(8,128)S(1)} %add_add_fusion.4), channel_id=1, source_target_pairs={{0,8},{2,10},{4,12},{6,14},{8,0},{10,2},{12,4},{14,6},{16,24},{18,... | collective-permute-start | bytes 442376 | tf_op jit(solution)/shard_map/ppermute | solution.py:649
  209.0 23.7 %collective-permute-start.29 = (f32[1,48,768]{2,1,0:T(8,128)S(1)}, f32[1,48,768]{2,1,0:T(8,128)S(1)}, u32[]{:S(2)}, u32[]{:S(2)}) collective-permute-start(f32[1,48,768]{2,1,0:T(8,128)S(1)} %dynamic-slice_add_fusion.18), channel_id=1, source_target_pairs={{0,8},{2,10},{4,12},{6,14},{8,0},{10,2},{12,4},{14,6},{16,24},{18,... | collective-permute-start | bytes 442376 | tf_op jit(solution)/shard_map/ppermute | solution.py:649
  215.2 8.3 %collective-permute-start.26 = (f32[1,96,768]{2,1,0:T(8,128)S(1)}, f32[1,96,768]{2,1,0:T(8,128)S(1)}, u32[]{:S(2)}, u32[]{:S(2)}) collective-permute-start(f32[1,96,768]{2,1,0:T(8,128)S(1)} %maximum_select_fusion.32), channel_id=1, source_target_pairs={{0,8},{2,10},{4,12},{6,14},{8,0},{10,2},{12,4},{14,6},{16,24},{18,... | collective-permute-start | bytes 884744 | tf_op jit(solution)/shard_map/ppermute | solution.py:649
  215.3 15.6 %collective-permute-start.27 = (f32[1,96,768]{2,1,0:T(8,128)S(1)}, f32[1,96,768]{2,1,0:T(8,128)S(1)}, u32[]{:S(2)}, u32[]{:S(2)}) collective-permute-start(f32[1,96,768]{2,1,0:T(8,128)S(1)} %maximum_select_fusion.33), channel_id=1, source_target_pairs={{0,16},{2,18},{4,20},{6,22},{8,24},{10,26},{12,28},{14,30},{16,0},... | collective-permute-start | bytes 884744 | tf_op jit(solution)/shard_map/ppermute | solution.py:649
  219.7 16.5 %collective-permute-start.30 = (f32[8,64,384]{2,1,0:T(8,128)S(1)}, f32[8,64,384]{2,1,0:T(8,128)S(1)}, u32[]{:S(2)}, u32[]{:S(2)}) collective-permute-start(f32[8,64,384]{2,1,0:T(8,128)S(1)} %get-tuple-element.237), channel_id=1, source_target_pairs={{0,4},{2,6},{4,0},{6,2},{8,12},{10,14},{12,8},{14,10},{16,20},{18,... | collective-permute-start | bytes 2359304 | tf_op jit(solution)/shard_map/ppermute | solution.py:649
  221.2 16.6 %collective-permute-start.31 = (f32[8,64,384]{2,1,0:T(8,128)S(1)}, f32[8,64,384]{2,1,0:T(8,128)S(1)}, u32[]{:S(2)}, u32[]{:S(2)}) collective-permute-start(f32[8,64,384]{2,1,0:T(8,128)S(1)} %get-tuple-element.235), channel_id=1, source_target_pairs={{0,2},{2,0},{4,6},{6,4},{8,10},{10,8},{12,14},{14,12},{16,18},{18,... | collective-permute-start | bytes 2359304 | tf_op jit(solution)/shard_map/ppermute | solution.py:649
  223.5 9.1 %collective-permute-start.28 = (f32[1,48,768]{2,1,0:T(8,128)S(1)}, f32[1,48,768]{2,1,0:T(8,128)S(1)}, u32[]{:S(2)}, u32[]{:S(2)}) collective-permute-start(f32[1,48,768]{2,1,0:T(8,128)S(1)} %dynamic-slice_add_fusion.19), channel_id=1, source_target_pairs={{0,16},{2,18},{4,20},{6,22},{8,24},{10,26},{12,28},{14,30},{16,0},... | collective-permute-start | bytes 442376 | tf_op jit(solution)/shard_map/ppermute | solution.py:649
  238.6 16.8 %collective-permute-start.33 = (f32[8,32,384]{2,1,0:T(8,128)}, f32[8,32,384]{2,1,0:T(8,128)}, u32[]{:S(2)}, u32[]{:S(2)}) collective-permute-start(f32[8,32,384]{2,1,0:T(8,128)} %get-tuple-element.255), channel_id=1, source_target_pairs={{0,16},{2,18},{4,20},{6,22},{8,24},{10,26},{12,28},{14,30},{16,0},... | collective-permute-start | bytes 1179656 | tf_op jit(solution)/shard_map/ppermute | solution.py:649
  239.8 15.7 %collective-permute-start.32 = (f32[8,32,384]{2,1,0:T(8,128)}, f32[8,32,384]{2,1,0:T(8,128)}, u32[]{:S(2)}, u32[]{:S(2)}) collective-permute-start(f32[8,32,384]{2,1,0:T(8,128)} %get-tuple-element.257), channel_id=1, source_target_pairs={{0,8},{2,10},{4,12},{6,14},{8,0},{10,2},{12,4},{14,6},{16,24},{18,... | collective-permute-start | bytes 1179656 | tf_op jit(solution)/shard_map/ppermute | solution.py:649
  240.2 18.5 %collective-permute-start.35 = (f32[1,192,768]{2,1,0:T(8,128)}, f32[1,192,768]{2,1,0:T(8,128)S(1)}, u32[]{:S(2)}, u32[]{:S(2)}) collective-permute-start(f32[1,192,768]{2,1,0:T(8,128)} %maximum_select_fusion.22), channel_id=1, source_target_pairs={{0,4},{2,6},{4,0},{6,2},{8,12},{10,14},{12,8},{14,10},{16,20},{18,... | collective-permute-start | bytes 1769480 | tf_op jit(solution)/shard_map/ppermute | solution.py:649
  240.5 18.2 %collective-permute-start.36 = (f32[1,192,768]{2,1,0:T(8,128)}, f32[1,192,768]{2,1,0:T(8,128)S(1)}, u32[]{:S(2)}, u32[]{:S(2)}) collective-permute-start(f32[1,192,768]{2,1,0:T(8,128)} %maximum_select_fusion.23), channel_id=1, source_target_pairs={{0,2},{2,0},{4,6},{6,4},{8,10},{10,8},{12,14},{14,12},{16,18},{18,... | collective-permute-start | bytes 1769480 | tf_op jit(solution)/shard_map/ppermute | solution.py:649
  242.0 16.1 %collective-permute-start.34 = (f32[1,11776]{1,0:T(1,128)S(1)}, f32[1,11776]{1,0:T(1,128)S(1)}, u32[]{:S(2)}, u32[]{:S(2)}) collective-permute-start(f32[1,11776]{1,0:T(1,128)S(1)} %constant_dynamic-update-slice_fusion.3), channel_id=1, source_target_pairs={{0,2},{2,0},{4,6},{6,4},{8,10},{10,8},{12,14},{14,12},{16,18},{18,... | collective-permute-start | bytes 141320 | tf_op jit(solution)/shard_map/ppermute | solution.py:649
  255.4 6.7 %collective-permute-start.37 = (f32[1,48,768]{2,1,0:T(8,128)S(1)}, f32[1,48,768]{2,1,0:T(8,128)S(1)}, u32[]{:S(2)}, u32[]{:S(2)}) collective-permute-start(f32[1,48,768]{2,1,0:T(8,128)S(1)} %add_add_fusion.3), channel_id=1, source_target_pairs={{0,16},{2,18},{4,20},{6,22},{8,24},{10,26},{12,28},{14,30},{16,0},... | collective-permute-start | bytes 442376 | tf_op jit(solution)/shard_map/ppermute | solution.py:649
  255.5 8.2 %collective-permute-start.38 = (f32[1,48,768]{2,1,0:T(8,128)S(1)}, f32[1,48,768]{2,1,0:T(8,128)S(1)}, u32[]{:S(2)}, u32[]{:S(2)}) collective-permute-start(f32[1,48,768]{2,1,0:T(8,128)S(1)} %add_add_fusion.2), channel_id=1, source_target_pairs={{0,8},{2,10},{4,12},{6,14},{8,0},{10,2},{12,4},{14,6},{16,24},{18,... | collective-permute-start | bytes 442376 | tf_op jit(solution)/shard_map/ppermute | solution.py:649
  258.3 7.3 %collective-permute-start.39 = (f32[1,11776]{1,0:T(1,128)S(1)}, f32[1,11776]{1,0:T(1,128)S(1)}, u32[]{:S(2)}, u32[]{:S(2)}) collective-permute-start(f32[1,11776]{1,0:T(1,128)S(1)} %add.441), channel_id=1, source_target_pairs={{0,4},{2,6},{4,0},{6,2},{8,12},{10,14},{12,8},{14,10},{16,20},{18,... | collective-permute-start | bytes 141320 | tf_op jit(solution)/shard_map/ppermute | solution.py:649
  258.8 29.4 %collective-permute-start.43 = (f32[1,384,768]{2,1,0:T(8,128)S(1)}, f32[1,384,768]{2,1,0:T(8,128)S(1)}, u32[]{:S(2)}, u32[]{:S(2)}) collective-permute-start(f32[1,384,768]{2,1,0:T(8,128)S(1)} %maximum_select_fusion.7), channel_id=1, source_target_pairs={{0,4},{2,6},{4,0},{6,2},{8,12},{10,14},{12,8},{14,10},{16,20},{18,... | collective-permute-start | bytes 3538952 | tf_op jit(solution)/shard_map/ppermute | solution.py:649
  260.6 28.8 %collective-permute-start.42 = (f32[1,384,768]{2,1,0:T(8,128)S(1)}, f32[1,384,768]{2,1,0:T(8,128)S(1)}, u32[]{:S(2)}, u32[]{:S(2)}) collective-permute-start(f32[1,384,768]{2,1,0:T(8,128)S(1)} %maximum_select_fusion.6), channel_id=1, source_target_pairs={{0,2},{2,0},{4,6},{6,4},{8,10},{10,8},{12,14},{14,12},{16,18},{18,... | collective-permute-start | bytes 3538952 | tf_op jit(solution)/shard_map/ppermute | solution.py:649
  263.8 14.9 %collective-permute-start.40 = (f32[1,96,768]{2,1,0:T(8,128)S(1)}, f32[1,96,768]{2,1,0:T(8,128)S(1)}, u32[]{:S(2)}, u32[]{:S(2)}) collective-permute-start(f32[1,96,768]{2,1,0:T(8,128)S(1)} %maximum_select_fusion.36), channel_id=1, source_target_pairs={{0,8},{2,10},{4,12},{6,14},{8,0},{10,2},{12,4},{14,6},{16,24},{18,... | collective-permute-start | bytes 884744 | tf_op jit(solution)/shard_map/ppermute | solution.py:649
  264.2 17.1 %collective-permute-start.41 = (f32[1,96,768]{2,1,0:T(8,128)S(1)}, f32[1,96,768]{2,1,0:T(8,128)S(1)}, u32[]{:S(2)}, u32[]{:S(2)}) collective-permute-start(f32[1,96,768]{2,1,0:T(8,128)S(1)} %maximum_select_fusion.37), channel_id=1, source_target_pairs={{0,16},{2,18},{4,20},{6,22},{8,24},{10,26},{12,28},{14,30},{16,0},... | collective-permute-start | bytes 884744 | tf_op jit(solution)/shard_map/ppermute | solution.py:649
  265.6 23.9 %collective-permute-start.45 = (f32[8,16,384]{2,1,0:T(8,128)S(1)}, f32[8,16,384]{2,1,0:T(8,128)S(1)}, u32[]{:S(2)}, u32[]{:S(2)}) collective-permute-start(f32[8,16,384]{2,1,0:T(8,128)S(1)} %dynamic-slice_add_fusion.16), channel_id=1, source_target_pairs={{0,8},{2,10},{4,12},{6,14},{8,0},{10,2},{12,4},{14,6},{16,24},{18,... | collective-permute-start | bytes 589832 | tf_op jit(solution)/shard_map/ppermute | solution.py:649
  278.7 11.9 %collective-permute-start.44 = (f32[8,16,384]{2,1,0:T(8,128)S(1)}, f32[8,16,384]{2,1,0:T(8,128)S(1)}, u32[]{:S(2)}, u32[]{:S(2)}) collective-permute-start(f32[8,16,384]{2,1,0:T(8,128)S(1)} %dynamic-slice_add_fusion.17), channel_id=1, source_target_pairs={{0,16},{2,18},{4,20},{6,22},{8,24},{10,26},{12,28},{14,30},{16,0},... | collective-permute-start | bytes 589832 | tf_op jit(solution)/shard_map/ppermute | solution.py:649
  281.3 17.1 %collective-permute-start.47 = (f32[1,192,768]{2,1,0:T(8,128)S(1)}, f32[1,192,768]{2,1,0:T(8,128)S(1)}, u32[]{:S(2)}, u32[]{:S(2)}) collective-permute-start(f32[1,192,768]{2,1,0:T(8,128)S(1)} %maximum_select_fusion.26), channel_id=1, source_target_pairs={{0,4},{2,6},{4,0},{6,2},{8,12},{10,14},{12,8},{14,10},{16,20},{18,... | collective-permute-start | bytes 1769480 | tf_op jit(solution)/shard_map/ppermute | solution.py:649
  288.2 11.0 %collective-permute-start.48 = (f32[1,192,768]{2,1,0:T(8,128)S(1)}, f32[1,192,768]{2,1,0:T(8,128)S(1)}, u32[]{:S(2)}, u32[]{:S(2)}) collective-permute-start(f32[1,192,768]{2,1,0:T(8,128)S(1)} %maximum_select_fusion.27), channel_id=1, source_target_pairs={{0,2},{2,0},{4,6},{6,4},{8,10},{10,8},{12,14},{14,12},{16,18},{18,... | collective-permute-start | bytes 1769480 | tf_op jit(solution)/shard_map/ppermute | solution.py:649
  289.4 69.7 %collective-permute-start.58 = (f32[1024,768]{1,0:T(8,128)}, f32[1024,768]{1,0:T(8,128)}, u32[]{:S(2)}, u32[]{:S(2)}) collective-permute-start(f32[1024,768]{1,0:T(8,128)} %get-tuple-element.152), channel_id=1, source_target_pairs={{0,1},{1,0},{2,3},{3,2},{4,5},{5,4},{6,7},{7,6},{8,9},{9,8},{10,11... | collective-permute-start | bytes 9437192 | tf_op jit(solution)/shard_map/ppermute | solution.py:644
  289.5 5.9 %collective-permute-start.46 = (f32[1,11776]{1,0:T(1,128)S(1)}, f32[1,11776]{1,0:T(1,128)S(1)}, u32[]{:S(2)}, u32[]{:S(2)}) collective-permute-start(f32[1,11776]{1,0:T(1,128)S(1)} %add.442), channel_id=1, source_target_pairs={{0,8},{2,10},{4,12},{6,14},{8,0},{10,2},{12,4},{14,6},{16,24},{18,... | collective-permute-start | bytes 141320 | tf_op jit(solution)/shard_map/ppermute | solution.py:649
  291.6 12.5 %collective-permute-start.49 = (f32[8,16,384]{2,1,0:T(8,128)S(1)}, f32[8,16,384]{2,1,0:T(8,128)S(1)}, u32[]{:S(2)}, u32[]{:S(2)}) collective-permute-start(f32[8,16,384]{2,1,0:T(8,128)S(1)} %add_add_fusion.1), channel_id=1, source_target_pairs={{0,16},{2,18},{4,20},{6,22},{8,24},{10,26},{12,28},{14,30},{16,0},... | collective-permute-start | bytes 589832 | tf_op jit(solution)/shard_map/ppermute | solution.py:649
  295.4 10.6 %collective-permute-start.50 = (f32[8,16,384]{2,1,0:T(8,128)S(1)}, f32[8,16,384]{2,1,0:T(8,128)S(1)}, u32[]{:S(2)}, u32[]{:S(2)}) collective-permute-start(f32[8,16,384]{2,1,0:T(8,128)S(1)} %add_add_fusion), channel_id=1, source_target_pairs={{0,8},{2,10},{4,12},{6,14},{8,0},{10,2},{12,4},{14,6},{16,24},{18,... | collective-permute-start | bytes 589832 | tf_op jit(solution)/shard_map/ppermute | solution.py:649
  300.3 34.2 %collective-permute-start.55 = (f32[1,384,768]{2,1,0:T(8,128)}, f32[1,384,768]{2,1,0:T(8,128)}, u32[]{:S(2)}, u32[]{:S(2)}) collective-permute-start(f32[1,384,768]{2,1,0:T(8,128)} %maximum_select_fusion.9), channel_id=1, source_target_pairs={{0,4},{2,6},{4,0},{6,2},{8,12},{10,14},{12,8},{14,10},{16,20},{18,... | collective-permute-start | bytes 3538952 | tf_op jit(solution)/shard_map/ppermute | solution.py:649
  303.2 31.3 %collective-permute-start.54 = (f32[1,384,768]{2,1,0:T(8,128)}, f32[1,384,768]{2,1,0:T(8,128)}, u32[]{:S(2)}, u32[]{:S(2)}) collective-permute-start(f32[1,384,768]{2,1,0:T(8,128)} %maximum_select_fusion.8), channel_id=1, source_target_pairs={{0,2},{2,0},{4,6},{6,4},{8,10},{10,8},{12,14},{14,12},{16,18},{18,... | collective-permute-start | bytes 3538952 | tf_op jit(solution)/shard_map/ppermute | solution.py:649
  306.1 18.8 %collective-permute-start.52 = (f32[8,32,384]{2,1,0:T(8,128)S(1)}, f32[8,32,384]{2,1,0:T(8,128)S(1)}, u32[]{:S(2)}, u32[]{:S(2)}) collective-permute-start(f32[8,32,384]{2,1,0:T(8,128)S(1)} %maximum_select_fusion.31), channel_id=1, source_target_pairs={{0,16},{2,18},{4,20},{6,22},{8,24},{10,26},{12,28},{14,30},{16,0},... | collective-permute-start | bytes 1179656 | tf_op jit(solution)/shard_map/ppermute | solution.py:649
  306.8 18.0 %collective-permute-start.51 = (f32[8,32,384]{2,1,0:T(8,128)S(1)}, f32[8,32,384]{2,1,0:T(8,128)S(1)}, u32[]{:S(2)}, u32[]{:S(2)}) collective-permute-start(f32[8,32,384]{2,1,0:T(8,128)S(1)} %maximum_select_fusion.30), channel_id=1, source_target_pairs={{0,8},{2,10},{4,12},{6,14},{8,0},{10,2},{12,4},{14,6},{16,24},{18,... | collective-permute-start | bytes 1179656 | tf_op jit(solution)/shard_map/ppermute | solution.py:649
  324.9 5.0 %collective-permute-start.53 = (f32[1,11776]{1,0:T(1,128)S(1)}, f32[1,11776]{1,0:T(1,128)S(1)}, u32[]{:S(2)}, u32[]{:S(2)}) collective-permute-start(f32[1,11776]{1,0:T(1,128)S(1)} %add.447), channel_id=1, source_target_pairs={{0,16},{2,18},{4,20},{6,22},{8,24},{10,26},{12,28},{14,30},{16,0},... | collective-permute-start | bytes 141320 | tf_op jit(solution)/shard_map/ppermute | solution.py:649
  325.9 19.8 %collective-permute-start.57 = (f32[8,64,384]{2,1,0:T(8,128)}, f32[8,64,384]{2,1,0:T(8,128)}, u32[]{:S(2)}, u32[]{:S(2)}) collective-permute-start(f32[8,64,384]{2,1,0:T(8,128)} %maximum_select_fusion.19), channel_id=1, source_target_pairs={{0,2},{2,0},{4,6},{6,4},{8,10},{10,8},{12,14},{14,12},{16,18},{18,... | collective-permute-start | bytes 2359304 | tf_op jit(solution)/shard_map/ppermute | solution.py:649
  329.8 18.5 %collective-permute-start.56 = (f32[8,64,384]{2,1,0:T(8,128)S(1)}, f32[8,64,384]{2,1,0:T(8,128)}, u32[]{:S(2)}, u32[]{:S(2)}) collective-permute-start(f32[8,64,384]{2,1,0:T(8,128)S(1)} %maximum_select_fusion.18), channel_id=1, source_target_pairs={{0,4},{2,6},{4,0},{6,2},{8,12},{10,14},{12,8},{14,10},{16,20},{18,... | collective-permute-start | bytes 2359304 | tf_op jit(solution)/shard_map/ppermute | solution.py:649
  350.3 34.4 %collective-permute-start.60 = (f32[8,128,384]{2,1,0:T(8,128)S(1)}, f32[8,128,384]{2,1,0:T(8,128)S(1)}, u32[]{:S(2)}, u32[]{:S(2)}) collective-permute-start(f32[8,128,384]{2,1,0:T(8,128)S(1)} %maximum_select_fusion.5), channel_id=1, source_target_pairs={{0,4},{2,6},{4,0},{6,2},{8,12},{10,14},{12,8},{14,10},{16,20},{18,... | collective-permute-start | bytes 4718600 | tf_op jit(solution)/shard_map/ppermute | solution.py:649
  352.7 34.1 %collective-permute-start.59 = (f32[8,128,384]{2,1,0:T(8,128)S(1)}, f32[8,128,384]{2,1,0:T(8,128)S(1)}, u32[]{:S(2)}, u32[]{:S(2)}) collective-permute-start(f32[8,128,384]{2,1,0:T(8,128)S(1)} %maximum_select_fusion.4), channel_id=1, source_target_pairs={{0,2},{2,0},{4,6},{6,4},{8,10},{10,8},{12,14},{14,12},{16,18},{18,... | collective-permute-start | bytes 4718600 | tf_op jit(solution)/shard_map/ppermute | solution.py:649
  (57 other events, 298.1 us)
